TPU v7x, 256 devices: a whole 4x4x8 slice. The times are simulated.
256 devices in a mesh: tm: 32 (over z, x), strip: 8 (over y, core).
Axes of the slice: x: 4, y: 4, z: 8, core: 2. Of those that a mesh axis runs over, the one named last changes fastest.
Arguments:
- coarse_feat: bfloat16 [128, 96, 4, 384], P('tm', 'strip'), may hold values from -6 to 6
- coarse_gain: float32 [384], replicated, may hold values from 0.5 to 2
- coarse_weight: bfloat16 [3, 3, 3, 384, 384], replicated, may hold values from -0.0625 to 0.0625
- coarse_bias: float32 [384], replicated, may hold values from -3 to 3
- up_weight: bfloat16 [3, 3, 384, 192], replicated, may hold values from -0.109375 to 0.109375
- up_bias: float32 [192], replicated, may hold values from -3 to 3
- fine_gain: float32 [192], replicated, may hold values from 0.5 to 2
- fine_weight: bfloat16 [3, 3, 3, 192, 192], replicated, may hold values from -0.078125 to 0.078125
- fine_bias: float32 [192], replicated, may hold values from -3 to 3
Outputs:
- decoded: bfloat16 [128, 192, 8, 192], P('tm', 'strip')
All inputs are finite; a program needn't handle non-finite values.
Results may differ from a plain program's by a relative error of at most 0.0095.
Values may be sent and summed in bfloat16 or wider, within the bound.
No kernel may reach another device: no remote copies, remote signals or barrier semaphores. Data moves between devices by JAX's collectives and lax.ppermute only.
A program may use at most 64 MiB of HBM per device.

v0:
```python
import jax
import jax.numpy as jnp
from jax import lax

eps = 1e-06


def prep(feat, gain):
    values = feat.astype(jnp.float32)
    meansq = jnp.mean(values * values, axis=-1, keepdims=True)
    return jax.nn.silu(values * lax.rsqrt(meansq + eps) * gain).astype(jnp.bfloat16)


def causal_conv(act, kernel):
    out = lax.conv_general_dilated(
        act.astype(jnp.float32)[None],
        kernel.astype(jnp.float32),
        (1, 1, 1),
        [(2, 0), (1, 1), (1, 1)],
        dimension_numbers=("NDHWC", "DHWIO", "NDHWC"),
    )
    return out[0]


def plane_conv(act, kernel):
    return lax.conv_general_dilated(
        act.astype(jnp.float32),
        kernel.astype(jnp.float32),
        (1, 1),
        [(1, 1), (1, 1)],
        dimension_numbers=("NHWC", "HWIO", "NHWC"),
    )


def reference(
    coarse_feat,
    coarse_gain,
    coarse_weight,
    coarse_bias,
    up_weight,
    up_bias,
    fine_gain,
    fine_weight,
    fine_bias,
):
    act0 = prep(coarse_feat, coarse_gain)
    coarse = (causal_conv(act0, coarse_weight) + coarse_bias).astype(jnp.bfloat16)
    upper = jnp.repeat(jnp.repeat(coarse, 2, axis=1), 2, axis=2)
    lifted = (plane_conv(upper, up_weight) + up_bias).astype(jnp.bfloat16)
    act1 = prep(lifted, fine_gain)
    decoded = causal_conv(act1, fine_weight) + fine_bias + lifted.astype(jnp.float32)
    return decoded.astype(jnp.bfloat16)


def solution(mesh):
    return reference
```

profile of v0, /device:TPU:137, one launch (start us, length us, event | category | flops | bytes accessed | tf_op | source)
XLA Modules:
  0.0 81.2 jit_solution(1148996847171034230)
XLA Ops:
  0.0 0.0 copy-start
  0.0 1.2 %fusion.33 = f32[4,12,4]{2,1,0:T(8,128)S(1)} fusion(bf16[4,12,4,384]{3,2,1,0:T(4,128)(2,1)} %param), kind=kLoop, calls=%fused_computation.44 | loop fusion | flops 220992 | bytes 148224 | tf_op jit(solution)/reduce_sum | solution.py:10
  1.2 1.2 %fusion.40 = bf16[1,4,12,4,384]{4,3,2,1,0:T(4,128)(2,1)S(1)} fusion(bf16[4,12,4,384]{3,2,1,0:T(4,128)(2,1)} %param, f32[384]{0:T(512)} %param.1, f32[4,12,4]{2,1,0:T(8,128)S(1)} %add_rsqrt_fusion), kind=kLoop, calls=%fused_computation.52 | loop fusion | flops 589824 | bytes 297216 | tf_op jit(solution)/broadcast_in_dim | solution.py:16
  2.4 3.1 %collective-permute-start = (bf16[1,2,12,4,384]{4,3,2,1,0:T(4,128)(2,1)S(1)}, bf16[1,2,12,4,384]{4,3,2,1,0:T(4,128)(2,1)S(1)}, u32[]{:S(2)}, u32[]{:S(2)}) collective-permute-start(bf16[1,2,12,4,384]{4,3,2,1,0:T(4,128)(2,1)S(1)} %slice.8), channel_id=1, source_target_pairs={{0,8},{1,9},{2,10},{3,11},{4,12},{5,13},{6,14},{7,15},{8,16},{9,17... | collective-permute-start | bytes 221192 | tf_op jit(solution)/conv_general_dilated | solution.py:15
  5.6 1.3 %dynamic-slice.4 = s32[1]{0:T(128)} dynamic-slice(s32[256]{0:T(256)} %constant.25, u32[]{:T(128)S(6)} %partition-id), dynamic_slice_sizes={1} | dynamic-slice | bytes 12 | tf_op jit(solution)/conv_general_dilated | solution.py:15
  7.5 3.4 %collective-permute-done = bf16[1,2,12,4,384]{4,3,2,1,0:T(4,128)(2,1)S(1)} collective-permute-done((bf16[1,2,12,4,384]{4,3,2,1,0:T(4,128)(2,1)S(1)}, bf16[1,2,12,4,384]{4,3,2,1,0:T(4,128)(2,1)S(1)}, u32[]{:S(2)}, u32[]{:S(2)}) %collective-permute-start) | collective-permute-done | bytes 73760 | tf_op jit(solution)/conv_general_dilated | solution.py:15
  10.9 0.1 fusion.30
  11.0 4.9 %collective-permute-start.1 = (bf16[1,6,1,4,384]{4,3,2,1,0:T(4,128)(2,1)S(1)}, bf16[1,6,1,4,384]{4,3,2,1,0:T(4,128)(2,1)S(1)}, u32[]{:S(2)}, u32[]{:S(2)}) collective-permute-start(bf16[1,6,1,4,384]{4,3,2,1,0:T(4,128)(2,1)S(1)} %get-tuple-element.8), channel_id=2, source_target_pairs={{0,1},{1,2},{2,3},{3,4},{4,5},{5,6},{6,7},{8,9},{9,10},{10,11},{11... | collective-permute-start | bytes 55304 | tf_op jit(solution)/conv_general_dilated | solution.py:15
  15.9 1.9 %collective-permute-start.2 = (bf16[1,6,1,4,384]{4,3,2,1,0:T(4,128)(2,1)S(1)}, bf16[1,6,1,4,384]{4,3,2,1,0:T(4,128)(2,1)S(1)}, u32[]{:S(2)}, u32[]{:S(2)}) collective-permute-start(bf16[1,6,1,4,384]{4,3,2,1,0:T(4,128)(2,1)S(1)} %get-tuple-element.9), channel_id=3, source_target_pairs={{1,0},{2,1},{3,2},{4,3},{5,4},{6,5},{7,6},{9,8},{10,9},{11,10},{12... | collective-permute-start | bytes 55304 | tf_op jit(solution)/conv_general_dilated | solution.py:15
  17.9 1.3 %dynamic-slice.5 = s32[1]{0:T(128)} dynamic-slice(s32[256]{0:T(256)} %constant.26, u32[]{:T(128)S(6)} %partition-id), dynamic_slice_sizes={1} | dynamic-slice | bytes 12 | tf_op jit(solution)/conv_general_dilated | solution.py:15
  19.8 0.0 collective-permute-done.1
  19.8 1.2 %collective-permute-done.2 = bf16[1,6,1,4,384]{4,3,2,1,0:T(4,128)(2,1)S(1)} collective-permute-done((bf16[1,6,1,4,384]{4,3,2,1,0:T(4,128)(2,1)S(1)}, bf16[1,6,1,4,384]{4,3,2,1,0:T(4,128)(2,1)S(1)}, u32[]{:S(2)}, u32[]{:S(2)}) %collective-permute-start.2) | collective-permute-done | bytes 18464 | tf_op jit(solution)/conv_general_dilated | solution.py:15
  21.0 0.2 fusion.29
  21.2 0.0 copy-start.1
  21.2 11.4 %fusion.24 = f32[1,4,12,4,384]{4,0,3,2,1:T(1,128)S(1)} fusion(bf16[3,3,3,384,384]{4,3,2,1,0:T(8,128)(2,1)} %param.2, bf16[1,6,14,4,384]{4,3,2,1,0:T(4,128)(2,1)S(1)} %fusion.29), kind=kOutput, calls=%fused_computation.30 | convolution fusion | flops 1274019840 | bytes 8515584 | tf_op jit(solution)/conv_general_dilated | solution.py:15
  32.6 0.0 copy-done.1
  32.6 0.0 copy-start.3
  32.7 0.0 copy-start.4
  32.7 0.1 fusion.39
  32.8 0.1 copy.12
  32.8 0.1 broadcast_in_dim.27
  32.9 0.2 broadcast_in_dim.28
  33.1 2.4 %collective-permute-start.3 = (bf16[4,1,8,384]{3,0,2,1:T(4,128)(2,1)S(1)}, bf16[4,1,8,384]{3,0,2,1:T(4,128)(2,1)S(1)}, u32[]{:S(2)}, u32[]{:S(2)}) collective-permute-start(bf16[4,1,8,384]{3,0,2,1:T(4,128)(2,1)S(1)} %get-tuple-element.6), channel_id=4, source_target_pairs={{0,1},{1,2},{2,3},{3,4},{4,5},{5,6},{6,7},{8,9},{9,10},{10,11},{11... | collective-permute-start | bytes 73736 | tf_op jit(solution)/conv_general_dilated | solution.py:26
  35.5 2.1 %collective-permute-start.4 = (bf16[4,1,8,384]{3,0,2,1:T(4,128)(2,1)S(1)}, bf16[4,1,8,384]{3,0,2,1:T(4,128)(2,1)S(1)}, u32[]{:S(2)}, u32[]{:S(2)}) collective-permute-start(bf16[4,1,8,384]{3,0,2,1:T(4,128)(2,1)S(1)} %get-tuple-element.7), channel_id=5, source_target_pairs={{1,0},{2,1},{3,2},{4,3},{5,4},{6,5},{7,6},{9,8},{10,9},{11,10},{12... | collective-permute-start | bytes 73736 | tf_op jit(solution)/conv_general_dilated | solution.py:26
  38.3 0.0 collective-permute-done.3
  38.3 2.4 %collective-permute-done.4 = bf16[4,1,8,384]{3,0,2,1:T(4,128)(2,1)S(1)} collective-permute-done((bf16[4,1,8,384]{3,0,2,1:T(4,128)(2,1)S(1)}, bf16[4,1,8,384]{3,0,2,1:T(4,128)(2,1)S(1)}, u32[]{:S(2)}, u32[]{:S(2)}) %collective-permute-start.4) | collective-permute-done | bytes 24608 | tf_op jit(solution)/conv_general_dilated | solution.py:26
  40.7 0.0 copy-done.3
  40.7 0.0 copy-done.4
  40.7 2.9 %multiply_reduce_fusion = (f32[4,24,8]{0,2,1:T(8,128)S(1)}, f32[4,24,8,192]{3,0,2,1:T(4,128)S(1)}) fusion(f32[192]{0:T(256)S(1)} %copy-done.4, bf16[3,3,384,192]{2,3,1,0:T(8,128)(2,1)S(1)} %copy-done.3, bf16[4,1,8,384]{3,0,2,1:T(4,128)(2,1)S(1)} %collective-permute-done.4, bf16[4,24,8,384]{3,0,2,1:T(4,128)(2,1)S(1)} %bitcast.24, ...), kind=kOutput, calls=%fused_computation.21 | convolution fusion | flops 938532096 | bytes 2559748 | tf_op jit(solution)/conv_general_dilated | solution.py:26
  43.6 0.1 copy.13
  43.7 0.6 add_rsqrt_fusion.1
  44.3 0.8 %copy.14 = f32[4,24,8]{0,2,1:T(8,128)S(1)} copy(f32[4,24,8]{1,2,0:T(8,128)} %add_rsqrt_fusion.1) | data formatting | bytes 6144 | tf_op jit(solution)/rsqrt | solution.py:11
  45.2 1.2 %fusion.31 = bf16[1,4,24,8,192]{4,1,3,2,0:T(4,128)(2,1)S(1)} fusion(f32[192]{0:T(256)} %param.6, f32[4,24,8,192]{3,0,2,1:T(4,128)S(1)} %get-tuple-element.11, f32[4,24,8]{0,2,1:T(8,128)S(1)} %copy.14), kind=kLoop, calls=%fused_computation.39 | loop fusion | flops 1032192 | bytes 888576 | tf_op jit(solution)/broadcast_in_dim | solution.py:16
  46.4 0.2 slice.13
  46.6 1.9 %collective-permute-start.5 = (bf16[1,2,24,8,192]{4,1,3,2,0:T(2,128)(2,1)S(1)}, bf16[1,2,24,8,192]{4,1,3,2,0:T(2,128)(2,1)S(1)}, u32[]{:S(2)}, u32[]{:S(2)}) collective-permute-start(bf16[1,2,24,8,192]{4,1,3,2,0:T(2,128)(2,1)S(1)} %slice.13), channel_id=6, source_target_pairs={{0,8},{1,9},{2,10},{3,11},{4,12},{5,13},{6,14},{7,15},{8,16},{9,17... | collective-permute-start | bytes 442376 | tf_op jit(solution)/conv_general_dilated | solution.py:15
  48.5 9.2 %collective-permute-done.5 = bf16[1,2,24,8,192]{4,1,3,2,0:T(2,128)(2,1)S(1)} collective-permute-done((bf16[1,2,24,8,192]{4,1,3,2,0:T(2,128)(2,1)S(1)}, bf16[1,2,24,8,192]{4,1,3,2,0:T(2,128)(2,1)S(1)}, u32[]{:S(2)}, u32[]{:S(2)}) %collective-permute-start.5) | collective-permute-done | bytes 147488 | tf_op jit(solution)/conv_general_dilated | solution.py:15
  57.7 0.5 fusion.4
  58.2 3.4 %collective-permute-start.6 = (bf16[1,6,1,8,192]{4,1,3,2,0:T(8,128)(2,1)S(1)}, bf16[1,6,1,8,192]{4,1,3,2,0:T(8,128)(2,1)S(1)}, u32[]{:S(2)}, u32[]{:S(2)}) collective-permute-start(bf16[1,6,1,8,192]{4,1,3,2,0:T(8,128)(2,1)S(1)} %get-tuple-element.4), channel_id=7, source_target_pairs={{0,1},{1,2},{2,3},{3,4},{4,5},{5,6},{6,7},{8,9},{9,10},{10,11},{11... | collective-permute-start | bytes 55304 | tf_op jit(solution)/conv_general_dilated | solution.py:15
  61.6 1.9 %collective-permute-start.7 = (bf16[1,6,1,8,192]{4,1,3,2,0:T(8,128)(2,1)S(1)}, bf16[1,6,1,8,192]{4,1,3,2,0:T(8,128)(2,1)S(1)}, u32[]{:S(2)}, u32[]{:S(2)}) collective-permute-start(bf16[1,6,1,8,192]{4,1,3,2,0:T(8,128)(2,1)S(1)} %get-tuple-element.5), channel_id=8, source_target_pairs={{1,0},{2,1},{3,2},{4,3},{5,4},{6,5},{7,6},{9,8},{10,9},{11,10},{12... | collective-permute-start | bytes 55304 | tf_op jit(solution)/conv_general_dilated | solution.py:15
  63.5 0.0 collective-permute-done.6
  63.5 3.3 %collective-permute-done.7 = bf16[1,6,1,8,192]{4,1,3,2,0:T(8,128)(2,1)S(1)} collective-permute-done((bf16[1,6,1,8,192]{4,1,3,2,0:T(8,128)(2,1)S(1)}, bf16[1,6,1,8,192]{4,1,3,2,0:T(8,128)(2,1)S(1)}, u32[]{:S(2)}, u32[]{:S(2)}) %collective-permute-start.7) | collective-permute-done | bytes 18464 | tf_op jit(solution)/conv_general_dilated | solution.py:15
  66.8 0.5 fusion.3
  67.4 0.0 copy-done
  67.4 0.0 copy-start.2
  67.4 12.4 %fusion.9 = f32[1,4,24,8,192]{4,0,3,2,1:T(1,128)S(1)} fusion(bf16[3,3,3,192,192]{4,3,2,1,0:T(8,128)(2,1)S(1)} %copy-done, bf16[1,6,26,8,192]{4,1,3,2,0:T(8,128)(2,1)S(1)} %fusion.3), kind=kOutput, calls=%fused_computation.12 | convolution fusion | flops 1401421824 | bytes 3059712 | tf_op jit(solution)/conv_general_dilated | solution.py:15
  79.8 0.0 copy-done.2
  79.8 0.6 fusion.14
  80.4 0.8 copy.17
  (5 shorter events, 0.1 us)
Async XLA Ops:
  0.0 67.4 %copy-start = (bf16[3,3,3,192,192]{4,3,2,1,0:T(8,128)(2,1)S(1)}, bf16[3,3,3,192,192]{4,3,2,1,0:T(8,128)(2,1)}, u32[]{:S(2)}) copy-start(bf16[3,3,3,192,192]{4,3,2,1,0:T(8,128)(2,1)} %param.7) | copy-start | bytes 5971972
  2.4 8.4 %collective-permute-start = (bf16[1,2,12,4,384]{4,3,2,1,0:T(4,128)(2,1)S(1)}, bf16[1,2,12,4,384]{4,3,2,1,0:T(4,128)(2,1)S(1)}, u32[]{:S(2)}, u32[]{:S(2)}) collective-permute-start(bf16[1,2,12,4,384]{4,3,2,1,0:T(4,128)(2,1)S(1)} %slice.8), channel_id=1, source_target_pairs={{0,8},{1,9},{2,10},{3,11},{4,12},{5,13},{6,14},{7,15},{8,16},{9,17... | collective-permute-start | bytes 221192 | tf_op jit(solution)/conv_general_dilated | solution.py:15
  11.0 8.8 %collective-permute-start.1 = (bf16[1,6,1,4,384]{4,3,2,1,0:T(4,128)(2,1)S(1)}, bf16[1,6,1,4,384]{4,3,2,1,0:T(4,128)(2,1)S(1)}, u32[]{:S(2)}, u32[]{:S(2)}) collective-permute-start(bf16[1,6,1,4,384]{4,3,2,1,0:T(4,128)(2,1)S(1)} %get-tuple-element.8), channel_id=2, source_target_pairs={{0,1},{1,2},{2,3},{3,4},{4,5},{5,6},{6,7},{8,9},{9,10},{10,11},{11... | collective-permute-start | bytes 55304 | tf_op jit(solution)/conv_general_dilated | solution.py:15
  15.9 5.1 %collective-permute-start.2 = (bf16[1,6,1,4,384]{4,3,2,1,0:T(4,128)(2,1)S(1)}, bf16[1,6,1,4,384]{4,3,2,1,0:T(4,128)(2,1)S(1)}, u32[]{:S(2)}, u32[]{:S(2)}) collective-permute-start(bf16[1,6,1,4,384]{4,3,2,1,0:T(4,128)(2,1)S(1)} %get-tuple-element.9), channel_id=3, source_target_pairs={{1,0},{2,1},{3,2},{4,3},{5,4},{6,5},{7,6},{9,8},{10,9},{11,10},{12... | collective-permute-start | bytes 55304 | tf_op jit(solution)/conv_general_dilated | solution.py:15
  21.2 11.4 %copy-start.1 = (f32[384]{0:T(512)S(1)}, f32[384]{0:T(512)}, u32[]{:S(2)}) copy-start(f32[384]{0:T(512)} %param.3) | copy-start | bytes 4612
  32.6 8.0 %copy-start.3 = (bf16[3,3,384,192]{2,3,1,0:T(8,128)(2,1)S(1)}, bf16[3,3,384,192]{2,3,1,0:T(8,128)(2,1)}, u32[]{:S(2)}) copy-start(bf16[3,3,384,192]{2,3,1,0:T(8,128)(2,1)} %param.4) | copy-start | bytes 3981316
  32.7 8.0 %copy-start.4 = (f32[192]{0:T(256)S(1)}, f32[192]{0:T(256)}, u32[]{:S(2)}) copy-start(f32[192]{0:T(256)} %param.5) | copy-start | bytes 2308
  33.1 5.2 %collective-permute-start.3 = (bf16[4,1,8,384]{3,0,2,1:T(4,128)(2,1)S(1)}, bf16[4,1,8,384]{3,0,2,1:T(4,128)(2,1)S(1)}, u32[]{:S(2)}, u32[]{:S(2)}) collective-permute-start(bf16[4,1,8,384]{3,0,2,1:T(4,128)(2,1)S(1)} %get-tuple-element.6), channel_id=4, source_target_pairs={{0,1},{1,2},{2,3},{3,4},{4,5},{5,6},{6,7},{8,9},{9,10},{10,11},{11... | collective-permute-start | bytes 73736 | tf_op jit(solution)/conv_general_dilated | solution.py:26
  35.5 5.1 %collective-permute-start.4 = (bf16[4,1,8,384]{3,0,2,1:T(4,128)(2,1)S(1)}, bf16[4,1,8,384]{3,0,2,1:T(4,128)(2,1)S(1)}, u32[]{:S(2)}, u32[]{:S(2)}) collective-permute-start(bf16[4,1,8,384]{3,0,2,1:T(4,128)(2,1)S(1)} %get-tuple-element.7), channel_id=5, source_target_pairs={{1,0},{2,1},{3,2},{4,3},{5,4},{6,5},{7,6},{9,8},{10,9},{11,10},{12... | collective-permute-start | bytes 73736 | tf_op jit(solution)/conv_general_dilated | solution.py:26
  46.6 11.1 %collective-permute-start.5 = (bf16[1,2,24,8,192]{4,1,3,2,0:T(2,128)(2,1)S(1)}, bf16[1,2,24,8,192]{4,1,3,2,0:T(2,128)(2,1)S(1)}, u32[]{:S(2)}, u32[]{:S(2)}) collective-permute-start(bf16[1,2,24,8,192]{4,1,3,2,0:T(2,128)(2,1)S(1)} %slice.13), channel_id=6, source_target_pairs={{0,8},{1,9},{2,10},{3,11},{4,12},{5,13},{6,14},{7,15},{8,16},{9,17... | collective-permute-start | bytes 442376 | tf_op jit(solution)/conv_general_dilated | solution.py:15
  58.2 5.3 %collective-permute-start.6 = (bf16[1,6,1,8,192]{4,1,3,2,0:T(8,128)(2,1)S(1)}, bf16[1,6,1,8,192]{4,1,3,2,0:T(8,128)(2,1)S(1)}, u32[]{:S(2)}, u32[]{:S(2)}) collective-permute-start(bf16[1,6,1,8,192]{4,1,3,2,0:T(8,128)(2,1)S(1)} %get-tuple-element.4), channel_id=7, source_target_pairs={{0,1},{1,2},{2,3},{3,4},{4,5},{5,6},{6,7},{8,9},{9,10},{10,11},{11... | collective-permute-start | bytes 55304 | tf_op jit(solution)/conv_general_dilated | solution.py:15
  61.6 5.2 %collective-permute-start.7 = (bf16[1,6,1,8,192]{4,1,3,2,0:T(8,128)(2,1)S(1)}, bf16[1,6,1,8,192]{4,1,3,2,0:T(8,128)(2,1)S(1)}, u32[]{:S(2)}, u32[]{:S(2)}) collective-permute-start(bf16[1,6,1,8,192]{4,1,3,2,0:T(8,128)(2,1)S(1)} %get-tuple-element.5), channel_id=8, source_target_pairs={{1,0},{2,1},{3,2},{4,3},{5,4},{6,5},{7,6},{9,8},{10,9},{11,10},{12... | collective-permute-start | bytes 55304 | tf_op jit(solution)/conv_general_dilated | solution.py:15
  67.4 12.4 %copy-start.2 = (f32[192]{0:T(256)S(1)}, f32[192]{0:T(256)}, u32[]{:S(2)}) copy-start(f32[192]{0:T(256)} %param.8) | copy-start | bytes 2308
where the time goes:
time: 81.7 us; the launch traced here: 81.2 us
  matrix products  26.7 us (33%)
  starting transfers between devices  21.7 us (27%)
  waiting for transfers between devices  19.5 us (24%)
  other arithmetic  6.23 us (8%)
  local copies, waits for them, and re-layouts  4.91 us (6%)
  between operations  2.24 us (3%)
    conv_general_dilated x2, matrix products, causal_conv(): lax.conv_general_dilated(act.astype(jnp.float32)[None], kernel.astype(jnp...  23.8 us
    conv_general_dilated x6, starting transfers between devices, causal_conv(): lax.conv_general_dilated(act.astype(jnp.float32)[None], kernel.astype(jnp...  17.2 us
    conv_general_dilated x6, waiting for transfers between devices, causal_conv(): lax.conv_general_dilated(act.astype(jnp.float32)[None], kernel.astype(jnp...  17.1 us
    conv_general_dilated x2, starting transfers between devices, plane_conv(): lax.conv_general_dilated(act.astype(jnp.float32), kernel.astype(jnp.float...  4.54 us
    conv_general_dilated x1, matrix products, plane_conv(): lax.conv_general_dilated(act.astype(jnp.float32), kernel.astype(jnp.float...  2.86 us
    conv_general_dilated x6, local copies, waits for them, and re-layouts, causal_conv(): lax.conv_general_dilated(act.astype(jnp.float32)[None], kernel.astype(jnp...  2.81 us
    conv_general_dilated x2, waiting for transfers between devices, plane_conv(): lax.conv_general_dilated(act.astype(jnp.float32), kernel.astype(jnp.float...  2.38 us
    broadcast_in_dim x2, other arithmetic, causal_conv(): act.astype(jnp.float32)[None]  2.36 us
  transfers between devices with their start and end apart: 8, of which 5 were waited for; matrix products, arithmetic and copies ran while one was open for 3% of the time, Pallas kernels for 0%

commit v1 on v0

v1 whole, which is shorter than its diff:
```python
import functools

import jax
import jax.numpy as jnp
from jax import lax
from jax.experimental import pallas as pl
from jax.experimental.pallas import tpu as pltpu
from jax.sharding import PartitionSpec as P

EPS = 1e-6
BF = jnp.bfloat16
F32 = jnp.float32


def silu(v):
    half = 0.5 * v
    return half + half * jnp.tanh(half)


def dot(a, b):
    return jnp.dot(a, b, preferred_element_type=F32)


def kernel(last, x, prev, above, below, gain0, wc, bias0, w4, bias1, gain1, wf, bias2, out,
           raw, left, mid, lift, planes, nat, back):
    group = lax.axis_index("tm")
    strip = lax.axis_index("strip")
    c0 = wc.shape[-1]
    c1 = wf.shape[-1]
    for t in range(8):
        src, f = (prev, t) if t < 4 else (x, t - 4)
        base = 64 * t
        for h in range(16):
            v = above[t, h] if h < 2 else below[t, h - 14] if h > 13 else src[f, h - 2]
            for c in range(3):
                raw[c, base + 4 * h:base + 4 * h + 4, :] = v[:, 128 * c:128 * c + 128].astype(F32)
    g0 = gain0[...]
    for t in range(8):
        v = jnp.concatenate([raw[c, 64 * t:64 * t + 64, :] for c in range(3)], axis=1)
        r = lax.rsqrt(jnp.mean(v * v, axis=-1, keepdims=True) + EPS)
        v = silu(v * r * g0)
        for c in range(3):
            raw[c, 64 * t:64 * t + 64, :] = v[:, 128 * c:128 * c + 128]
    for kh in range(3):
        for t in range(8):
            for w in range(4):
                for c in range(3):
                    v = raw[c, pl.ds(64 * t + 4 * kh + w, 16, stride=4), :]
                    left[kh, 64 * t + 16 * w:64 * t + 16 * w + 16, 128 * c:128 * c + 128] = v.astype(BF)

    def taps(kw, lo, n):
        cols = []
        for kt in range(3):
            for kh in range(3):
                cols.append(jnp.concatenate(
                    [left[kh, 64 * (t + kt) + 16 * lo:64 * (t + kt) + 16 * (lo + n), :] for t in range(6)], axis=0))
        lhs = jnp.concatenate(cols, axis=1)
        rhs = jnp.concatenate([wc[kt, kh, kw] for kt in range(3) for kh in range(3)], axis=0)
        return dot(lhs, rhs)

    b0 = bias0[...]
    mid[0:384, :] = taps(1, 0, 4) + b0
    p = taps(0, 0, 3)
    for t in range(6):
        mid[64 * t + 16:64 * t + 64, :] += p[48 * t:48 * t + 48]
    p = taps(2, 1, 3)
    for t in range(6):
        mid[64 * t:64 * t + 48, :] += p[48 * t:48 * t + 48]
    row = lax.broadcasted_iota(jnp.int32, (16, c0), 0)
    keep = jnp.logical_and(jnp.logical_or(strip > 0, row != 0), jnp.logical_or(strip < last, row != 13))
    for t in range(6):
        for w in range(4):
            at = 64 * t + 16 * w
            v = jnp.where(keep, mid[at:at + 16, :], 0.0)
            mid[at:at + 16, :] = v
    for t in range(6):
        for w in range(4):
            at = 64 * t + 16 * w
            left[0, at:at + 16, :] = mid[at:at + 16, :].astype(BF)
            left[1, at:at + 16, :] = mid[at + 1:at + 17, :].astype(BF)

    def ups(lo, n):
        a = jnp.concatenate([left[0, 64 * t + 16 * lo:64 * t + 16 * (lo + n), :] for t in range(6)], axis=0)
        b = jnp.concatenate([left[1, 64 * t + 16 * lo:64 * t + 16 * (lo + n), :] for t in range(6)], axis=0)
        return jnp.concatenate([a, b], axis=1)

    b1 = bias1[...]
    b1 = jnp.concatenate([b1, b1], axis=1)
    g1 = gain1[...]
    g1 = jnp.concatenate([g1, g1], axis=1)
    lane = lax.broadcasted_iota(jnp.int32, (16, 2 * c1), 1)
    even = lane < c1
    row = lax.broadcasted_iota(jnp.int32, (16, 2 * c1), 0)

    def finish(u, p, t, a):
        l = (u + b1).astype(BF).astype(F32)
        lift[a, p, 16 * t:16 * t + 16, :] = l
        sq = l * l
        me = jnp.sum(jnp.where(even, sq, 0.0), axis=-1, keepdims=True) * (1.0 / c1)
        mo = jnp.sum(jnp.where(even, 0.0, sq), axis=-1, keepdims=True) * (1.0 / c1)
        r = jnp.where(even, lax.rsqrt(me + EPS), lax.rsqrt(mo + EPS))
        v = silu(l * r * g1)
        if p == 0:
            v = jnp.where(even, v, 0.0)
        if p == 4:
            v = jnp.where(even, 0.0, v)
        if a == 0:
            ok = jnp.logical_or(strip < last, row != 12)
        else:
            ok = jnp.logical_or(strip > 0, row != 0)
        if t < 2:
            ok = jnp.logical_and(ok, group > 0)
        nat[a, 0:16, 0:2 * c1] = jnp.where(ok, v, 0.0)
        planes[a, 0, p, 16 * t:16 * t + 16, :] = nat[a, 0:16, 0:2 * c1].astype(BF)
        planes[a, 1, p, 16 * t:16 * t + 16, :] = nat[a, 1:17, 0:2 * c1].astype(BF)

    u = dot(jnp.concatenate([ups(0, 3), ups(1, 3)], axis=1), w4[...])
    for t in range(6):
        for p in range(1, 4):
            for a in range(2):
                finish(u[48 * t + 16 * p - 16:48 * t + 16 * p, 2 * c1 * a:2 * c1 * (a + 1)], p, t, a)
    u = dot(ups(0, 1), w4[2 * c0:, :])
    for t in range(6):
        for a in range(2):
            finish(u[16 * t:16 * t + 16, 2 * c1 * a:2 * c1 * (a + 1)], 0, t, a)
    u = dot(ups(3, 1), w4[:2 * c0, :])
    for t in range(6):
        for a in range(2):
            finish(u[16 * t:16 * t + 16, 2 * c1 * a:2 * c1 * (a + 1)], 4, t, a)

    b2 = bias2[...]
    zero = jnp.zeros((64, c1), BF)
    for a in range(2):
        reads = ((1, 0), (0, 0), (1, 1)) if a == 0 else ((0, 0), (1, 1), (0, 1))
        for b in range(2):
            cols, rhs = [], []
            for kt in range(3):
                for kh in range(3):
                    ph, sh = reads[kh]
                    first = jnp.concatenate([planes[ph, sh, q, 16 * kt:16 * kt + 64, :] for q in range(4)], axis=0)
                    second = jnp.concatenate([planes[ph, sh, q + 1, 16 * kt:16 * kt + 64, :] for q in range(4)], axis=0)
                    k0, k1, k2 = (wf[kt, kh, kw] for kw in range(3))
                    if b == 0:
                        cols += [first, second[:, 128:]]
                        rhs += [k1, k0, zero, k2]
                    else:
                        cols += [first[:, :256], second]
                        rhs += [k0, zero, k2, k1]
            d = dot(jnp.concatenate(cols, axis=1), jnp.concatenate(rhs, axis=0)) + b2
            for q in range(4):
                for t in range(4):
                    p = q if b == 0 else q + 1
                    at = 16 * (t + 2) + a
                    l = lift[a, p, at:at + 12, :]
                    l = l[:, :c1] if b == 0 else l[:, c1:]
                    v = d[64 * q + 16 * t:64 * q + 16 * t + 12, :] + l
                    nat_rows = pl.ds((24 * t + a) * 8 + 2 * q + b, 12, stride=16)
                    back[0, nat_rows, :] = v[:, :128]
                    back[1, nat_rows, 0:64] = v[:, 128:]
    for t in range(4):
        v = jnp.concatenate([back[0, 192 * t:192 * t + 192, :], back[1, 192 * t:192 * t + 192, 0:64]], axis=1)
        out[t] = v.reshape(24, 8, c1).astype(BF)


def block(x, gain0, wc, bias0, wu, bias1, gain1, wf, bias2, *, nt, ns):
    c0, c1 = wc.shape[-1], wf.shape[-1]
    at = lambda t, s: t * ns + s
    axes = ("tm", "strip")
    prev = lax.ppermute(x, axes, [(at(t, s), at(t + 1, s)) for t in range(nt - 1) for s in range(ns)])
    both = jnp.concatenate([prev, x], axis=0)
    above = lax.ppermute(both[:, 10:], axes, [(at(t, s), at(t, s + 1)) for t in range(nt) for s in range(ns - 1)])
    below = lax.ppermute(both[:, :2], axes, [(at(t, s + 1), at(t, s)) for t in range(nt) for s in range(ns - 1)])
    f = wu.astype(F32)
    first, second = ((0,), (1, 2)), ((0, 1), (2,))
    pick = (first, second)
    rows = []
    for wcol in range(2):
        for hrow in range(2):
            rows.append(jnp.concatenate(
                [sum(f[kh, kw] for kh in pick[a][hrow] for kw in pick[b][wcol]) for a in range(2) for b in range(2)],
                axis=1))
    w4 = jnp.concatenate(rows, axis=0).astype(BF)
    vm = pl.BlockSpec(memory_space=pltpu.VMEM)
    two = lambda v: v.reshape(1, -1)
    return pl.pallas_call(
        functools.partial(kernel, ns - 1),
        out_shape=jax.ShapeDtypeStruct((4, 24, 8, c1), BF),
        in_specs=[vm] * 12,
        out_specs=vm,
        scratch_shapes=[
            pltpu.VMEM((3, 528, 128), F32),
            pltpu.VMEM((3, 512, c0), BF),
            pltpu.VMEM((400, c0), F32),
            pltpu.VMEM((2, 5, 112, 2 * c1), F32),
            pltpu.VMEM((2, 2, 5, 96, 2 * c1), BF),
            pltpu.VMEM((2, 32, 2 * c1), F32),
            pltpu.VMEM((2, 768, 128), F32),
        ],
        compiler_params=pltpu.CompilerParams(vmem_limit_bytes=40 << 20),
    )(x, prev, above, below, two(gain0), wc, two(bias0), w4, jnp.concatenate([two(bias1)], axis=1), two(gain1), wf, two(bias2))


def solution(mesh):
    nt, ns = mesh.shape["tm"], mesh.shape["strip"]
    part = P("tm", "strip", None, None)
    return jax.shard_map(
        functools.partial(block, nt=nt, ns=ns), mesh=mesh,
        in_specs=(part,) + (P(),) * 8, out_specs=part, check_vma=False)
```

time: 81.7 us -> 52.4 us (0.64)
  matrix products: 26.7 us -> 0 us
  other arithmetic: 6.23 us -> 25.9 us
  waiting for transfers between devices: 19.5 us -> 3.36 us
  starting transfers between devices: 21.7 us -> 9.65 us
  Pallas kernels: 0 us -> 10.2 us
  local copies, waits for them, and re-layouts: 4.91 us -> 2.83 us
  between operations: 2.24 us -> 0.27 us
    conv_general_dilated x3 -> x0, matrix products: 26.7 us -> none  [the longest x2 23.8 us: causal_conv(): lax.conv_general_dilated(act.astype(jnp.float32)[None], kernel.astype(jnp...]
    concatenate x0 -> x1, other arithmetic: none -> 25 us  [block(): w4 = jnp.concatenate(rows, axis=0).astype(BF)]
    conv_general_dilated x8 -> x0, starting transfers between devices: 21.7 us -> none  [the longest x6 17.2 us: causal_conv(): lax.conv_general_dilated(act.astype(jnp.float32)[None], kernel.astype(jnp...]
    conv_general_dilated x8 -> x0, waiting for transfers between devices: 19.5 us -> none  [the longest x6 17.1 us: causal_conv(): lax.conv_general_dilated(act.astype(jnp.float32)[None], kernel.astype(jnp...]
    pallas_call x0 -> x1, Pallas kernels: none -> 10.2 us  [block(): pl.pallas_call(functools.partial(kernel, ns - 1), out_shape=jax.ShapeDtyp...]
    ppermute x0 -> x3, starting transfers between devices: none -> 9.65 us  [the longest x1 4.62 us: block(): lax.ppermute(both[:, 10:], axes, [(at(t, s), at(t, s + 1)) for t in range...]
    ppermute x0 -> x3, waiting for transfers between devices: none -> 3.36 us  [the longest x1 3.35 us: block(): lax.ppermute(x, axes, [(at(t, s), at(t + 1, s)) for t in range(nt - 1) fo...]
    conv_general_dilated x7 -> x0, local copies, waits for them, and re-layouts: 2.83 us -> none  [the longest x6 2.81 us: causal_conv(): lax.conv_general_dilated(act.astype(jnp.float32)[None], kernel.astype(jnp...]
  transfers between devices with their start and end apart: 8 -> 3, of which waited for: 5 -> 1; matrix products, arithmetic and copies ran while one was open for 3% -> 55% of each run, Pallas kernels for 0% -> 0%
where the time goes in v1:
time: 52.4 us; the launch traced here: 52.2 us
  other arithmetic  25.9 us (49%)
  Pallas kernels  10.2 us (19%)
  starting transfers between devices  9.65 us (18%)
  waiting for transfers between devices  3.36 us (6%)
  local copies, waits for them, and re-layouts  2.83 us (5%)
    concatenate x1, other arithmetic, block(): w4 = jnp.concatenate(rows, axis=0).astype(BF)  25 us
    pallas_call x1, Pallas kernels, block(): pl.pallas_call(functools.partial(kernel, ns - 1), out_shape=jax.ShapeDtyp...  10.2 us
    ppermute x1, starting transfers between devices, block(): lax.ppermute(both[:, 10:], axes, [(at(t, s), at(t, s + 1)) for t in range...  4.62 us
    ppermute x1, waiting for transfers between devices, block(): lax.ppermute(x, axes, [(at(t, s), at(t + 1, s)) for t in range(nt - 1) fo...  3.35 us
    ppermute x1, starting transfers between devices, block(): lax.ppermute(x, axes, [(at(t, s), at(t + 1, s)) for t in range(nt - 1) fo...  3.11 us
    unnamed x20, local copies, waits for them, and re-layouts  2.64 us
    ppermute x1, starting transfers between devices, block(): lax.ppermute(both[:, :2], axes, [(at(t, s + 1), at(t, s)) for t in range(...  1.92 us
  transfers between devices with their start and end apart: 3, of which 1 were waited for; matrix products, arithmetic and copies ran while one was open for 55% of the time, Pallas kernels for 0%

profile of v1, /device:TPU:137, one launch (start us, length us, event | category | flops | bytes accessed | tf_op | source)
XLA Modules:
  0.0 52.2 jit_solution(10847720417862881537)
XLA Ops:
  0.0 3.1 %collective-permute-start = (bf16[4,12,4,384]{3,2,1,0:T(4,128)(2,1)}, bf16[4,12,4,384]{3,2,1,0:T(4,128)(2,1)S(1)}, u32[]{:S(2)}, u32[]{:S(2)}) collective-permute-start(bf16[4,12,4,384]{3,2,1,0:T(4,128)(2,1)} %x.1), channel_id=1, source_target_pairs={{0,8},{1,9},{2,10},{3,11},{4,12},{5,13},{6,14},{7,15},{8,16},{9,17... | collective-permute-start | bytes 442376 | tf_op jit(solution)/shard_map/ppermute | solution.py:169
  3.1 2.5 %copy.10 = bf16[3,3,384,192]{3,2,1,0:T(8,128)(2,1)S(1)} copy(bf16[3,3,384,192]{2,3,1,0:T(8,128)(2,1)} %param.13) | data formatting | bytes 2654208 | tf_op args[4]
  5.7 0.3 convert_element_type.4
  6.0 0.0 copy-start.1
  6.0 0.0 slice-start
  6.0 0.3 fusion.6
  6.3 0.0 slice-start.1
  6.4 0.3 add_convert_fusion.8
  6.6 0.0 copy-start.5
  6.6 0.0 copy-start.6
  6.7 0.0 copy-start
  6.7 0.0 copy-start.2
  6.7 0.0 copy-start.3
  6.7 0.0 copy-start.4
  6.7 0.1 fusion.2
  6.8 3.4 %collective-permute-done.prev = bf16[4,12,4,384]{3,2,1,0:T(4,128)(2,1)S(1)} collective-permute-done((bf16[4,12,4,384]{3,2,1,0:T(4,128)(2,1)}, bf16[4,12,4,384]{3,2,1,0:T(4,128)(2,1)S(1)}, u32[]{:S(2)}, u32[]{:S(2)}) %collective-permute-start) | collective-permute-done | bytes 147488 | tf_op jit(solution)/shard_map/ppermute | solution.py:169
  10.1 0.1 constant_dynamic-update-slice_fusion.1
  10.2 0.0 copy-done.1
  10.2 0.1 constant_dynamic-update-slice_fusion
  10.3 4.6 %collective-permute-start.1 = (bf16[8,2,4,384]{3,2,1,0:T(4,128)(2,1)S(1)}, bf16[8,2,4,384]{3,2,1,0:T(4,128)(2,1)S(1)}, u32[]{:S(2)}, u32[]{:S(2)}) collective-permute-start(bf16[8,2,4,384]{3,2,1,0:T(4,128)(2,1)S(1)} %get-tuple-element.22), channel_id=1, source_target_pairs={{0,1},{1,2},{2,3},{3,4},{4,5},{5,6},{6,7},{8,9},{9,10},{10,11},{11... | collective-permute-start | bytes 147464 | tf_op jit(solution)/shard_map/ppermute | solution.py:171
  15.0 1.9 %collective-permute-start.2 = (bf16[8,2,4,384]{3,2,1,0:T(4,128)(2,1)S(1)}, bf16[8,2,4,384]{3,2,1,0:T(4,128)(2,1)S(1)}, u32[]{:S(2)}, u32[]{:S(2)}) collective-permute-start(bf16[8,2,4,384]{3,2,1,0:T(4,128)(2,1)S(1)} %get-tuple-element.21), channel_id=1, source_target_pairs={{1,0},{2,1},{3,2},{4,3},{5,4},{6,5},{7,6},{9,8},{10,9},{11,10},{12... | collective-permute-start | bytes 147464 | tf_op jit(solution)/shard_map/ppermute | solution.py:172
  16.9 25.0 %maximum_maximum_fusion.w4 = bf16[1536,768]{1,0:T(8,128)(2,1)S(1)} fusion(bf16[384,192]{1,0:T(8,128)(2,1)S(1)} %get-tuple-element.6, bf16[384,192]{1,0:T(8,128)(2,1)S(1)} %get-tuple-element.19, bf16[384,192]{1,0:T(8,128)(2,1)S(1)} %get-tuple-element.18, bf16[384,192]{1,0:T(8,128)(2,1)S(1)} %get-tuple-element.11, bf16[384,192]{1,0:T(8,128)(2,1)S(1)} %get-tuple-element.14, ...), kind=kLoop, calls=%fused_computation | loop fusion | flops 37748736 | bytes 4718592 | tf_op jit(solution)/shard_map/concatenate | solution.py:182
  41.9 0.0 copy-done.5
  41.9 0.0 copy-done.6
  42.0 0.0 collective-permute-done.1.above
  42.0 0.0 collective-permute-done.2.below
  42.0 0.0 slice-done
  42.0 0.0 slice-done.1
  42.0 0.0 copy-done
  42.0 0.0 copy-done.2
  42.0 0.0 copy-done.3
  42.0 0.0 copy-done.4
  42.0 10.2 %shard_map.91 = bf16[4,24,8,192]{3,2,1,0:T(8,128)(2,1)} custom-call(bf16[4,12,4,384]{3,2,1,0:T(4,128)(2,1)S(1)} %copy-done.1, bf16[4,12,4,384]{3,2,1,0:T(4,128)(2,1)S(1)} %collective-permute-done.prev, bf16[8,2,4,384]{3,2,1,0:T(4,128)(2,1)S(1)} %collective-permute-done.1.above, bf16[8,2,4,384]{3,2,1,0:T(4,128)(2,1)S(1)} %collective-permute-done.2.below, ...), custom_call_target="tpu_custom_call" | custom-call | tf_op jit(solution)/shard_map/pallas_call | solution.py:185
  (4 shorter events, 0.0 us)
Async XLA Ops:
  0.0 10.1 %collective-permute-start = (bf16[4,12,4,384]{3,2,1,0:T(4,128)(2,1)}, bf16[4,12,4,384]{3,2,1,0:T(4,128)(2,1)S(1)}, u32[]{:S(2)}, u32[]{:S(2)}) collective-permute-start(bf16[4,12,4,384]{3,2,1,0:T(4,128)(2,1)} %x.1), channel_id=1, source_target_pairs={{0,8},{1,9},{2,10},{3,11},{4,12},{5,13},{6,14},{7,15},{8,16},{9,17... | collective-permute-start | bytes 442376 | tf_op jit(solution)/shard_map/ppermute | solution.py:169
  6.0 4.2 %copy-start.1 = (bf16[4,12,4,384]{3,2,1,0:T(4,128)(2,1)S(1)}, bf16[4,12,4,384]{3,2,1,0:T(4,128)(2,1)}, u32[]{:S(2)}) copy-start(bf16[4,12,4,384]{3,2,1,0:T(4,128)(2,1)} %x.1) | copy-start | bytes 442372
  6.0 36.0 %slice-start = ((s8[7962624]{0:T(1024)(128)(4,1)}), s8[4194304]{0:T(1024)(128)(4,1)S(1)}, s32[]{:S(2)}) async-start(s8[7962624]{0:T(1024)(128)(4,1)} %bitcast.101), calls=%async_computation | async-start | bytes 8388608
  6.3 35.6 %slice-start.1 = ((s8[7962624]{0:T(1024)(128)(4,1)}), s8[3768320]{0:T(1024)(128)(4,1)S(1)}, s32[]{:S(2)}) async-start(s8[7962624]{0:T(1024)(128)(4,1)} %bitcast.101), calls=%async_computation.1 | async-start | bytes 7536640
  6.6 35.3 %copy-start.5 = (f32[384]{0:T(512)S(1)}, f32[384]{0:T(512)}, u32[]{:S(2)}) copy-start(f32[384]{0:T(512)} %param.10) | copy-start | bytes 4612
  6.6 35.3 %copy-start.6 = (f32[384]{0:T(512)S(1)}, f32[384]{0:T(512)}, u32[]{:S(2)}) copy-start(f32[384]{0:T(512)} %param.12) | copy-start | bytes 4612
  6.7 35.3 %copy-start = (bf16[3,3,3,192,192]{4,3,2,1,0:T(8,128)(2,1)S(1)}, bf16[3,3,3,192,192]{4,3,2,1,0:T(8,128)(2,1)}, u32[]{:S(2)}) copy-start(bf16[3,3,3,192,192]{4,3,2,1,0:T(8,128)(2,1)} %wf.1) | copy-start | bytes 5971972
  6.7 35.3 %copy-start.2 = (f32[192]{0:T(256)S(1)}, f32[192]{0:T(256)}, u32[]{:S(2)}) copy-start(f32[192]{0:T(256)} %param.14) | copy-start | bytes 2308
  6.7 35.3 %copy-start.3 = (f32[192]{0:T(256)S(1)}, f32[192]{0:T(256)}, u32[]{:S(2)}) copy-start(f32[192]{0:T(256)} %param.15) | copy-start | bytes 2308
  6.7 35.3 %copy-start.4 = (f32[192]{0:T(256)S(1)}, f32[192]{0:T(256)}, u32[]{:S(2)}) copy-start(f32[192]{0:T(256)} %param.17) | copy-start | bytes 2308
  10.3 31.6 %collective-permute-start.1 = (bf16[8,2,4,384]{3,2,1,0:T(4,128)(2,1)S(1)}, bf16[8,2,4,384]{3,2,1,0:T(4,128)(2,1)S(1)}, u32[]{:S(2)}, u32[]{:S(2)}) collective-permute-start(bf16[8,2,4,384]{3,2,1,0:T(4,128)(2,1)S(1)} %get-tuple-element.22), channel_id=1, source_target_pairs={{0,1},{1,2},{2,3},{3,4},{4,5},{5,6},{6,7},{8,9},{9,10},{10,11},{11... | collective-permute-start | bytes 147464 | tf_op jit(solution)/shard_map/ppermute | solution.py:171
  15.0 27.0 %collective-permute-start.2 = (bf16[8,2,4,384]{3,2,1,0:T(4,128)(2,1)S(1)}, bf16[8,2,4,384]{3,2,1,0:T(4,128)(2,1)S(1)}, u32[]{:S(2)}, u32[]{:S(2)}) collective-permute-start(bf16[8,2,4,384]{3,2,1,0:T(4,128)(2,1)S(1)} %get-tuple-element.21), channel_id=1, source_target_pairs={{1,0},{2,1},{3,2},{4,3},{5,4},{6,5},{7,6},{9,8},{10,9},{11,10},{12... | collective-permute-start | bytes 147464 | tf_op jit(solution)/shard_map/ppermute | solution.py:172

commit v2 on v1

--- a/solution.py
+++ b/solution.py
@@ -7,6 +7,7 @@
 from jax.experimental.pallas import tpu as pltpu
 from jax.sharding import PartitionSpec as P
 
+
 EPS = 1e-6
 BF = jnp.bfloat16
 F32 = jnp.float32
@@ -21,51 +22,153 @@
     return jnp.dot(a, b, preferred_element_type=F32)
 
 
-def kernel(last, x, prev, above, below, gain0, wc, bias0, w4, bias1, gain1, wf, bias2, out,
-           raw, left, mid, lift, planes, nat, back):
+def phases(wu, w4, turned):
+    c1, c0 = wu.shape[2:]
+    for r in range(0, c1, 16):
+        f = [[wu[kh, kw, r:r + 16, :].astype(F32) for kw in range(3)] for kh in range(3)]
+        cols = [[(k[0], k[1] + k[2]), (k[0] + k[1], k[2])] for k in f]
+        for wcol in range(2):
+            tap = [[cols[kh][b][wcol] for b in range(2)] for kh in range(3)]
+            first = tap[0] + [tap[0][b] + tap[1][b] for b in range(2)]
+            second = [tap[1][b] + tap[2][b] for b in range(2)] + tap[2]
+            for hrow, parts in enumerate((first, second)):
+                at = (2 * wcol + hrow) * c0
+                for i, v in enumerate(parts):
+                    turned[c1 * i + r:c1 * i + r + 16, at:at + c0] = v.astype(BF)
+    for k in range(0, 4 * c0, 128):
+        w4[k:k + 128, :] = turned[:, k:k + 128].T
+
+
+def put(raw, row, v):
+    for c in range(3):
+        raw[c, row:row + v.shape[0], :] = v[:, 128 * c:128 * c + 128]
+
+
+def normed(raw, row, g0):
+    v = jnp.concatenate([raw[c, row:row + 64, :] for c in range(3)], axis=1)
+    r = lax.rsqrt(jnp.mean(v * v, axis=-1, keepdims=True) + EPS)
+    return silu(v * r * g0)
+
+
+def spread(raw, left, t):
+    for kh in range(3):
+        for w in range(4):
+            for c in range(3):
+                v = raw[c, pl.ds(64 * t + 4 * kh + w, 16, stride=4), :]
+                left[kh, 64 * t + 16 * w:64 * t + 16 * w + 16, 128 * c:128 * c + 128] = v.astype(BF)
+
+
+SPAN = ((0, 3), (0, 4), (1, 3))
+
+
+def own(x, gain0, wc, wu, w4, wv, part, turned, raw, left, sems):
+    copies = {}
+    for kt in (2, 1, 0):
+        copies[kt] = pltpu.make_async_copy(wc.at[kt], wv.at[kt], sems.at[kt])
+        copies[kt].start()
+    phases(wu, w4, turned)
+    g0 = gain0[...]
+    zero = jnp.zeros((8, x.shape[-1]), F32)
+    for t in range(4):
+        put(raw, 64 * t, zero)
+        put(raw, 64 * t + 56, zero)
+        for h in range(12):
+            put(raw, 64 * t + 8 + 4 * h, x[t, h].astype(F32))
+    put(raw, 256, zero)
+    for t in range(4):
+        put(raw, 64 * t, normed(raw, 64 * t, g0))
+    for t in range(4):
+        spread(raw, left, t)
+    for kt in (2, 1, 0):
+        copies[kt].wait()
+        n = kt + 2
+        for kw in (1, 0, 2):
+            lo, m = SPAN[kw]
+            lhs = jnp.concatenate(
+                [jnp.concatenate([left[kh, 64 * t + 16 * lo:64 * t + 16 * (lo + m), :] for t in range(n)], axis=0)
+                 for kh in range(3)], axis=1)
+            d = dot(lhs, jnp.concatenate([wv[kt, kh, kw] for kh in range(3)], axis=0))
+            for t in range(n):
+                at = 64 * (t + 2 - kt) + 16 * (lo + 1 - kw)
+                v = d[16 * m * t:16 * m * (t + 1)]
+                if kt == 2 and kw == 1:
+                    part[at:at + 16 * m, :] = v
+                else:
+                    part[at:at + 16 * m, :] += v
+
+
+def kernel(last, part, prev, outer, inner, gain0, wc, bias0, w4, bias1, gain1, wf, bias2, out,
+           raw, left, ends, tail, mid, lift, planes, nat, back):
     group = lax.axis_index("tm")
     strip = lax.axis_index("strip")
     c0 = wc.shape[-1]
     c1 = wf.shape[-1]
-    for t in range(8):
-        src, f = (prev, t) if t < 4 else (x, t - 4)
-        base = 64 * t
+    odd = strip % 2 == 1
+
+    def margin(t, h):
+        i, o = inner[t, h % 2].astype(F32), outer[t, h % 2].astype(F32)
+        return jnp.where(odd, i, o) if h < 2 else jnp.where(odd, o, i)
+
+    for t in range(4):
         for h in range(16):
-            v = above[t, h] if h < 2 else below[t, h - 14] if h > 13 else src[f, h - 2]
+            put(raw, 64 * t + 4 * h, prev[t, h - 2].astype(F32) if 1 < h < 14 else margin(t, h))
+        for i, h in enumerate((0, 1, 14, 15)):
+            put(raw, 256 + 16 * t + 4 * i, margin(4 + t, h))
+    g0 = gain0[...]
+    for t in range(4):
+        put(raw, 64 * t, normed(raw, 64 * t, g0))
+    v = normed(raw, 256, g0)
+    row = lax.broadcasted_iota(jnp.int32, (8, c0), 0)
+    none = jnp.zeros((8, c0), F32)
+    for t in range(4):
+        up, down = v[16 * t:16 * t + 8], v[16 * t + 8:16 * t + 16]
+        for kh in range(3):
+            a = (up, jnp.where(row < 4, pltpu.roll(up, 4, 0), 0.0), none)[kh]
+            b = (none, jnp.where(row < 4, 0.0, pltpu.roll(down, 4, 0)), down)[kh]
+            for kw in range(3):
+                if kw == 0:
+                    e = [jnp.where(row % 4 == 0, 0.0, pltpu.roll(z, 1, 0)) for z in (a, b)]
+                elif kw == 2:
+                    e = [jnp.where(row % 4 == 3, 0.0, pltpu.roll(z, 7, 0)) for z in (a, b)]
+                else:
+                    e = [a, b]
+                ends[kw, kh, 16 * t:16 * t + 16, :] = jnp.concatenate(e, axis=0).astype(BF)
+    for t in range(4):
+        spread(raw, left, t)
+
+    b0 = bias0[...]
+    for t in range(2):
+        mid[64 * t:64 * t + 64, :] = jnp.broadcast_to(b0, (64, c0))
+    mid[128:384, :] = part[...] + b0
+    for kt in range(3):
+        n = 4 - kt
+        for kw in range(3):
+            lo, m = SPAN[kw]
+            lhs = jnp.concatenate(
+                [jnp.concatenate(
+                    [left[kh, 64 * (u + kt) + 16 * lo:64 * (u + kt) + 16 * (lo + m), :] for u in range(n)]
+                    + [ends[kw, kh, 0:16 * (kt + 2), :]], axis=0)
+                 for kh in range(3)], axis=1)
+            d = dot(lhs, jnp.concatenate([wc[kt, kh, kw] for kh in range(3)], axis=0))
+            for u in range(n):
+                at = 64 * u + 16 * (lo + 1 - kw)
+                mid[at:at + 16 * m, :] += d[16 * m * u:16 * m * (u + 1)]
+            for i in range(kt + 2):
+                e = d[16 * (m * n + i):16 * (m * n + i + 1)]
+                at = 16 * (i + 2 - kt)
+                for c in range(3):
+                    if kt == 0 and kw == 0:
+                        tail[c, at:at + 16, :] = e[:, 128 * c:128 * c + 128]
+                    else:
+                        new = kw == 0 and i == 0
+                        old = 0.0 if new else tail[c, at:at + 16, :]
+                        tail[c, at:at + 16, :] = old + e[:, 128 * c:128 * c + 128]
+    for t in range(4):
+        for w in range(4):
             for c in range(3):
-                raw[c, base + 4 * h:base + 4 * h + 4, :] = v[:, 128 * c:128 * c + 128].astype(F32)
-    g0 = gain0[...]
-    for t in range(8):
-        v = jnp.concatenate([raw[c, 64 * t:64 * t + 64, :] for c in range(3)], axis=1)
-        r = lax.rsqrt(jnp.mean(v * v, axis=-1, keepdims=True) + EPS)
-        v = silu(v * r * g0)
-        for c in range(3):
-            raw[c, 64 * t:64 * t + 64, :] = v[:, 128 * c:128 * c + 128]
-    for kh in range(3):
-        for t in range(8):
-            for w in range(4):
-                for c in range(3):
-                    v = raw[c, pl.ds(64 * t + 4 * kh + w, 16, stride=4), :]
-                    left[kh, 64 * t + 16 * w:64 * t + 16 * w + 16, 128 * c:128 * c + 128] = v.astype(BF)
-
-    def taps(kw, lo, n):
-        cols = []
-        for kt in range(3):
-            for kh in range(3):
-                cols.append(jnp.concatenate(
-                    [left[kh, 64 * (t + kt) + 16 * lo:64 * (t + kt) + 16 * (lo + n), :] for t in range(6)], axis=0))
-        lhs = jnp.concatenate(cols, axis=1)
-        rhs = jnp.concatenate([wc[kt, kh, kw] for kt in range(3) for kh in range(3)], axis=0)
-        return dot(lhs, rhs)
-
-    b0 = bias0[...]
-    mid[0:384, :] = taps(1, 0, 4) + b0
-    p = taps(0, 0, 3)
-    for t in range(6):
-        mid[64 * t + 16:64 * t + 64, :] += p[48 * t:48 * t + 48]
-    p = taps(2, 1, 3)
-    for t in range(6):
-        mid[64 * t:64 * t + 48, :] += p[48 * t:48 * t + 48]
+                for i, r in enumerate((0, 12)):
+                    at = 64 * (t + 2) + 16 * w + r
+                    mid[at:at + 2, 128 * c:128 * c + 128] += tail[c, pl.ds(16 * t + 8 * i + w, 2, stride=4), :]
     row = lax.broadcasted_iota(jnp.int32, (16, c0), 0)
     keep = jnp.logical_and(jnp.logical_or(strip > 0, row != 0), jnp.logical_or(strip < last, row != 13))
     for t in range(6):
@@ -168,36 +271,46 @@
     axes = ("tm", "strip")
     prev = lax.ppermute(x, axes, [(at(t, s), at(t + 1, s)) for t in range(nt - 1) for s in range(ns)])
     both = jnp.concatenate([prev, x], axis=0)
-    above = lax.ppermute(both[:, 10:], axes, [(at(t, s), at(t, s + 1)) for t in range(nt) for s in range(ns - 1)])
-    below = lax.ppermute(both[:, :2], axes, [(at(t, s + 1), at(t, s)) for t in range(nt) for s in range(ns - 1)])
-    f = wu.astype(F32)
-    first, second = ((0,), (1, 2)), ((0, 1), (2,))
-    pick = (first, second)
-    rows = []
-    for wcol in range(2):
-        for hrow in range(2):
-            rows.append(jnp.concatenate(
-                [sum(f[kh, kw] for kh in pick[a][hrow] for kw in pick[b][wcol]) for a in range(2) for b in range(2)],
-                axis=1))
-    w4 = jnp.concatenate(rows, axis=0).astype(BF)
+    odd = lax.axis_index("strip") % 2 == 1
+    top, bottom = both[:, :2], both[:, 10:]
+    outer = lax.ppermute(jnp.where(odd, bottom, top), axes,
+                         [(at(t, s), at(t, s + 1 if s % 2 else s - 1)) for t in range(nt) for s in range(1, ns - 1)])
+    inner = lax.ppermute(jnp.where(odd, top, bottom), axes,
+                         [(at(t, s), at(t, s ^ 1)) for t in range(nt) for s in range(ns - ns % 2)])
     vm = pl.BlockSpec(memory_space=pltpu.VMEM)
     two = lambda v: v.reshape(1, -1)
+    w4, wv, part = pl.pallas_call(
+        own,
+        out_shape=(jax.ShapeDtypeStruct((4 * c0, 4 * c1), BF), jax.ShapeDtypeStruct(wc.shape, BF),
+                   jax.ShapeDtypeStruct((256, c0), F32)),
+        in_specs=[vm, vm, pl.BlockSpec(memory_space=pltpu.HBM), vm],
+        out_specs=(vm, vm, vm),
+        scratch_shapes=[
+            pltpu.VMEM((4 * c1, 4 * c0), BF),
+            pltpu.VMEM((3, 272, 128), F32),
+            pltpu.VMEM((3, 256, c0), BF),
+            pltpu.SemaphoreType.DMA((3,)),
+        ],
+        compiler_params=pltpu.CompilerParams(vmem_limit_bytes=26 << 20),
+    )(x, two(gain0), pltpu.with_memory_space_constraint(wc, pltpu.HBM), jnp.swapaxes(wu, 2, 3))
     return pl.pallas_call(
         functools.partial(kernel, ns - 1),
         out_shape=jax.ShapeDtypeStruct((4, 24, 8, c1), BF),
         in_specs=[vm] * 12,
         out_specs=vm,
         scratch_shapes=[
-            pltpu.VMEM((3, 528, 128), F32),
-            pltpu.VMEM((3, 512, c0), BF),
+            pltpu.VMEM((3, 336, 128), F32),
+            pltpu.VMEM((3, 384, c0), BF),
+            pltpu.VMEM((3, 3, 64, c0), BF),
+            pltpu.VMEM((3, 64, 128), F32),
             pltpu.VMEM((400, c0), F32),
             pltpu.VMEM((2, 5, 112, 2 * c1), F32),
             pltpu.VMEM((2, 2, 5, 96, 2 * c1), BF),
             pltpu.VMEM((2, 32, 2 * c1), F32),
             pltpu.VMEM((2, 768, 128), F32),
         ],
-        compiler_params=pltpu.CompilerParams(vmem_limit_bytes=40 << 20),
-    )(x, prev, above, below, two(gain0), wc, two(bias0), w4, jnp.concatenate([two(bias1)], axis=1), two(gain1), wf, two(bias2))
+        compiler_params=pltpu.CompilerParams(vmem_limit_bytes=14 << 20),
+    )(part, prev, outer, inner, two(gain0), wv, two(bias0), w4, two(bias1), two(gain1), wf, two(bias2))
 
 
 def solution(mesh):

time: 52.4 us -> 33.6 us (0.64)
  other arithmetic: 25.9 us -> 0.05 us
  waiting for transfers between devices: 3.36 us -> 7.02 us
  Pallas kernels: 10.2 us -> 13.7 us
  local copies, waits for them, and re-layouts: 2.83 us -> 4.65 us
  starting transfers between devices: 9.65 us -> 7.83 us
    concatenate x1 -> x0, other arithmetic: 25 us -> none  [block(): w4 = jnp.concatenate(rows, axis=0).astype(BF)]
    pallas_call x0 -> x1, Pallas kernels: none -> 4.54 us  [block(): pl.pallas_call(own, out_shape=(jax.ShapeDtypeStruct((4 * c0, 4 * c1), BF)...]
    ppermute x1, waiting for transfers between devices: 3.35 us -> 7.02 us  [block(): lax.ppermute(x, axes, [(at(t, s), at(t + 1, s)) for t in range(nt - 1) fo...]
    ppermute x2, starting transfers between devices: 6.54 us -> 4.72 us  [the longest x1 3.1 us: block(): lax.ppermute(jnp.where(odd, bottom, top), axes, [(at(t, s), at(t, s + 1 i...]
    reshape x2, local copies, waits for them, and re-layouts: 0.01 us -> 1.37 us  [block(): two = lambda v: v.reshape(1, -1)]
    pallas_call x1, Pallas kernels: 10.2 us -> 9.2 us  [block(): pl.pallas_call(functools.partial(kernel, ns - 1), out_shape=jax.ShapeDtyp...]
    concatenate x1, local copies, waits for them, and re-layouts: 0.07 us -> 0.98 us  [block(): both = jnp.concatenate([prev, x], axis=0)]
    another operation x2 -> x0, other arithmetic: 0.6 us -> none
  transfers between devices with their start and end apart: 3 -> 3, of which waited for: 1 -> 1; matrix products, arithmetic and copies ran while one was open for 55% -> 4% of each run, Pallas kernels for 0% -> 14%
where the time goes in v2:
time: 33.6 us; the launch traced here: 33.4 us
  Pallas kernels  13.7 us (41%)
  starting transfers between devices  7.83 us (23%)
  waiting for transfers between devices  7.02 us (21%)
  local copies, waits for them, and re-layouts  4.65 us (14%)
    pallas_call x1, Pallas kernels, block(): pl.pallas_call(functools.partial(kernel, ns - 1), out_shape=jax.ShapeDtyp...  9.2 us
    ppermute x1, waiting for transfers between devices, block(): lax.ppermute(x, axes, [(at(t, s), at(t + 1, s)) for t in range(nt - 1) fo...  7.02 us
    pallas_call x1, Pallas kernels, block(): pl.pallas_call(own, out_shape=(jax.ShapeDtypeStruct((4 * c0, 4 * c1), BF)...  4.54 us
    ppermute x1, starting transfers between devices, block(): lax.ppermute(x, axes, [(at(t, s), at(t + 1, s)) for t in range(nt - 1) fo...  3.11 us
    ppermute x1, starting transfers between devices, block(): lax.ppermute(jnp.where(odd, bottom, top), axes, [(at(t, s), at(t, s + 1 i...  3.1 us
    unnamed x13, local copies, waits for them, and re-layouts  2.3 us
    ppermute x1, starting transfers between devices, block(): lax.ppermute(jnp.where(odd, top, bottom), axes, [(at(t, s), at(t, s ^ 1))...  1.62 us
    reshape x2, local copies, waits for them, and re-layouts, block(): two = lambda v: v.reshape(1, -1)  1.37 us
  transfers between devices with their start and end apart: 3, of which 1 were waited for; matrix products, arithmetic and copies ran while one was open for 4% of the time, Pallas kernels for 14%

profile of v2, /device:TPU:137, one launch (start us, length us, event | category | flops | bytes accessed | tf_op | source)
XLA Modules:
  0.0 33.4 jit_solution(15586442063370369467)
XLA Ops:
  0.0 3.1 %collective-permute-start = (bf16[4,12,4,384]{3,2,1,0:T(4,128)(2,1)}, bf16[4,12,4,384]{3,2,1,0:T(4,128)(2,1)S(1)}, u32[]{:S(2)}, u32[]{:S(2)}) collective-permute-start(bf16[4,12,4,384]{3,2,1,0:T(4,128)(2,1)} %x.1), channel_id=1, source_target_pairs={{0,8},{1,9},{2,10},{3,11},{4,12},{5,13},{6,14},{7,15},{8,16},{9,17... | collective-permute-start | bytes 442376 | tf_op jit(solution)/shard_map/ppermute | solution.py:272
  3.1 7.0 %collective-permute-done.prev = bf16[4,12,4,384]{3,2,1,0:T(4,128)(2,1)S(1)} collective-permute-done((bf16[4,12,4,384]{3,2,1,0:T(4,128)(2,1)}, bf16[4,12,4,384]{3,2,1,0:T(4,128)(2,1)S(1)}, u32[]{:S(2)}, u32[]{:S(2)}) %collective-permute-start) | collective-permute-done | bytes 147488 | tf_op jit(solution)/shard_map/ppermute | solution.py:272
  10.1 0.1 constant_dynamic-update-slice_fusion.1
  10.2 1.0 %constant_dynamic-update-slice_fusion = bf16[8,12,4,384]{3,2,1,0:T(4,128)(2,1)S(1)} fusion(bf16[8,12,4,384]{3,2,1,0:T(4,128)(2,1)S(1)} %constant_dynamic-update-slice_fusion.1, bf16[4,12,4,384]{3,2,1,0:T(4,128)(2,1)} %x.1), kind=kLoop, calls=%fused_computation.2 | loop fusion | bytes 294912 | tf_op jit(solution)/shard_map/concatenate | solution.py:273
  11.2 1.6 %collective-permute-start.2 = (bf16[8,2,4,384]{3,2,1,0:T(4,128)(2,1)S(1)}, bf16[8,2,4,384]{3,2,1,0:T(4,128)(2,1)S(1)}, u32[]{:S(2)}, u32[]{:S(2)}) collective-permute-start(bf16[8,2,4,384]{3,2,1,0:T(4,128)(2,1)S(1)} %get-tuple-element.11), channel_id=1, source_target_pairs={{0,1},{1,0},{2,3},{3,2},{4,5},{5,4},{6,7},{7,6},{8,9},{9,8},{10,11... | collective-permute-start | bytes 147464 | tf_op jit(solution)/shard_map/ppermute | solution.py:278
  12.9 3.1 %collective-permute-start.1 = (bf16[8,2,4,384]{3,2,1,0:T(4,128)(2,1)S(1)}, bf16[8,2,4,384]{3,2,1,0:T(4,128)(2,1)S(1)}, u32[]{:S(2)}, u32[]{:S(2)}) collective-permute-start(bf16[8,2,4,384]{3,2,1,0:T(4,128)(2,1)S(1)} %get-tuple-element.12), channel_id=1, source_target_pairs={{1,2},{2,1},{3,4},{4,3},{5,6},{6,5},{9,10},{10,9},{11,12},{12,11},... | collective-permute-start | bytes 147464 | tf_op jit(solution)/shard_map/ppermute | solution.py:276
  16.0 0.7 %reshape.16.gain0 = f32[1,384]{1,0:T(1,128)S(1)} reshape(f32[384]{0:T(512)} %param.10) | data formatting | bytes 3072 | tf_op jit(solution)/shard_map/reshape | solution.py:281
  16.7 0.7 %reshape.17.bias0 = f32[1,384]{1,0:T(1,128)S(1)} reshape(f32[384]{0:T(512)} %param.12) | data formatting | bytes 3072 | tf_op jit(solution)/shard_map/reshape | solution.py:281
  17.3 0.0 copy-start.1
  17.3 1.3 %copy-done.1 = bf16[3,3,384,192]{2,3,1,0:T(8,128)(2,1)S(1)} copy-done((bf16[3,3,384,192]{2,3,1,0:T(8,128)(2,1)S(1)}, bf16[3,3,384,192]{2,3,1,0:T(8,128)(2,1)}, u32[]{:S(2)}) %copy-start.1) | copy-done | bytes 1327128
  18.7 0.0 copy-start.2
  18.7 0.9 %copy-done.2 = bf16[4,12,4,384]{3,2,1,0:T(4,128)(2,1)S(1)} copy-done((bf16[4,12,4,384]{3,2,1,0:T(4,128)(2,1)S(1)}, bf16[4,12,4,384]{3,2,1,0:T(4,128)(2,1)}, u32[]{:S(2)}) %copy-start.2) | copy-done | bytes 147480
  19.6 0.0 copy-start
  19.6 0.0 copy-start.3
  19.6 0.0 copy-start.4
  19.6 0.0 copy-start.5
  19.6 4.5 %shard_map.91 = (bf16[1536,768]{1,0:T(8,128)(2,1)S(1)}, bf16[3,3,3,384,384]{4,3,2,1,0:T(8,128)(2,1)S(1)}, f32[256,384]{1,0:T(8,128)S(1)}) custom-call(bf16[4,12,4,384]{3,2,1,0:T(4,128)(2,1)S(1)} %copy-done.2, f32[1,384]{1,0:T(1,128)S(1)} %reshape.16.gain0, bf16[3,3,3,384,384]{4,3,2,1,0:T(8,128)(2,1)} %wc.1, bf16[3,3,192,384]{3,2,1,0:T(8,128)(2,1)S(1)} %bitcast.4), custom_call_target="tpu_custom_call" | custom-call | tf_op jit(solution)/shard_map/pallas_call | solution.py:282
  24.1 0.0 collective-permute-done.2.inner
  24.1 0.0 collective-permute-done.1.outer
  24.1 0.0 copy-done
  24.2 0.0 copy-done.3
  24.2 0.0 copy-done.4
  24.2 0.0 copy-done.5
  24.2 9.2 %shard_map.92 = bf16[4,24,8,192]{3,2,1,0:T(8,128)(2,1)} custom-call(f32[256,384]{1,0:T(8,128)S(1)} %get-tuple-element.8.part, bf16[4,12,4,384]{3,2,1,0:T(4,128)(2,1)S(1)} %collective-permute-done.prev, bf16[8,2,4,384]{3,2,1,0:T(4,128)(2,1)S(1)} %collective-permute-done.1.outer, bf16[8,2,4,384]{3,2,1,0:T(4,128)(2,1)S(1)} %collective-permute-done.2.inner, ...), custom_call_target="tpu_custom_call" | custom-call | tf_op jit(solution)/shard_map/pallas_call | solution.py:296
  (1 shorter events, 0.0 us)
Async XLA Ops:
  0.0 10.1 %collective-permute-start = (bf16[4,12,4,384]{3,2,1,0:T(4,128)(2,1)}, bf16[4,12,4,384]{3,2,1,0:T(4,128)(2,1)S(1)}, u32[]{:S(2)}, u32[]{:S(2)}) collective-permute-start(bf16[4,12,4,384]{3,2,1,0:T(4,128)(2,1)} %x.1), channel_id=1, source_target_pairs={{0,8},{1,9},{2,10},{3,11},{4,12},{5,13},{6,14},{7,15},{8,16},{9,17... | collective-permute-start | bytes 442376 | tf_op jit(solution)/shard_map/ppermute | solution.py:272
  11.2 12.9 %collective-permute-start.2 = (bf16[8,2,4,384]{3,2,1,0:T(4,128)(2,1)S(1)}, bf16[8,2,4,384]{3,2,1,0:T(4,128)(2,1)S(1)}, u32[]{:S(2)}, u32[]{:S(2)}) collective-permute-start(bf16[8,2,4,384]{3,2,1,0:T(4,128)(2,1)S(1)} %get-tuple-element.11), channel_id=1, source_target_pairs={{0,1},{1,0},{2,3},{3,2},{4,5},{5,4},{6,7},{7,6},{8,9},{9,8},{10,11... | collective-permute-start | bytes 147464 | tf_op jit(solution)/shard_map/ppermute | solution.py:278
  12.9 11.3 %collective-permute-start.1 = (bf16[8,2,4,384]{3,2,1,0:T(4,128)(2,1)S(1)}, bf16[8,2,4,384]{3,2,1,0:T(4,128)(2,1)S(1)}, u32[]{:S(2)}, u32[]{:S(2)}) collective-permute-start(bf16[8,2,4,384]{3,2,1,0:T(4,128)(2,1)S(1)} %get-tuple-element.12), channel_id=1, source_target_pairs={{1,2},{2,1},{3,4},{4,3},{5,6},{6,5},{9,10},{10,9},{11,12},{12,11},... | collective-permute-start | bytes 147464 | tf_op jit(solution)/shard_map/ppermute | solution.py:276
  17.3 1.3 %copy-start.1 = (bf16[3,3,384,192]{2,3,1,0:T(8,128)(2,1)S(1)}, bf16[3,3,384,192]{2,3,1,0:T(8,128)(2,1)}, u32[]{:S(2)}) copy-start(bf16[3,3,384,192]{2,3,1,0:T(8,128)(2,1)} %param.13) | copy-start | bytes 3981316
  18.7 0.9 %copy-start.2 = (bf16[4,12,4,384]{3,2,1,0:T(4,128)(2,1)S(1)}, bf16[4,12,4,384]{3,2,1,0:T(4,128)(2,1)}, u32[]{:S(2)}) copy-start(bf16[4,12,4,384]{3,2,1,0:T(4,128)(2,1)} %x.1) | copy-start | bytes 442372
  19.6 4.6 %copy-start = (bf16[3,3,3,192,192]{4,3,2,1,0:T(8,128)(2,1)S(1)}, bf16[3,3,3,192,192]{4,3,2,1,0:T(8,128)(2,1)}, u32[]{:S(2)}) copy-start(bf16[3,3,3,192,192]{4,3,2,1,0:T(8,128)(2,1)} %wf.1) | copy-start | bytes 5971972
  19.6 4.6 %copy-start.3 = (f32[192]{0:T(256)S(1)}, f32[192]{0:T(256)}, u32[]{:S(2)}) copy-start(f32[192]{0:T(256)} %param.14) | copy-start | bytes 2308
  19.6 4.6 %copy-start.4 = (f32[192]{0:T(256)S(1)}, f32[192]{0:T(256)}, u32[]{:S(2)}) copy-start(f32[192]{0:T(256)} %param.15) | copy-start | bytes 2308
  19.6 4.6 %copy-start.5 = (f32[192]{0:T(256)S(1)}, f32[192]{0:T(256)}, u32[]{:S(2)}) copy-start(f32[192]{0:T(256)} %param.17) | copy-start | bytes 2308

commit v3 on v2

--- a/solution.py
+++ b/solution.py
@@ -61,33 +61,51 @@
 SPAN = ((0, 3), (0, 4), (1, 3))
 
 
-def own(x, gain0, wc, wu, w4, wv, part, turned, raw, left, sems):
+def blank(raw, n):
+    zero = jnp.zeros((8, 3 * raw.shape[-1]), F32)
+    for t in range(n):
+        put(raw, 64 * t, zero)
+        put(raw, 64 * t + 56, zero)
+    put(raw, 64 * n, zero)
+
+
+def gather(left, lo, m, first, n):
+    return jnp.concatenate(
+        [jnp.concatenate([left[kh, 64 * t + 16 * lo:64 * t + 16 * (lo + m), :] for t in range(first, first + n)], axis=0)
+         for kh in range(3)], axis=1)
+
+
+def stack(wc, kt, kw):
+    return jnp.concatenate([wc[kt, kh, kw] for kh in range(3)], axis=0)
+
+
+def own(x_hbm, gain0, wc, wu_hbm, w4, wv, part, x, wu, turned, raw, left, sems):
+    c0 = x.shape[-1]
+    get_x = pltpu.make_async_copy(x_hbm, x, sems.at[3])
+    get_x.start()
+    get_u = pltpu.make_async_copy(wu_hbm, wu, sems.at[4])
+    get_u.start()
     copies = {}
     for kt in (2, 1, 0):
         copies[kt] = pltpu.make_async_copy(wc.at[kt], wv.at[kt], sems.at[kt])
         copies[kt].start()
-    phases(wu, w4, turned)
-    g0 = gain0[...]
-    zero = jnp.zeros((8, x.shape[-1]), F32)
-    for t in range(4):
-        put(raw, 64 * t, zero)
-        put(raw, 64 * t + 56, zero)
+    g0 = gain0[...].reshape(1, c0)
+    blank(raw, 4)
+    get_x.wait()
+    for t in range(4):
         for h in range(12):
             put(raw, 64 * t + 8 + 4 * h, x[t, h].astype(F32))
-    put(raw, 256, zero)
-    for t in range(4):
         put(raw, 64 * t, normed(raw, 64 * t, g0))
     for t in range(4):
         spread(raw, left, t)
+    get_u.wait()
+    phases(wu, w4, turned)
     for kt in (2, 1, 0):
         copies[kt].wait()
         n = kt + 2
         for kw in (1, 0, 2):
             lo, m = SPAN[kw]
-            lhs = jnp.concatenate(
-                [jnp.concatenate([left[kh, 64 * t + 16 * lo:64 * t + 16 * (lo + m), :] for t in range(n)], axis=0)
-                 for kh in range(3)], axis=1)
-            d = dot(lhs, jnp.concatenate([wv[kt, kh, kw] for kh in range(3)], axis=0))
+            d = dot(gather(left, lo, m, 0, n), stack(wv, kt, kw))
             for t in range(n):
                 at = 64 * (t + 2 - kt) + 16 * (lo + 1 - kw)
                 v = d[16 * m * t:16 * m * (t + 1)]
@@ -97,7 +115,30 @@
                     part[at:at + 16 * m, :] += v
 
 
-def kernel(last, part, prev, outer, inner, gain0, wc, bias0, w4, bias1, gain1, wf, bias2, out,
+def old(part, prev, gain0, wc, bias0, mid, raw, left):
+    c0 = prev.shape[-1]
+    g0 = gain0[...].reshape(1, c0)
+    b0 = bias0[...].reshape(1, c0)
+    blank(raw, 4)
+    for t in range(4):
+        for h in range(12):
+            put(raw, 64 * t + 8 + 4 * h, prev[t, h].astype(F32))
+        put(raw, 64 * t, normed(raw, 64 * t, g0))
+    for t in range(4):
+        spread(raw, left, t)
+    mid[0:128, :] = jnp.broadcast_to(b0, (128, c0))
+    mid[128:384, :] = part[...] + b0
+    for kt in range(3):
+        n = 4 - kt
+        for kw in range(3):
+            lo, m = SPAN[kw]
+            d = dot(gather(left, lo, m, kt, n), stack(wc, kt, kw))
+            for u in range(n):
+                at = 64 * u + 16 * (lo + 1 - kw)
+                mid[at:at + 16 * m, :] += d[16 * m * u:16 * m * (u + 1)]
+
+
+def kernel(last, sums, inner, outer, gain0, wc, w4, bias1, gain1, wf, bias2, out,
            raw, left, ends, tail, mid, lift, planes, nat, back):
     group = lax.axis_index("tm")
     strip = lax.axis_index("strip")
@@ -105,69 +146,41 @@
     c1 = wf.shape[-1]
     odd = strip % 2 == 1
 
-    def margin(t, h):
-        i, o = inner[t, h % 2].astype(F32), outer[t, h % 2].astype(F32)
-        return jnp.where(odd, i, o) if h < 2 else jnp.where(odd, o, i)
-
-    for t in range(4):
-        for h in range(16):
-            put(raw, 64 * t + 4 * h, prev[t, h - 2].astype(F32) if 1 < h < 14 else margin(t, h))
-        for i, h in enumerate((0, 1, 14, 15)):
-            put(raw, 256 + 16 * t + 4 * i, margin(4 + t, h))
-    g0 = gain0[...]
-    for t in range(4):
-        put(raw, 64 * t, normed(raw, 64 * t, g0))
-    v = normed(raw, 256, g0)
+    for t in range(8):
+        for i in range(2):
+            a, b = inner[t, i].astype(F32), outer[t, i].astype(F32)
+            put(raw, 16 * t + 4 * i, jnp.where(odd, a, b))
+            put(raw, 16 * t + 8 + 4 * i, jnp.where(odd, b, a))
+    g0 = gain0[...].reshape(1, c0)
     row = lax.broadcasted_iota(jnp.int32, (8, c0), 0)
     none = jnp.zeros((8, c0), F32)
-    for t in range(4):
-        up, down = v[16 * t:16 * t + 8], v[16 * t + 8:16 * t + 16]
-        for kh in range(3):
-            a = (up, jnp.where(row < 4, pltpu.roll(up, 4, 0), 0.0), none)[kh]
-            b = (none, jnp.where(row < 4, 0.0, pltpu.roll(down, 4, 0)), down)[kh]
-            for kw in range(3):
-                if kw == 0:
-                    e = [jnp.where(row % 4 == 0, 0.0, pltpu.roll(z, 1, 0)) for z in (a, b)]
-                elif kw == 2:
-                    e = [jnp.where(row % 4 == 3, 0.0, pltpu.roll(z, 7, 0)) for z in (a, b)]
-                else:
-                    e = [a, b]
-                ends[kw, kh, 16 * t:16 * t + 16, :] = jnp.concatenate(e, axis=0).astype(BF)
-    for t in range(4):
-        spread(raw, left, t)
-
-    b0 = bias0[...]
-    for t in range(2):
-        mid[64 * t:64 * t + 64, :] = jnp.broadcast_to(b0, (64, c0))
-    mid[128:384, :] = part[...] + b0
-    for kt in range(3):
-        n = 4 - kt
-        for kw in range(3):
-            lo, m = SPAN[kw]
-            lhs = jnp.concatenate(
-                [jnp.concatenate(
-                    [left[kh, 64 * (u + kt) + 16 * lo:64 * (u + kt) + 16 * (lo + m), :] for u in range(n)]
-                    + [ends[kw, kh, 0:16 * (kt + 2), :]], axis=0)
-                 for kh in range(3)], axis=1)
-            d = dot(lhs, jnp.concatenate([wc[kt, kh, kw] for kh in range(3)], axis=0))
-            for u in range(n):
-                at = 64 * u + 16 * (lo + 1 - kw)
-                mid[at:at + 16 * m, :] += d[16 * m * u:16 * m * (u + 1)]
-            for i in range(kt + 2):
-                e = d[16 * (m * n + i):16 * (m * n + i + 1)]
-                at = 16 * (i + 2 - kt)
-                for c in range(3):
-                    if kt == 0 and kw == 0:
-                        tail[c, at:at + 16, :] = e[:, 128 * c:128 * c + 128]
+    for half in range(2):
+        v = normed(raw, 64 * half, g0)
+        for i in range(4):
+            t = 4 * half + i
+            up, down = v[16 * i:16 * i + 8], v[16 * i + 8:16 * i + 16]
+            for kh in range(3):
+                a = (up, jnp.where(row < 4, pltpu.roll(up, 4, 0), 0.0), none)[kh]
+                b = (none, jnp.where(row < 4, 0.0, pltpu.roll(down, 4, 0)), down)[kh]
+                for kw in range(3):
+                    if kw == 0:
+                        e = [jnp.where(row % 4 == 0, 0.0, pltpu.roll(z, 1, 0)) for z in (a, b)]
+                    elif kw == 2:
+                        e = [jnp.where(row % 4 == 3, 0.0, pltpu.roll(z, 7, 0)) for z in (a, b)]
                     else:
-                        new = kw == 0 and i == 0
-                        old = 0.0 if new else tail[c, at:at + 16, :]
-                        tail[c, at:at + 16, :] = old + e[:, 128 * c:128 * c + 128]
-    for t in range(4):
+                        e = [a, b]
+                    ends[kw, kh, 16 * t:16 * t + 16, :] = jnp.concatenate(e, axis=0).astype(BF)
+    every = [(kt, kw, kh) for kt in range(3) for kw in range(3) for kh in range(3)]
+    d = dot(jnp.concatenate([ends[kw, kh, 16 * kt:16 * kt + 96, :] for kt, kw, kh in every], axis=1),
+            jnp.concatenate([wc[kt, kh, kw] for kt, kw, kh in every], axis=0))
+    for c in range(3):
+        tail[c] = d[:, 128 * c:128 * c + 128]
+    mid[0:384, :] = sums[...]
+    for t in range(6):
         for w in range(4):
             for c in range(3):
                 for i, r in enumerate((0, 12)):
-                    at = 64 * (t + 2) + 16 * w + r
+                    at = 64 * t + 16 * w + r
                     mid[at:at + 2, 128 * c:128 * c + 128] += tail[c, pl.ds(16 * t + 8 * i + w, 2, stride=4), :]
     row = lax.broadcasted_iota(jnp.int32, (16, c0), 0)
     keep = jnp.logical_and(jnp.logical_or(strip > 0, row != 0), jnp.logical_or(strip < last, row != 13))
@@ -268,41 +281,53 @@
 def block(x, gain0, wc, bias0, wu, bias1, gain1, wf, bias2, *, nt, ns):
     c0, c1 = wc.shape[-1], wf.shape[-1]
     at = lambda t, s: t * ns + s
+    vm = pl.BlockSpec(memory_space=pltpu.VMEM)
+    hbm = pl.BlockSpec(memory_space=pltpu.HBM)
+    far = lambda v: pltpu.with_memory_space_constraint(v, pltpu.HBM)
+    two = lambda v: v.reshape(1, -1)
     axes = ("tm", "strip")
     prev = lax.ppermute(x, axes, [(at(t, s), at(t + 1, s)) for t in range(nt - 1) for s in range(ns)])
-    both = jnp.concatenate([prev, x], axis=0)
-    odd = lax.axis_index("strip") % 2 == 1
-    top, bottom = both[:, :2], both[:, 10:]
-    outer = lax.ppermute(jnp.where(odd, bottom, top), axes,
-                         [(at(t, s), at(t, s + 1 if s % 2 else s - 1)) for t in range(nt) for s in range(1, ns - 1)])
-    inner = lax.ppermute(jnp.where(odd, top, bottom), axes,
-                         [(at(t, s), at(t, s ^ 1)) for t in range(nt) for s in range(ns - ns % 2)])
-    vm = pl.BlockSpec(memory_space=pltpu.VMEM)
-    two = lambda v: v.reshape(1, -1)
     w4, wv, part = pl.pallas_call(
         own,
         out_shape=(jax.ShapeDtypeStruct((4 * c0, 4 * c1), BF), jax.ShapeDtypeStruct(wc.shape, BF),
                    jax.ShapeDtypeStruct((256, c0), F32)),
-        in_specs=[vm, vm, pl.BlockSpec(memory_space=pltpu.HBM), vm],
+        in_specs=[hbm, vm, hbm, hbm],
         out_specs=(vm, vm, vm),
         scratch_shapes=[
+            pltpu.VMEM(x.shape, BF),
+            pltpu.VMEM((3, 3, c1, c0), BF),
             pltpu.VMEM((4 * c1, 4 * c0), BF),
             pltpu.VMEM((3, 272, 128), F32),
             pltpu.VMEM((3, 256, c0), BF),
-            pltpu.SemaphoreType.DMA((3,)),
+            pltpu.SemaphoreType.DMA((5,)),
         ],
         compiler_params=pltpu.CompilerParams(vmem_limit_bytes=26 << 20),
-    )(x, two(gain0), pltpu.with_memory_space_constraint(wc, pltpu.HBM), jnp.swapaxes(wu, 2, 3))
+    )(far(x), gain0, far(wc), far(jnp.swapaxes(wu, 2, 3)))
+    both = jnp.concatenate([prev, x], axis=0)
+    odd = lax.axis_index("strip") % 2 == 1
+    top, bottom = both[:, :2], both[:, 10:]
+    inner = lax.ppermute(jnp.where(odd, top, bottom), axes,
+                         [(at(t, s), at(t, s ^ 1)) for t in range(nt) for s in range(ns)])
+    outer = lax.ppermute(jnp.where(odd, bottom, top), axes,
+                         [(at(t, s), at(t, s + 1 if s % 2 else s - 1)) for t in range(nt) for s in range(1, ns - 1)])
+    sums = pl.pallas_call(
+        old,
+        out_shape=jax.ShapeDtypeStruct((384, c0), F32),
+        in_specs=[vm] * 5,
+        out_specs=vm,
+        scratch_shapes=[pltpu.VMEM((3, 272, 128), F32), pltpu.VMEM((3, 256, c0), BF)],
+        compiler_params=pltpu.CompilerParams(vmem_limit_bytes=14 << 20),
+    )(part, prev, gain0, wv, bias0)
     return pl.pallas_call(
         functools.partial(kernel, ns - 1),
         out_shape=jax.ShapeDtypeStruct((4, 24, 8, c1), BF),
-        in_specs=[vm] * 12,
+        in_specs=[vm] * 10,
         out_specs=vm,
         scratch_shapes=[
-            pltpu.VMEM((3, 336, 128), F32),
-            pltpu.VMEM((3, 384, c0), BF),
-            pltpu.VMEM((3, 3, 64, c0), BF),
-            pltpu.VMEM((3, 64, 128), F32),
+            pltpu.VMEM((3, 128, 128), F32),
+            pltpu.VMEM((2, 384, c0), BF),
+            pltpu.VMEM((3, 3, 128, c0), BF),
+            pltpu.VMEM((3, 96, 128), F32),
             pltpu.VMEM((400, c0), F32),
             pltpu.VMEM((2, 5, 112, 2 * c1), F32),
             pltpu.VMEM((2, 2, 5, 96, 2 * c1), BF),
@@ -310,7 +335,7 @@
             pltpu.VMEM((2, 768, 128), F32),
         ],
         compiler_params=pltpu.CompilerParams(vmem_limit_bytes=14 << 20),
-    )(part, prev, outer, inner, two(gain0), wv, two(bias0), w4, two(bias1), two(gain1), wf, two(bias2))
+    )(sums, inner, outer, gain0, wv, w4, two(bias1), two(gain1), wf, two(bias2))
 
 
 def solution(mesh):

time: 33.6 us -> 32.2 us (0.958)
  local copies, waits for them, and re-layouts: 4.65 us -> 1.74 us
  Pallas kernels: 13.7 us -> 15.2 us
    pallas_call x0 -> x1, Pallas kernels: none -> 2.36 us  [block(): pl.pallas_call(old, out_shape=jax.ShapeDtypeStruct((384, c0), F32), in_sp...]
    unnamed x13, local copies, waits for them, and re-layouts: 2.3 us -> 0.76 us
    reshape x2 -> x0, local copies, waits for them, and re-layouts: 1.37 us -> none  [block(): two = lambda v: v.reshape(1, -1)]
    pallas_call x1, Pallas kernels: 9.2 us -> 8.04 us  [block(): pl.pallas_call(functools.partial(kernel, ns - 1), out_shape=jax.ShapeDtyp...]
  transfers between devices with their start and end apart: 3 -> 3, of which waited for: 1 -> 1; matrix products, arithmetic and copies ran while one was open for 4% -> 0% of each run, Pallas kernels for 14% -> 22%
where the time goes in v3:
time: 32.2 us; the launch traced here: 32 us
  Pallas kernels  15.2 us (47%)
  starting transfers between devices  7.83 us (24%)
  waiting for transfers between devices  7.02 us (22%)
  local copies, waits for them, and re-layouts  1.74 us (5%)
    pallas_call x1, Pallas kernels, block(): pl.pallas_call(functools.partial(kernel, ns - 1), out_shape=jax.ShapeDtyp...  8.04 us
    ppermute x1, waiting for transfers between devices, block(): lax.ppermute(x, axes, [(at(t, s), at(t + 1, s)) for t in range(nt - 1) fo...  7.02 us
    pallas_call x1, Pallas kernels, block(): pl.pallas_call(own, out_shape=(jax.ShapeDtypeStruct((4 * c0, 4 * c1), BF)...  4.84 us
    ppermute x1, starting transfers between devices, block(): lax.ppermute(x, axes, [(at(t, s), at(t + 1, s)) for t in range(nt - 1) fo...  3.11 us
    ppermute x1, starting transfers between devices, block(): lax.ppermute(jnp.where(odd, bottom, top), axes, [(at(t, s), at(t, s + 1 i...  3.1 us
    pallas_call x1, Pallas kernels, block(): pl.pallas_call(old, out_shape=jax.ShapeDtypeStruct((384, c0), F32), in_sp...  2.36 us
    ppermute x1, starting transfers between devices, block(): lax.ppermute(jnp.where(odd, top, bottom), axes, [(at(t, s), at(t, s ^ 1))...  1.62 us
    concatenate x1, local copies, waits for them, and re-layouts, block(): both = jnp.concatenate([prev, x], axis=0)  0.98 us
  transfers between devices with their start and end apart: 3, of which 1 were waited for; matrix products, arithmetic and copies ran while one was open for 0% of the time, Pallas kernels for 22%

profile of v3, /device:TPU:137, one launch (start us, length us, event | category | flops | bytes accessed | tf_op | source)
XLA Modules:
  0.0 32.0 jit_solution(4845648603472548760)
XLA Ops:
  0.0 3.1 %collective-permute-start = (bf16[4,12,4,384]{3,2,1,0:T(4,128)(2,1)}, bf16[4,12,4,384]{3,2,1,0:T(4,128)(2,1)S(1)}, u32[]{:S(2)}, u32[]{:S(2)}) collective-permute-start(bf16[4,12,4,384]{3,2,1,0:T(4,128)(2,1)} %x_hbm.1), channel_id=1, source_target_pairs={{0,8},{1,9},{2,10},{3,11},{4,12},{5,13},{6,14},{7,15},{8,16},{9,17... | collective-permute-start | bytes 442376 | tf_op jit(solution)/shard_map/ppermute | solution.py:289
  3.1 7.0 %collective-permute-done.prev = bf16[4,12,4,384]{3,2,1,0:T(4,128)(2,1)S(1)} collective-permute-done((bf16[4,12,4,384]{3,2,1,0:T(4,128)(2,1)}, bf16[4,12,4,384]{3,2,1,0:T(4,128)(2,1)S(1)}, u32[]{:S(2)}, u32[]{:S(2)}) %collective-permute-start) | collective-permute-done | bytes 147488 | tf_op jit(solution)/shard_map/ppermute | solution.py:289
  10.1 0.1 constant_dynamic-update-slice_fusion.1
  10.2 1.0 %constant_dynamic-update-slice_fusion = bf16[8,12,4,384]{3,2,1,0:T(4,128)(2,1)S(1)} fusion(bf16[8,12,4,384]{3,2,1,0:T(4,128)(2,1)S(1)} %constant_dynamic-update-slice_fusion.1, bf16[4,12,4,384]{3,2,1,0:T(4,128)(2,1)} %x_hbm.1), kind=kLoop, calls=%fused_computation.2 | loop fusion | bytes 294912 | tf_op jit(solution)/shard_map/concatenate | solution.py:306
  11.2 1.6 %collective-permute-start.1 = (bf16[8,2,4,384]{3,2,1,0:T(4,128)(2,1)S(1)}, bf16[8,2,4,384]{3,2,1,0:T(4,128)(2,1)S(1)}, u32[]{:S(2)}, u32[]{:S(2)}) collective-permute-start(bf16[8,2,4,384]{3,2,1,0:T(4,128)(2,1)S(1)} %get-tuple-element.12), channel_id=1, source_target_pairs={{0,1},{1,0},{2,3},{3,2},{4,5},{5,4},{6,7},{7,6},{8,9},{9,8},{10,11... | collective-permute-start | bytes 147464 | tf_op jit(solution)/shard_map/ppermute | solution.py:309
  12.9 3.1 %collective-permute-start.2 = (bf16[8,2,4,384]{3,2,1,0:T(4,128)(2,1)S(1)}, bf16[8,2,4,384]{3,2,1,0:T(4,128)(2,1)S(1)}, u32[]{:S(2)}, u32[]{:S(2)}) collective-permute-start(bf16[8,2,4,384]{3,2,1,0:T(4,128)(2,1)S(1)} %get-tuple-element.11), channel_id=1, source_target_pairs={{1,2},{2,1},{3,4},{4,3},{5,6},{6,5},{9,10},{10,9},{11,12},{12,11},... | collective-permute-start | bytes 147464 | tf_op jit(solution)/shard_map/ppermute | solution.py:311
  16.0 0.0 copy-start.1
  16.0 0.7 %copy-done.1 = f32[384]{0:T(512)S(1)} copy-done((f32[384]{0:T(512)S(1)}, f32[384]{0:T(512)}, u32[]{:S(2)}) %copy-start.1) | copy-done | bytes 1560
  16.7 0.0 copy-start.2
  16.7 4.8 %shard_map.91 = (bf16[1536,768]{1,0:T(8,128)(2,1)S(1)}, bf16[3,3,3,384,384]{4,3,2,1,0:T(8,128)(2,1)S(1)}, f32[256,384]{1,0:T(8,128)S(1)}) custom-call(bf16[4,12,4,384]{3,2,1,0:T(4,128)(2,1)} %x_hbm.1, f32[384]{0:T(512)S(1)} %copy-done.1, bf16[3,3,3,384,384]{4,3,2,1,0:T(8,128)(2,1)} %wc.1, bf16[3,3,192,384]{3,2,1,0:T(8,128)(2,1)} %bitcast.7), custom_call_target="tpu_custom_call" | custom-call | tf_op jit(solution)/shard_map/pallas_call | solution.py:290
  21.5 0.0 copy-done.2
  21.5 0.0 copy-start
  21.5 0.0 copy-start.3
  21.5 0.0 copy-start.4
  21.5 0.0 copy-start.5
  21.6 2.4 %shard_map.92.sums = f32[384,384]{1,0:T(8,128)S(1)} custom-call(f32[256,384]{1,0:T(8,128)S(1)} %get-tuple-element.8.part, bf16[4,12,4,384]{3,2,1,0:T(4,128)(2,1)S(1)} %collective-permute-done.prev, f32[384]{0:T(512)S(1)} %copy-done.1, bf16[3,3,3,384,384]{4,3,2,1,0:T(8,128)(2,1)S(1)} %get-tuple-element.9.wc, f32[384]{0:T(512)S(1)} %copy-done.2), custom_call_target="tpu_custom_call" | custom-call | tf_op jit(solution)/shard_map/pallas_call | solution.py:313
  23.9 0.0 collective-permute-done.1.inner
  23.9 0.0 collective-permute-done.2.outer
  23.9 0.0 copy-done
  24.0 0.0 copy-done.3
  24.0 0.0 copy-done.4
  24.0 0.0 copy-done.5
  24.0 8.0 %shard_map.93 = bf16[4,24,8,192]{3,2,1,0:T(8,128)(2,1)} custom-call(f32[384,384]{1,0:T(8,128)S(1)} %shard_map.92.sums, bf16[8,2,4,384]{3,2,1,0:T(4,128)(2,1)S(1)} %collective-permute-done.1.inner, bf16[8,2,4,384]{3,2,1,0:T(4,128)(2,1)S(1)} %collective-permute-done.2.outer, f32[384]{0:T(512)S(1)} %copy-done.1, ...), custom_call_target="tpu_custom_call" | custom-call | tf_op jit(solution)/shard_map/pallas_call | solution.py:321
  (1 shorter events, 0.0 us)
Async XLA Ops:
  0.0 10.1 %collective-permute-start = (bf16[4,12,4,384]{3,2,1,0:T(4,128)(2,1)}, bf16[4,12,4,384]{3,2,1,0:T(4,128)(2,1)S(1)}, u32[]{:S(2)}, u32[]{:S(2)}) collective-permute-start(bf16[4,12,4,384]{3,2,1,0:T(4,128)(2,1)} %x_hbm.1), channel_id=1, source_target_pairs={{0,8},{1,9},{2,10},{3,11},{4,12},{5,13},{6,14},{7,15},{8,16},{9,17... | collective-permute-start | bytes 442376 | tf_op jit(solution)/shard_map/ppermute | solution.py:289
  11.2 12.7 %collective-permute-start.1 = (bf16[8,2,4,384]{3,2,1,0:T(4,128)(2,1)S(1)}, bf16[8,2,4,384]{3,2,1,0:T(4,128)(2,1)S(1)}, u32[]{:S(2)}, u32[]{:S(2)}) collective-permute-start(bf16[8,2,4,384]{3,2,1,0:T(4,128)(2,1)S(1)} %get-tuple-element.12), channel_id=1, source_target_pairs={{0,1},{1,0},{2,3},{3,2},{4,5},{5,4},{6,7},{7,6},{8,9},{9,8},{10,11... | collective-permute-start | bytes 147464 | tf_op jit(solution)/shard_map/ppermute | solution.py:309
  12.9 11.1 %collective-permute-start.2 = (bf16[8,2,4,384]{3,2,1,0:T(4,128)(2,1)S(1)}, bf16[8,2,4,384]{3,2,1,0:T(4,128)(2,1)S(1)}, u32[]{:S(2)}, u32[]{:S(2)}) collective-permute-start(bf16[8,2,4,384]{3,2,1,0:T(4,128)(2,1)S(1)} %get-tuple-element.11), channel_id=1, source_target_pairs={{1,2},{2,1},{3,4},{4,3},{5,6},{6,5},{9,10},{10,9},{11,12},{12,11},... | collective-permute-start | bytes 147464 | tf_op jit(solution)/shard_map/ppermute | solution.py:311
  16.0 0.7 %copy-start.1 = (f32[384]{0:T(512)S(1)}, f32[384]{0:T(512)}, u32[]{:S(2)}) copy-start(f32[384]{0:T(512)} %gain0.5) | copy-start | bytes 4612
  16.7 4.8 %copy-start.2 = (f32[384]{0:T(512)S(1)}, f32[384]{0:T(512)}, u32[]{:S(2)}) copy-start(f32[384]{0:T(512)} %bias0.1) | copy-start | bytes 4612
  21.5 2.4 %copy-start = (bf16[3,3,3,192,192]{4,3,2,1,0:T(8,128)(2,1)S(1)}, bf16[3,3,3,192,192]{4,3,2,1,0:T(8,128)(2,1)}, u32[]{:S(2)}) copy-start(bf16[3,3,3,192,192]{4,3,2,1,0:T(8,128)(2,1)} %wf.1) | copy-start | bytes 5971972
  21.5 2.4 %copy-start.3 = (f32[192]{0:T(256)S(1)}, f32[192]{0:T(256)}, u32[]{:S(2)}) copy-start(f32[192]{0:T(256)} %param.14) | copy-start | bytes 2308
  21.5 2.4 %copy-start.4 = (f32[192]{0:T(256)S(1)}, f32[192]{0:T(256)}, u32[]{:S(2)}) copy-start(f32[192]{0:T(256)} %param.15) | copy-start | bytes 2308
  21.5 2.4 %copy-start.5 = (f32[192]{0:T(256)S(1)}, f32[192]{0:T(256)}, u32[]{:S(2)}) copy-start(f32[192]{0:T(256)} %param.17) | copy-start | bytes 2308

commit v4 on v3

--- a/solution.py
+++ b/solution.py
@@ -139,7 +139,7 @@
 
 
 def kernel(last, sums, inner, outer, gain0, wc, w4, bias1, gain1, wf, bias2, out,
-           raw, left, ends, tail, mid, lift, planes, nat, back):
+           raw, left, ends, tail, mid, lift, lines, planes, back):
     group = lax.axis_index("tm")
     strip = lax.axis_index("strip")
     c0 = wc.shape[-1]
@@ -174,87 +174,107 @@
     d = dot(jnp.concatenate([ends[kw, kh, 16 * kt:16 * kt + 96, :] for kt, kw, kh in every], axis=1),
             jnp.concatenate([wc[kt, kh, kw] for kt, kw, kh in every], axis=0))
     for c in range(3):
-        tail[c] = d[:, 128 * c:128 * c + 128]
-    mid[0:384, :] = sums[...]
-    for t in range(6):
-        for w in range(4):
-            for c in range(3):
-                for i, r in enumerate((0, 12)):
-                    at = 64 * t + 16 * w + r
-                    mid[at:at + 2, 128 * c:128 * c + 128] += tail[c, pl.ds(16 * t + 8 * i + w, 2, stride=4), :]
-    row = lax.broadcasted_iota(jnp.int32, (16, c0), 0)
-    keep = jnp.logical_and(jnp.logical_or(strip > 0, row != 0), jnp.logical_or(strip < last, row != 13))
+        tail[c, 8:104, :] = d[:, 128 * c:128 * c + 128]
+    sub = lax.broadcasted_iota(jnp.int32, (8, 128), 0)
+    keep_top = jnp.logical_or(strip > 0, sub != 0)
+    keep_end = jnp.logical_or(strip < last, sub != 5)
     for t in range(6):
         for w in range(4):
             at = 64 * t + 16 * w
-            v = jnp.where(keep, mid[at:at + 16, :], 0.0)
-            mid[at:at + 16, :] = v
-    for t in range(6):
-        for w in range(4):
-            at = 64 * t + 16 * w
-            left[0, at:at + 16, :] = mid[at:at + 16, :].astype(BF)
-            left[1, at:at + 16, :] = mid[at + 1:at + 17, :].astype(BF)
-
-    def ups(lo, n):
-        a = jnp.concatenate([left[0, 64 * t + 16 * lo:64 * t + 16 * (lo + n), :] for t in range(6)], axis=0)
-        b = jnp.concatenate([left[1, 64 * t + 16 * lo:64 * t + 16 * (lo + n), :] for t in range(6)], axis=0)
-        return jnp.concatenate([a, b], axis=1)
-
-    b1 = bias1[...]
-    b1 = jnp.concatenate([b1, b1], axis=1)
-    g1 = gain1[...]
-    g1 = jnp.concatenate([g1, g1], axis=1)
-    lane = lax.broadcasted_iota(jnp.int32, (16, 2 * c1), 1)
-    even = lane < c1
-    row = lax.broadcasted_iota(jnp.int32, (16, 2 * c1), 0)
+            for c in range(3):
+                lanes = slice(128 * c, 128 * c + 128)
+                top = sums[at:at + 8, lanes] + jnp.where(sub < 2, tail[c, pl.ds(16 * t + w + 8, 8, stride=4), :], 0.0)
+                add = jnp.where(sub // 2 == 2, tail[c, pl.ds(16 * t + w, 8, stride=4), :], 0.0)
+                end = sums[at + 8:at + 16, lanes] + add
+                v = jnp.concatenate([jnp.where(keep_top, top, 0.0), jnp.where(keep_end, end, 0.0)], axis=0)
+                mid[c, at:at + 16, :] = v
+                left[0, at:at + 16, lanes] = v.astype(BF)
+    for at in range(0, 384, 16):
+        for c in range(3):
+            left[1, at:at + 16, 128 * c:128 * c + 128] = mid[c, at + 1:at + 17, :].astype(BF)
+
+    def ups(lo, n, first, count):
+        both = [jnp.concatenate([left[i, 64 * t + 16 * lo:64 * t + 16 * (lo + n), :] for t in range(first, first + count)],
+                                axis=0) for i in range(2)]
+        return jnp.concatenate(both, axis=1)
+
+    def thirds(v):
+        v = jnp.concatenate([v, v], axis=1)
+        return [v[:, 128 * c:128 * c + 128] for c in range(3)]
+
+    b1 = thirds(bias1[...])
+    g1 = thirds(0.5 * gain1[...])
+    low = lax.broadcasted_iota(jnp.int32, (16, 128), 1) < 64
+    row = lax.broadcasted_iota(jnp.int32, (16, 1), 0)
+    ok_end = jnp.logical_or(strip < last, row != 12)
+    ok_top = jnp.logical_or(strip > 0, row != 0)
+    early = [jnp.logical_and(ok, group > 0) for ok in (ok_end, ok_top)]
 
     def finish(u, p, t, a):
-        l = (u + b1).astype(BF).astype(F32)
-        lift[a, p, 16 * t:16 * t + 16, :] = l
-        sq = l * l
-        me = jnp.sum(jnp.where(even, sq, 0.0), axis=-1, keepdims=True) * (1.0 / c1)
-        mo = jnp.sum(jnp.where(even, 0.0, sq), axis=-1, keepdims=True) * (1.0 / c1)
-        r = jnp.where(even, lax.rsqrt(me + EPS), lax.rsqrt(mo + EPS))
-        v = silu(l * r * g1)
-        if p == 0:
-            v = jnp.where(even, v, 0.0)
-        if p == 4:
-            v = jnp.where(even, 0.0, v)
-        if a == 0:
-            ok = jnp.logical_or(strip < last, row != 12)
-        else:
-            ok = jnp.logical_or(strip > 0, row != 0)
-        if t < 2:
-            ok = jnp.logical_and(ok, group > 0)
-        nat[a, 0:16, 0:2 * c1] = jnp.where(ok, v, 0.0)
-        planes[a, 0, p, 16 * t:16 * t + 16, :] = nat[a, 0:16, 0:2 * c1].astype(BF)
-        planes[a, 1, p, 16 * t:16 * t + 16, :] = nat[a, 1:17, 0:2 * c1].astype(BF)
-
-    u = dot(jnp.concatenate([ups(0, 3), ups(1, 3)], axis=1), w4[...])
-    for t in range(6):
-        for p in range(1, 4):
+        l = [(u[:, 128 * c:128 * c + 128] + b1[c]).astype(BF).astype(F32) for c in range(3)]
+        at = 16 * t
+        for c in range(3):
+            lift[a, p, c, at:at + 16, :] = l[c]
+        ok = early[a] if t < 2 else (ok_end, ok_top)[a]
+        mids = l[1] * l[1]
+        part = jnp.where(low, mids, 0.0)
+        none = jnp.zeros((16, 1), F32)
+        re = ro = none
+        if p < 4:
+            re = jnp.sum(l[0] * l[0] + part, axis=-1, keepdims=True) * (1.0 / c1)
+            re = jnp.where(ok, lax.rsqrt(re + EPS), 0.0)
+        if p > 0:
+            ro = jnp.sum(l[2] * l[2] + (mids - part), axis=-1, keepdims=True) * (1.0 / c1)
+            ro = jnp.where(ok, lax.rsqrt(ro + EPS), 0.0)
+        for c, r in enumerate((re, jnp.where(low, re, ro), ro)):
+            if r is none:
+                lines[a, p, c, at:at + 16, :] = jnp.zeros((16, 128), F32)
+            else:
+                h = l[c] * (r * g1[c])
+                lines[a, p, c, at:at + 16, :] = h + h * jnp.tanh(h)
+
+    def dense(ref, s, kt):
+        rows = lambda t, k: ref[16 * t + s + k:16 * t + s + k + 8, :]
+        seam = lambda t: jnp.where(sub < 4, rows(t, 8), rows(t + 1, -4))
+        return jnp.concatenate(
+            [rows(kt, 0), seam(kt), rows(kt + 1, 4), rows(kt + 2, 0), seam(kt + 2), rows(kt + 3, 4)], axis=0)
+
+    def pack(p):
+        for a in range(2):
+            for s in range(2):
+                for kt in range(3):
+                    for c in range(3):
+                        planes[a, s, p, kt, :, 128 * c:128 * c + 128] = dense(lines.at[a, p, c], s, kt).astype(BF)
+
+    u0 = dot(ups(0, 1, 0, 6), w4[2 * c0:, :])
+    u4 = dot(ups(3, 1, 0, 6), w4[:2 * c0, :])
+    chunks = [dot(jnp.concatenate([ups(0, 3, 0, 3), ups(1, 3, 0, 3)], axis=1), w4[...])]
+    for p, u in ((0, u0), (4, u4)):
+        for t in range(6):
             for a in range(2):
-                finish(u[48 * t + 16 * p - 16:48 * t + 16 * p, 2 * c1 * a:2 * c1 * (a + 1)], p, t, a)
-    u = dot(ups(0, 1), w4[2 * c0:, :])
-    for t in range(6):
-        for a in range(2):
-            finish(u[16 * t:16 * t + 16, 2 * c1 * a:2 * c1 * (a + 1)], 0, t, a)
-    u = dot(ups(3, 1), w4[:2 * c0, :])
-    for t in range(6):
-        for a in range(2):
-            finish(u[16 * t:16 * t + 16, 2 * c1 * a:2 * c1 * (a + 1)], 4, t, a)
+                finish(u[16 * t:16 * t + 16, 2 * c1 * a:2 * c1 * (a + 1)], p, t, a)
+        pack(p)
+    chunks.append(dot(jnp.concatenate([ups(0, 3, 3, 3), ups(1, 3, 3, 3)], axis=1), w4[...]))
+    for i in range(2):
+        for t in range(3):
+            for p in range(1, 4):
+                at = 48 * t + 16 * (p - 1)
+                for a in range(2):
+                    finish(chunks[i][at:at + 16, 2 * c1 * a:2 * c1 * (a + 1)], p, 3 * i + t, a)
+    for p in range(1, 4):
+        pack(p)
 
     b2 = bias2[...]
     zero = jnp.zeros((64, c1), BF)
     for a in range(2):
         reads = ((1, 0), (0, 0), (1, 1)) if a == 0 else ((0, 0), (1, 1), (0, 1))
-        for b in range(2):
+        for b in (1, 0):
             cols, rhs = [], []
             for kt in range(3):
                 for kh in range(3):
                     ph, sh = reads[kh]
-                    first = jnp.concatenate([planes[ph, sh, q, 16 * kt:16 * kt + 64, :] for q in range(4)], axis=0)
-                    second = jnp.concatenate([planes[ph, sh, q + 1, 16 * kt:16 * kt + 64, :] for q in range(4)], axis=0)
+                    first = jnp.concatenate([planes[ph, sh, q, kt] for q in range(4)], axis=0)
+                    second = jnp.concatenate([planes[ph, sh, q + 1, kt] for q in range(4)], axis=0)
                     k0, k1, k2 = (wf[kt, kh, kw] for kw in range(3))
                     if b == 0:
                         cols += [first, second[:, 128:]]
@@ -262,20 +282,16 @@
                     else:
                         cols += [first[:, :256], second]
                         rhs += [k0, zero, k2, k1]
-            d = dot(jnp.concatenate(cols, axis=1), jnp.concatenate(rhs, axis=0)) + b2
+            d = dot(jnp.concatenate(cols, axis=1), jnp.concatenate(rhs, axis=0))
             for q in range(4):
-                for t in range(4):
-                    p = q if b == 0 else q + 1
-                    at = 16 * (t + 2) + a
-                    l = lift[a, p, at:at + 12, :]
-                    l = l[:, :c1] if b == 0 else l[:, c1:]
-                    v = d[64 * q + 16 * t:64 * q + 16 * t + 12, :] + l
-                    nat_rows = pl.ds((24 * t + a) * 8 + 2 * q + b, 12, stride=16)
-                    back[0, nat_rows, :] = v[:, :128]
-                    back[1, nat_rows, 0:64] = v[:, 128:]
-    for t in range(4):
-        v = jnp.concatenate([back[0, 192 * t:192 * t + 192, :], back[1, 192 * t:192 * t + 192, 0:64]], axis=1)
-        out[t] = v.reshape(24, 8, c1).astype(BF)
+                l = jnp.concatenate([dense(lift.at[a, q + b, b + c], a, 2) for c in range(2)], axis=1)
+                v = d[48 * q:48 * q + 48] + ((l[:, 64:] if b else l[:, :c1]) + b2)
+                back[a, 0, pl.ds(2 * q + b, 48, stride=8), :] = v[:, :128]
+                back[a, 1, pl.ds(2 * q + b, 48, stride=8), 0:64] = v[:, 128:]
+        for t in range(4):
+            for i in range(12):
+                at = 96 * t + 8 * i
+                out[t, 2 * i + a] = jnp.concatenate([back[a, 0, at:at + 8, :], back[a, 1, at:at + 8, 0:64]], axis=1).astype(BF)
 
 
 def block(x, gain0, wc, bias0, wu, bias1, gain1, wf, bias2, *, nt, ns):
@@ -327,12 +343,12 @@
             pltpu.VMEM((3, 128, 128), F32),
             pltpu.VMEM((2, 384, c0), BF),
             pltpu.VMEM((3, 3, 128, c0), BF),
-            pltpu.VMEM((3, 96, 128), F32),
-            pltpu.VMEM((400, c0), F32),
-            pltpu.VMEM((2, 5, 112, 2 * c1), F32),
-            pltpu.VMEM((2, 2, 5, 96, 2 * c1), BF),
-            pltpu.VMEM((2, 32, 2 * c1), F32),
-            pltpu.VMEM((2, 768, 128), F32),
+            pltpu.VMEM((3, 128, 128), F32),
+            pltpu.VMEM((3, 400, 128), F32),
+            pltpu.VMEM((2, 5, 3, 112, 128), F32),
+            pltpu.VMEM((2, 5, 3, 112, 128), F32),
+            pltpu.VMEM((2, 2, 5, 3, 48, 2 * c1), BF),
+            pltpu.VMEM((2, 2, 384, 128), F32),
         ],
         compiler_params=pltpu.CompilerParams(vmem_limit_bytes=14 << 20),
     )(sums, inner, outer, gain0, wv, w4, two(bias1), two(gain1), wf, two(bias2))

time: 32.2 us -> 31.2 us (0.969)
  Pallas kernels: 15.2 us -> 14.2 us
    pallas_call x1, Pallas kernels: 8.04 us -> 7.01 us  [block(): pl.pallas_call(functools.partial(kernel, ns - 1), out_shape=jax.ShapeDtyp...]
  transfers between devices with their start and end apart: 3 -> 3, of which waited for: 1 -> 1; matrix products, arithmetic and copies ran while one was open for 0% -> 0% of each run, Pallas kernels for 22% -> 23%
where the time goes in v4:
time: 31.2 us; the launch traced here: 31 us
  Pallas kernels  14.2 us (46%)
  starting transfers between devices  7.83 us (25%)
  waiting for transfers between devices  7.02 us (22%)
  local copies, waits for them, and re-layouts  1.74 us (6%)
    ppermute x1, waiting for transfers between devices, block(): lax.ppermute(x, axes, [(at(t, s), at(t + 1, s)) for t in range(nt - 1) fo...  7.02 us
    pallas_call x1, Pallas kernels, block(): pl.pallas_call(functools.partial(kernel, ns - 1), out_shape=jax.ShapeDtyp...  7.01 us
    pallas_call x1, Pallas kernels, block(): pl.pallas_call(own, out_shape=(jax.ShapeDtypeStruct((4 * c0, 4 * c1), BF)...  4.84 us
    ppermute x1, starting transfers between devices, block(): lax.ppermute(x, axes, [(at(t, s), at(t + 1, s)) for t in range(nt - 1) fo...  3.11 us
    ppermute x1, starting transfers between devices, block(): lax.ppermute(jnp.where(odd, bottom, top), axes, [(at(t, s), at(t, s + 1 i...  3.1 us
    pallas_call x1, Pallas kernels, block(): pl.pallas_call(old, out_shape=jax.ShapeDtypeStruct((384, c0), F32), in_sp...  2.36 us
    ppermute x1, starting transfers between devices, block(): lax.ppermute(jnp.where(odd, top, bottom), axes, [(at(t, s), at(t, s ^ 1))...  1.62 us
    concatenate x1, local copies, waits for them, and re-layouts, block(): both = jnp.concatenate([prev, x], axis=0)  0.98 us
  transfers between devices with their start and end apart: 3, of which 1 were waited for; matrix products, arithmetic and copies ran while one was open for 0% of the time, Pallas kernels for 23%

profile of v4, /device:TPU:137, one launch (start us, length us, event | category | flops | bytes accessed | tf_op | source)
XLA Modules:
  0.0 31.0 jit_solution(10206036877085166333)
XLA Ops:
  0.0 3.1 %collective-permute-start = (bf16[4,12,4,384]{3,2,1,0:T(4,128)(2,1)}, bf16[4,12,4,384]{3,2,1,0:T(4,128)(2,1)S(1)}, u32[]{:S(2)}, u32[]{:S(2)}) collective-permute-start(bf16[4,12,4,384]{3,2,1,0:T(4,128)(2,1)} %x_hbm.1), channel_id=1, source_target_pairs={{0,8},{1,9},{2,10},{3,11},{4,12},{5,13},{6,14},{7,15},{8,16},{9,17... | collective-permute-start | bytes 442376 | tf_op jit(solution)/shard_map/ppermute | solution.py:305
  3.1 7.0 %collective-permute-done.prev = bf16[4,12,4,384]{3,2,1,0:T(4,128)(2,1)S(1)} collective-permute-done((bf16[4,12,4,384]{3,2,1,0:T(4,128)(2,1)}, bf16[4,12,4,384]{3,2,1,0:T(4,128)(2,1)S(1)}, u32[]{:S(2)}, u32[]{:S(2)}) %collective-permute-start) | collective-permute-done | bytes 147488 | tf_op jit(solution)/shard_map/ppermute | solution.py:305
  10.1 0.1 constant_dynamic-update-slice_fusion.1
  10.2 1.0 %constant_dynamic-update-slice_fusion = bf16[8,12,4,384]{3,2,1,0:T(4,128)(2,1)S(1)} fusion(bf16[8,12,4,384]{3,2,1,0:T(4,128)(2,1)S(1)} %constant_dynamic-update-slice_fusion.1, bf16[4,12,4,384]{3,2,1,0:T(4,128)(2,1)} %x_hbm.1), kind=kLoop, calls=%fused_computation.2 | loop fusion | bytes 294912 | tf_op jit(solution)/shard_map/concatenate | solution.py:322
  11.2 1.6 %collective-permute-start.1 = (bf16[8,2,4,384]{3,2,1,0:T(4,128)(2,1)S(1)}, bf16[8,2,4,384]{3,2,1,0:T(4,128)(2,1)S(1)}, u32[]{:S(2)}, u32[]{:S(2)}) collective-permute-start(bf16[8,2,4,384]{3,2,1,0:T(4,128)(2,1)S(1)} %get-tuple-element.12), channel_id=1, source_target_pairs={{0,1},{1,0},{2,3},{3,2},{4,5},{5,4},{6,7},{7,6},{8,9},{9,8},{10,11... | collective-permute-start | bytes 147464 | tf_op jit(solution)/shard_map/ppermute | solution.py:325
  12.9 3.1 %collective-permute-start.2 = (bf16[8,2,4,384]{3,2,1,0:T(4,128)(2,1)S(1)}, bf16[8,2,4,384]{3,2,1,0:T(4,128)(2,1)S(1)}, u32[]{:S(2)}, u32[]{:S(2)}) collective-permute-start(bf16[8,2,4,384]{3,2,1,0:T(4,128)(2,1)S(1)} %get-tuple-element.11), channel_id=1, source_target_pairs={{1,2},{2,1},{3,4},{4,3},{5,6},{6,5},{9,10},{10,9},{11,12},{12,11},... | collective-permute-start | bytes 147464 | tf_op jit(solution)/shard_map/ppermute | solution.py:327
  16.0 0.0 copy-start.1
  16.0 0.7 %copy-done.1 = f32[384]{0:T(512)S(1)} copy-done((f32[384]{0:T(512)S(1)}, f32[384]{0:T(512)}, u32[]{:S(2)}) %copy-start.1) | copy-done | bytes 1560
  16.7 0.0 copy-start.2
  16.7 4.8 %shard_map.91 = (bf16[1536,768]{1,0:T(8,128)(2,1)S(1)}, bf16[3,3,3,384,384]{4,3,2,1,0:T(8,128)(2,1)S(1)}, f32[256,384]{1,0:T(8,128)S(1)}) custom-call(bf16[4,12,4,384]{3,2,1,0:T(4,128)(2,1)} %x_hbm.1, f32[384]{0:T(512)S(1)} %copy-done.1, bf16[3,3,3,384,384]{4,3,2,1,0:T(8,128)(2,1)} %wc.1, bf16[3,3,192,384]{3,2,1,0:T(8,128)(2,1)} %bitcast.7), custom_call_target="tpu_custom_call" | custom-call | tf_op jit(solution)/shard_map/pallas_call | solution.py:306
  21.5 0.0 copy-done.2
  21.5 0.0 copy-start
  21.5 0.0 copy-start.3
  21.5 0.0 copy-start.4
  21.5 0.0 copy-start.5
  21.6 2.4 %shard_map.92.sums = f32[384,384]{1,0:T(8,128)S(1)} custom-call(f32[256,384]{1,0:T(8,128)S(1)} %get-tuple-element.8.part, bf16[4,12,4,384]{3,2,1,0:T(4,128)(2,1)S(1)} %collective-permute-done.prev, f32[384]{0:T(512)S(1)} %copy-done.1, bf16[3,3,3,384,384]{4,3,2,1,0:T(8,128)(2,1)S(1)} %get-tuple-element.9.wc, f32[384]{0:T(512)S(1)} %copy-done.2), custom_call_target="tpu_custom_call" | custom-call | tf_op jit(solution)/shard_map/pallas_call | solution.py:329
  23.9 0.0 collective-permute-done.1.inner
  23.9 0.0 collective-permute-done.2.outer
  23.9 0.0 copy-done
  24.0 0.0 copy-done.3
  24.0 0.0 copy-done.4
  24.0 0.0 copy-done.5
  24.0 7.0 %shard_map.93 = bf16[4,24,8,192]{3,2,1,0:T(8,128)(2,1)} custom-call(f32[384,384]{1,0:T(8,128)S(1)} %shard_map.92.sums, bf16[8,2,4,384]{3,2,1,0:T(4,128)(2,1)S(1)} %collective-permute-done.1.inner, bf16[8,2,4,384]{3,2,1,0:T(4,128)(2,1)S(1)} %collective-permute-done.2.outer, f32[384]{0:T(512)S(1)} %copy-done.1, ...), custom_call_target="tpu_custom_call" | custom-call | tf_op jit(solution)/shard_map/pallas_call | solution.py:337
  (1 shorter events, 0.0 us)
Async XLA Ops:
  0.0 10.1 %collective-permute-start = (bf16[4,12,4,384]{3,2,1,0:T(4,128)(2,1)}, bf16[4,12,4,384]{3,2,1,0:T(4,128)(2,1)S(1)}, u32[]{:S(2)}, u32[]{:S(2)}) collective-permute-start(bf16[4,12,4,384]{3,2,1,0:T(4,128)(2,1)} %x_hbm.1), channel_id=1, source_target_pairs={{0,8},{1,9},{2,10},{3,11},{4,12},{5,13},{6,14},{7,15},{8,16},{9,17... | collective-permute-start | bytes 442376 | tf_op jit(solution)/shard_map/ppermute | solution.py:305
  11.2 12.7 %collective-permute-start.1 = (bf16[8,2,4,384]{3,2,1,0:T(4,128)(2,1)S(1)}, bf16[8,2,4,384]{3,2,1,0:T(4,128)(2,1)S(1)}, u32[]{:S(2)}, u32[]{:S(2)}) collective-permute-start(bf16[8,2,4,384]{3,2,1,0:T(4,128)(2,1)S(1)} %get-tuple-element.12), channel_id=1, source_target_pairs={{0,1},{1,0},{2,3},{3,2},{4,5},{5,4},{6,7},{7,6},{8,9},{9,8},{10,11... | collective-permute-start | bytes 147464 | tf_op jit(solution)/shard_map/ppermute | solution.py:325
  12.9 11.1 %collective-permute-start.2 = (bf16[8,2,4,384]{3,2,1,0:T(4,128)(2,1)S(1)}, bf16[8,2,4,384]{3,2,1,0:T(4,128)(2,1)S(1)}, u32[]{:S(2)}, u32[]{:S(2)}) collective-permute-start(bf16[8,2,4,384]{3,2,1,0:T(4,128)(2,1)S(1)} %get-tuple-element.11), channel_id=1, source_target_pairs={{1,2},{2,1},{3,4},{4,3},{5,6},{6,5},{9,10},{10,9},{11,12},{12,11},... | collective-permute-start | bytes 147464 | tf_op jit(solution)/shard_map/ppermute | solution.py:327
  16.0 0.7 %copy-start.1 = (f32[384]{0:T(512)S(1)}, f32[384]{0:T(512)}, u32[]{:S(2)}) copy-start(f32[384]{0:T(512)} %gain0.5) | copy-start | bytes 4612
  16.7 4.8 %copy-start.2 = (f32[384]{0:T(512)S(1)}, f32[384]{0:T(512)}, u32[]{:S(2)}) copy-start(f32[384]{0:T(512)} %bias0.1) | copy-start | bytes 4612
  21.5 2.4 %copy-start = (bf16[3,3,3,192,192]{4,3,2,1,0:T(8,128)(2,1)S(1)}, bf16[3,3,3,192,192]{4,3,2,1,0:T(8,128)(2,1)}, u32[]{:S(2)}) copy-start(bf16[3,3,3,192,192]{4,3,2,1,0:T(8,128)(2,1)} %wf.1) | copy-start | bytes 5971972
  21.5 2.4 %copy-start.3 = (f32[192]{0:T(256)S(1)}, f32[192]{0:T(256)}, u32[]{:S(2)}) copy-start(f32[192]{0:T(256)} %param.14) | copy-start | bytes 2308
  21.5 2.4 %copy-start.4 = (f32[192]{0:T(256)S(1)}, f32[192]{0:T(256)}, u32[]{:S(2)}) copy-start(f32[192]{0:T(256)} %param.15) | copy-start | bytes 2308
  21.5 2.4 %copy-start.5 = (f32[192]{0:T(256)S(1)}, f32[192]{0:T(256)}, u32[]{:S(2)}) copy-start(f32[192]{0:T(256)} %param.17) | copy-start | bytes 2308

commit v5 on v4

--- a/solution.py
+++ b/solution.py
@@ -79,19 +79,22 @@
     return jnp.concatenate([wc[kt, kh, kw] for kh in range(3)], axis=0)
 
 
-def own(x_hbm, gain0, wc, wu_hbm, w4, wv, part, x, wu, turned, raw, left, sems):
+def own(x_hbm, gain0_hbm, wc, wu_hbm, w4, wv, part, x, gain0, wu, turned, raw, left, sems):
     c0 = x.shape[-1]
     get_x = pltpu.make_async_copy(x_hbm, x, sems.at[3])
     get_x.start()
+    get_g = pltpu.make_async_copy(gain0_hbm, gain0, sems.at[5])
+    get_g.start()
     get_u = pltpu.make_async_copy(wu_hbm, wu, sems.at[4])
     get_u.start()
     copies = {}
     for kt in (2, 1, 0):
         copies[kt] = pltpu.make_async_copy(wc.at[kt], wv.at[kt], sems.at[kt])
         copies[kt].start()
-    g0 = gain0[...].reshape(1, c0)
     blank(raw, 4)
     get_x.wait()
+    get_g.wait()
+    g0 = gain0[...].reshape(1, c0)
     for t in range(4):
         for h in range(12):
             put(raw, 64 * t + 8 + 4 * h, x[t, h].astype(F32))
@@ -146,52 +149,55 @@
     c1 = wf.shape[-1]
     odd = strip % 2 == 1
 
-    for t in range(8):
-        for i in range(2):
-            a, b = inner[t, i].astype(F32), outer[t, i].astype(F32)
-            put(raw, 16 * t + 4 * i, jnp.where(odd, a, b))
-            put(raw, 16 * t + 8 + 4 * i, jnp.where(odd, b, a))
-    g0 = gain0[...].reshape(1, c0)
-    row = lax.broadcasted_iota(jnp.int32, (8, c0), 0)
-    none = jnp.zeros((8, c0), F32)
-    for half in range(2):
-        v = normed(raw, 64 * half, g0)
-        for i in range(4):
-            t = 4 * half + i
-            up, down = v[16 * i:16 * i + 8], v[16 * i + 8:16 * i + 16]
-            for kh in range(3):
-                a = (up, jnp.where(row < 4, pltpu.roll(up, 4, 0), 0.0), none)[kh]
-                b = (none, jnp.where(row < 4, 0.0, pltpu.roll(down, 4, 0)), down)[kh]
-                for kw in range(3):
-                    if kw == 0:
-                        e = [jnp.where(row % 4 == 0, 0.0, pltpu.roll(z, 1, 0)) for z in (a, b)]
-                    elif kw == 2:
-                        e = [jnp.where(row % 4 == 3, 0.0, pltpu.roll(z, 7, 0)) for z in (a, b)]
-                    else:
-                        e = [a, b]
-                    ends[kw, kh, 16 * t:16 * t + 16, :] = jnp.concatenate(e, axis=0).astype(BF)
-    every = [(kt, kw, kh) for kt in range(3) for kw in range(3) for kh in range(3)]
-    d = dot(jnp.concatenate([ends[kw, kh, 16 * kt:16 * kt + 96, :] for kt, kw, kh in every], axis=1),
-            jnp.concatenate([wc[kt, kh, kw] for kt, kw, kh in every], axis=0))
-    for c in range(3):
-        tail[c, 8:104, :] = d[:, 128 * c:128 * c + 128]
     sub = lax.broadcasted_iota(jnp.int32, (8, 128), 0)
-    keep_top = jnp.logical_or(strip > 0, sub != 0)
-    keep_end = jnp.logical_or(strip < last, sub != 5)
-    for t in range(6):
-        for w in range(4):
-            at = 64 * t + 16 * w
+
+    @pl.when(strip >= 0)
+    def _():
+        for t in range(8):
+            for i in range(2):
+                a, b = inner[t, i].astype(F32), outer[t, i].astype(F32)
+                put(raw, 16 * t + 4 * i, jnp.where(odd, a, b))
+                put(raw, 16 * t + 8 + 4 * i, jnp.where(odd, b, a))
+        g0 = gain0[...].reshape(1, c0)
+        row = lax.broadcasted_iota(jnp.int32, (8, c0), 0)
+        none = jnp.zeros((8, c0), F32)
+        for half in range(2):
+            v = normed(raw, 64 * half, g0)
+            for i in range(4):
+                t = 4 * half + i
+                up, down = v[16 * i:16 * i + 8], v[16 * i + 8:16 * i + 16]
+                for kh in range(3):
+                    a = (up, jnp.where(row < 4, pltpu.roll(up, 4, 0), 0.0), none)[kh]
+                    b = (none, jnp.where(row < 4, 0.0, pltpu.roll(down, 4, 0)), down)[kh]
+                    for kw in range(3):
+                        if kw == 0:
+                            e = [jnp.where(row % 4 == 0, 0.0, pltpu.roll(z, 1, 0)) for z in (a, b)]
+                        elif kw == 2:
+                            e = [jnp.where(row % 4 == 3, 0.0, pltpu.roll(z, 7, 0)) for z in (a, b)]
+                        else:
+                            e = [a, b]
+                        ends[kw, kh, 16 * t:16 * t + 16, :] = jnp.concatenate(e, axis=0).astype(BF)
+        every = [(kt, kw, kh) for kt in range(3) for kw in range(3) for kh in range(3)]
+        d = dot(jnp.concatenate([ends[kw, kh, 16 * kt:16 * kt + 96, :] for kt, kw, kh in every], axis=1),
+                jnp.concatenate([wc[kt, kh, kw] for kt, kw, kh in every], axis=0))
+        for c in range(3):
+            tail[c, 8:104, :] = d[:, 128 * c:128 * c + 128]
+        keep_top = jnp.logical_or(strip > 0, sub != 0)
+        keep_end = jnp.logical_or(strip < last, sub != 5)
+        for t in range(6):
+            for w in range(4):
+                at = 64 * t + 16 * w
+                for c in range(3):
+                    lanes = slice(128 * c, 128 * c + 128)
+                    top = sums[at:at + 8, lanes] + jnp.where(sub < 2, tail[c, pl.ds(16 * t + w + 8, 8, stride=4), :], 0.0)
+                    add = jnp.where(sub // 2 == 2, tail[c, pl.ds(16 * t + w, 8, stride=4), :], 0.0)
+                    end = sums[at + 8:at + 16, lanes] + add
+                    v = jnp.concatenate([jnp.where(keep_top, top, 0.0), jnp.where(keep_end, end, 0.0)], axis=0)
+                    mid[c, at:at + 16, :] = v
+                    left[0, at:at + 16, lanes] = v.astype(BF)
+        for at in range(0, 384, 16):
             for c in range(3):
-                lanes = slice(128 * c, 128 * c + 128)
-                top = sums[at:at + 8, lanes] + jnp.where(sub < 2, tail[c, pl.ds(16 * t + w + 8, 8, stride=4), :], 0.0)
-                add = jnp.where(sub // 2 == 2, tail[c, pl.ds(16 * t + w, 8, stride=4), :], 0.0)
-                end = sums[at + 8:at + 16, lanes] + add
-                v = jnp.concatenate([jnp.where(keep_top, top, 0.0), jnp.where(keep_end, end, 0.0)], axis=0)
-                mid[c, at:at + 16, :] = v
-                left[0, at:at + 16, lanes] = v.astype(BF)
-    for at in range(0, 384, 16):
-        for c in range(3):
-            left[1, at:at + 16, 128 * c:128 * c + 128] = mid[c, at + 1:at + 17, :].astype(BF)
+                left[1, at:at + 16, 128 * c:128 * c + 128] = mid[c, at + 1:at + 17, :].astype(BF)
 
     def ups(lo, n, first, count):
         both = [jnp.concatenate([left[i, 64 * t + 16 * lo:64 * t + 16 * (lo + n), :] for t in range(first, first + count)],
@@ -211,15 +217,15 @@
     early = [jnp.logical_and(ok, group > 0) for ok in (ok_end, ok_top)]
 
     def finish(u, p, t, a):
-        l = [(u[:, 128 * c:128 * c + 128] + b1[c]).astype(BF).astype(F32) for c in range(3)]
+        l = [None if u[c] is None else (u[c] + b1[c]).astype(BF).astype(F32) for c in range(3)]
         at = 16 * t
         for c in range(3):
-            lift[a, p, c, at:at + 16, :] = l[c]
+            if l[c] is not None:
+                lift[a, p, c, at:at + 16, :] = l[c]
         ok = early[a] if t < 2 else (ok_end, ok_top)[a]
         mids = l[1] * l[1]
         part = jnp.where(low, mids, 0.0)
-        none = jnp.zeros((16, 1), F32)
-        re = ro = none
+        re = ro = jnp.zeros((16, 1), F32)
         if p < 4:
             re = jnp.sum(l[0] * l[0] + part, axis=-1, keepdims=True) * (1.0 / c1)
             re = jnp.where(ok, lax.rsqrt(re + EPS), 0.0)
@@ -227,9 +233,7 @@
             ro = jnp.sum(l[2] * l[2] + (mids - part), axis=-1, keepdims=True) * (1.0 / c1)
             ro = jnp.where(ok, lax.rsqrt(ro + EPS), 0.0)
         for c, r in enumerate((re, jnp.where(low, re, ro), ro)):
-            if r is none:
-                lines[a, p, c, at:at + 16, :] = jnp.zeros((16, 128), F32)
-            else:
+            if l[c] is not None:
                 h = l[c] * (r * g1[c])
                 lines[a, p, c, at:at + 16, :] = h + h * jnp.tanh(h)
 
@@ -239,31 +243,52 @@
         return jnp.concatenate(
             [rows(kt, 0), seam(kt), rows(kt + 1, 4), rows(kt + 2, 0), seam(kt + 2), rows(kt + 3, 4)], axis=0)
 
-    def pack(p):
+    def pack(p, kts=range(3)):
+        for kt in kts:
+            for a in range(2):
+                for s in range(2):
+                    for c in range(3):
+                        none = p == 0 and c == 2 or p == 4 and c == 0
+                        v = jnp.zeros((48, 128), BF) if none else dense(lines.at[a, p, c], s, kt).astype(BF)
+                        planes[a, s, p, kt, :, 128 * c:128 * c + 128] = v
+
+    def edge(p):
+        lhs, rhs = (ups(0, 1, 0, 6), slice(2 * c0, 4 * c0)) if p == 0 else (ups(3, 1, 0, 6), slice(0, 2 * c0))
+        u = []
         for a in range(2):
-            for s in range(2):
-                for kt in range(3):
-                    for c in range(3):
-                        planes[a, s, p, kt, :, 128 * c:128 * c + 128] = dense(lines.at[a, p, c], s, kt).astype(BF)
-
-    u0 = dot(ups(0, 1, 0, 6), w4[2 * c0:, :])
-    u4 = dot(ups(3, 1, 0, 6), w4[:2 * c0, :])
-    chunks = [dot(jnp.concatenate([ups(0, 3, 0, 3), ups(1, 3, 0, 3)], axis=1), w4[...])]
-    for p, u in ((0, u0), (4, u4)):
+            n = 2 * c1 * a + (0 if p == 0 else 128)
+            d = dot(lhs, w4[rhs, n:n + 256])
+            u.append([d[:, :128], d[:, 128:], None] if p == 0 else [None, d[:, :128], d[:, 128:]])
+        return u
+
+    def chunk(first, count):
+        return dot(jnp.concatenate([ups(0, 3, first, count), ups(1, 3, first, count)], axis=1), w4[...])
+
+    def finish_edge(u, p):
         for t in range(6):
             for a in range(2):
-                finish(u[16 * t:16 * t + 16, 2 * c1 * a:2 * c1 * (a + 1)], p, t, a)
+                finish([v if v is None else v[16 * t:16 * t + 16] for v in u[a]], p, t, a)
         pack(p)
-    chunks.append(dot(jnp.concatenate([ups(0, 3, 3, 3), ups(1, 3, 3, 3)], axis=1), w4[...]))
-    for i in range(2):
-        for t in range(3):
+
+    def finish_chunk(u, first, count):
+        for t in range(count):
             for p in range(1, 4):
                 at = 48 * t + 16 * (p - 1)
                 for a in range(2):
-                    finish(chunks[i][at:at + 16, 2 * c1 * a:2 * c1 * (a + 1)], p, 3 * i + t, a)
+                    n = 2 * c1 * a
+                    finish([u[at:at + 16, n + 128 * c:n + 128 * c + 128] for c in range(3)], p, first + t, a)
+
+    ua = chunk(0, 4)
+    u0, u4 = edge(0), edge(4)
+    finish_chunk(ua, 0, 4)
+    ub = chunk(4, 2)
     for p in range(1, 4):
-        pack(p)
-
+        pack(p, (0,))
+    finish_edge(u0, 0)
+    finish_edge(u4, 4)
+    finish_chunk(ub, 4, 2)
+    for p in range(1, 4):
+        pack(p, (1, 2))
     b2 = bias2[...]
     zero = jnp.zeros((64, c1), BF)
     for a in range(2):
@@ -307,18 +332,19 @@
         own,
         out_shape=(jax.ShapeDtypeStruct((4 * c0, 4 * c1), BF), jax.ShapeDtypeStruct(wc.shape, BF),
                    jax.ShapeDtypeStruct((256, c0), F32)),
-        in_specs=[hbm, vm, hbm, hbm],
+        in_specs=[hbm] * 4,
         out_specs=(vm, vm, vm),
         scratch_shapes=[
             pltpu.VMEM(x.shape, BF),
+            pltpu.VMEM((c0,), F32),
             pltpu.VMEM((3, 3, c1, c0), BF),
             pltpu.VMEM((4 * c1, 4 * c0), BF),
             pltpu.VMEM((3, 272, 128), F32),
             pltpu.VMEM((3, 256, c0), BF),
-            pltpu.SemaphoreType.DMA((5,)),
+            pltpu.SemaphoreType.DMA((6,)),
         ],
         compiler_params=pltpu.CompilerParams(vmem_limit_bytes=26 << 20),
-    )(far(x), gain0, far(wc), far(jnp.swapaxes(wu, 2, 3)))
+    )(far(x), far(gain0), far(wc), far(jnp.swapaxes(wu, 2, 3)))
     both = jnp.concatenate([prev, x], axis=0)
     odd = lax.axis_index("strip") % 2 == 1
     top, bottom = both[:, :2], both[:, 10:]

time: 31.2 us -> 29.8 us (0.955)
  Pallas kernels: 14.2 us -> 13.5 us
  local copies, waits for them, and re-layouts: 1.74 us -> 1.07 us
    unnamed x13, local copies, waits for them, and re-layouts: 0.76 us -> 0.09 us
    pallas_call x1, Pallas kernels: 7.01 us -> 6.48 us  [block(): pl.pallas_call(functools.partial(kernel, ns - 1), out_shape=jax.ShapeDtyp...]
  transfers between devices with their start and end apart: 3 -> 3, of which waited for: 1 -> 1; matrix products, arithmetic and copies ran while one was open for 0% -> 0% of each run, Pallas kernels for 23% -> 24%
where the time goes in v5:
time: 29.8 us; the launch traced here: 29.7 us
  Pallas kernels  13.5 us (45%)
  starting transfers between devices  7.83 us (26%)
  waiting for transfers between devices  7.02 us (24%)
  local copies, waits for them, and re-layouts  1.07 us (4%)
    ppermute x1, waiting for transfers between devices, block(): lax.ppermute(x, axes, [(at(t, s), at(t + 1, s)) for t in range(nt - 1) fo...  7.02 us
    pallas_call x1, Pallas kernels, block(): pl.pallas_call(functools.partial(kernel, ns - 1), out_shape=jax.ShapeDtyp...  6.48 us
    pallas_call x1, Pallas kernels, block(): pl.pallas_call(own, out_shape=(jax.ShapeDtypeStruct((4 * c0, 4 * c1), BF)...  4.79 us
    ppermute x1, starting transfers between devices, block(): lax.ppermute(x, axes, [(at(t, s), at(t + 1, s)) for t in range(nt - 1) fo...  3.11 us
    ppermute x1, starting transfers between devices, block(): lax.ppermute(jnp.where(odd, bottom, top), axes, [(at(t, s), at(t, s + 1 i...  3.1 us
    pallas_call x1, Pallas kernels, block(): pl.pallas_call(old, out_shape=jax.ShapeDtypeStruct((384, c0), F32), in_sp...  2.25 us
    ppermute x1, starting transfers between devices, block(): lax.ppermute(jnp.where(odd, top, bottom), axes, [(at(t, s), at(t, s ^ 1))...  1.62 us
    concatenate x1, local copies, waits for them, and re-layouts, block(): both = jnp.concatenate([prev, x], axis=0)  0.98 us
  transfers between devices with their start and end apart: 3, of which 1 were waited for; matrix products, arithmetic and copies ran while one was open for 0% of the time, Pallas kernels for 24%

profile of v5, /device:TPU:137, one launch (start us, length us, event | category | flops | bytes accessed | tf_op | source)
XLA Modules:
  0.0 29.7 jit_solution(10792412050389990005)
XLA Ops:
  0.0 3.1 %collective-permute-start = (bf16[4,12,4,384]{3,2,1,0:T(4,128)(2,1)}, bf16[4,12,4,384]{3,2,1,0:T(4,128)(2,1)S(1)}, u32[]{:S(2)}, u32[]{:S(2)}) collective-permute-start(bf16[4,12,4,384]{3,2,1,0:T(4,128)(2,1)} %x_hbm.1), channel_id=1, source_target_pairs={{0,8},{1,9},{2,10},{3,11},{4,12},{5,13},{6,14},{7,15},{8,16},{9,17... | collective-permute-start | bytes 442376 | tf_op jit(solution)/shard_map/ppermute | solution.py:330
  3.1 7.0 %collective-permute-done.prev = bf16[4,12,4,384]{3,2,1,0:T(4,128)(2,1)S(1)} collective-permute-done((bf16[4,12,4,384]{3,2,1,0:T(4,128)(2,1)}, bf16[4,12,4,384]{3,2,1,0:T(4,128)(2,1)S(1)}, u32[]{:S(2)}, u32[]{:S(2)}) %collective-permute-start) | collective-permute-done | bytes 147488 | tf_op jit(solution)/shard_map/ppermute | solution.py:330
  10.1 0.1 constant_dynamic-update-slice_fusion.1
  10.2 1.0 %constant_dynamic-update-slice_fusion = bf16[8,12,4,384]{3,2,1,0:T(4,128)(2,1)S(1)} fusion(bf16[8,12,4,384]{3,2,1,0:T(4,128)(2,1)S(1)} %constant_dynamic-update-slice_fusion.1, bf16[4,12,4,384]{3,2,1,0:T(4,128)(2,1)} %x_hbm.1), kind=kLoop, calls=%fused_computation.2 | loop fusion | bytes 294912 | tf_op jit(solution)/shard_map/concatenate | solution.py:348
  11.2 1.6 %collective-permute-start.1 = (bf16[8,2,4,384]{3,2,1,0:T(4,128)(2,1)S(1)}, bf16[8,2,4,384]{3,2,1,0:T(4,128)(2,1)S(1)}, u32[]{:S(2)}, u32[]{:S(2)}) collective-permute-start(bf16[8,2,4,384]{3,2,1,0:T(4,128)(2,1)S(1)} %get-tuple-element.12), channel_id=1, source_target_pairs={{0,1},{1,0},{2,3},{3,2},{4,5},{5,4},{6,7},{7,6},{8,9},{9,8},{10,11... | collective-permute-start | bytes 147464 | tf_op jit(solution)/shard_map/ppermute | solution.py:351
  12.9 3.1 %collective-permute-start.2 = (bf16[8,2,4,384]{3,2,1,0:T(4,128)(2,1)S(1)}, bf16[8,2,4,384]{3,2,1,0:T(4,128)(2,1)S(1)}, u32[]{:S(2)}, u32[]{:S(2)}) collective-permute-start(bf16[8,2,4,384]{3,2,1,0:T(4,128)(2,1)S(1)} %get-tuple-element.11), channel_id=1, source_target_pairs={{1,2},{2,1},{3,4},{4,3},{5,6},{6,5},{9,10},{10,9},{11,12},{12,11},... | collective-permute-start | bytes 147464 | tf_op jit(solution)/shard_map/ppermute | solution.py:353
  16.0 0.0 copy-start.1
  16.0 0.0 copy-start.2
  16.0 4.8 %shard_map.91 = (bf16[1536,768]{1,0:T(8,128)(2,1)S(1)}, bf16[3,3,3,384,384]{4,3,2,1,0:T(8,128)(2,1)S(1)}, f32[256,384]{1,0:T(8,128)S(1)}) custom-call(bf16[4,12,4,384]{3,2,1,0:T(4,128)(2,1)} %x_hbm.1, f32[384]{0:T(512)} %gain0.3, bf16[3,3,3,384,384]{4,3,2,1,0:T(8,128)(2,1)} %wc.1, bf16[3,3,192,384]{3,2,1,0:T(8,128)(2,1)} %bitcast.7), custom_call_target="tpu_custom_call" | custom-call | tf_op jit(solution)/shard_map/pallas_call | solution.py:331
  20.8 0.0 copy-done.1
  20.8 0.0 copy-done.2
  20.8 0.0 copy-start
  20.8 0.0 copy-start.3
  20.8 0.0 copy-start.4
  20.8 0.0 copy-start.5
  20.9 2.2 %shard_map.92.sums = f32[384,384]{1,0:T(8,128)S(1)} custom-call(f32[256,384]{1,0:T(8,128)S(1)} %get-tuple-element.8.part, bf16[4,12,4,384]{3,2,1,0:T(4,128)(2,1)S(1)} %collective-permute-done.prev, f32[384]{0:T(512)S(1)} %copy-done.1, bf16[3,3,3,384,384]{4,3,2,1,0:T(8,128)(2,1)S(1)} %get-tuple-element.9.wc, f32[384]{0:T(512)S(1)} %copy-done.2), custom_call_target="tpu_custom_call" | custom-call | tf_op jit(solution)/shard_map/pallas_call | solution.py:355
  23.1 0.0 collective-permute-done.1.inner
  23.1 0.0 collective-permute-done.2.outer
  23.1 0.0 copy-done
  23.1 0.0 copy-done.3
  23.2 0.0 copy-done.4
  23.2 0.0 copy-done.5
  23.2 6.5 %shard_map.93 = bf16[4,24,8,192]{3,2,1,0:T(8,128)(2,1)} custom-call(f32[384,384]{1,0:T(8,128)S(1)} %shard_map.92.sums, bf16[8,2,4,384]{3,2,1,0:T(4,128)(2,1)S(1)} %collective-permute-done.1.inner, bf16[8,2,4,384]{3,2,1,0:T(4,128)(2,1)S(1)} %collective-permute-done.2.outer, f32[384]{0:T(512)S(1)} %copy-done.1, ...), custom_call_target="tpu_custom_call" | custom-call | tf_op jit(solution)/shard_map/pallas_call | solution.py:363
  (1 shorter events, 0.0 us)
Async XLA Ops:
  0.0 10.1 %collective-permute-start = (bf16[4,12,4,384]{3,2,1,0:T(4,128)(2,1)}, bf16[4,12,4,384]{3,2,1,0:T(4,128)(2,1)S(1)}, u32[]{:S(2)}, u32[]{:S(2)}) collective-permute-start(bf16[4,12,4,384]{3,2,1,0:T(4,128)(2,1)} %x_hbm.1), channel_id=1, source_target_pairs={{0,8},{1,9},{2,10},{3,11},{4,12},{5,13},{6,14},{7,15},{8,16},{9,17... | collective-permute-start | bytes 442376 | tf_op jit(solution)/shard_map/ppermute | solution.py:330
  11.2 11.9 %collective-permute-start.1 = (bf16[8,2,4,384]{3,2,1,0:T(4,128)(2,1)S(1)}, bf16[8,2,4,384]{3,2,1,0:T(4,128)(2,1)S(1)}, u32[]{:S(2)}, u32[]{:S(2)}) collective-permute-start(bf16[8,2,4,384]{3,2,1,0:T(4,128)(2,1)S(1)} %get-tuple-element.12), channel_id=1, source_target_pairs={{0,1},{1,0},{2,3},{3,2},{4,5},{5,4},{6,7},{7,6},{8,9},{9,8},{10,11... | collective-permute-start | bytes 147464 | tf_op jit(solution)/shard_map/ppermute | solution.py:351
  12.9 10.3 %collective-permute-start.2 = (bf16[8,2,4,384]{3,2,1,0:T(4,128)(2,1)S(1)}, bf16[8,2,4,384]{3,2,1,0:T(4,128)(2,1)S(1)}, u32[]{:S(2)}, u32[]{:S(2)}) collective-permute-start(bf16[8,2,4,384]{3,2,1,0:T(4,128)(2,1)S(1)} %get-tuple-element.11), channel_id=1, source_target_pairs={{1,2},{2,1},{3,4},{4,3},{5,6},{6,5},{9,10},{10,9},{11,12},{12,11},... | collective-permute-start | bytes 147464 | tf_op jit(solution)/shard_map/ppermute | solution.py:353
  16.0 4.8 %copy-start.1 = (f32[384]{0:T(512)S(1)}, f32[384]{0:T(512)}, u32[]{:S(2)}) copy-start(f32[384]{0:T(512)} %gain0.3) | copy-start | bytes 4612
  16.0 4.8 %copy-start.2 = (f32[384]{0:T(512)S(1)}, f32[384]{0:T(512)}, u32[]{:S(2)}) copy-start(f32[384]{0:T(512)} %bias0.1) | copy-start | bytes 4612
  20.8 2.3 %copy-start = (bf16[3,3,3,192,192]{4,3,2,1,0:T(8,128)(2,1)S(1)}, bf16[3,3,3,192,192]{4,3,2,1,0:T(8,128)(2,1)}, u32[]{:S(2)}) copy-start(bf16[3,3,3,192,192]{4,3,2,1,0:T(8,128)(2,1)} %wf.1) | copy-start | bytes 5971972
  20.8 2.3 %copy-start.3 = (f32[192]{0:T(256)S(1)}, f32[192]{0:T(256)}, u32[]{:S(2)}) copy-start(f32[192]{0:T(256)} %param.14) | copy-start | bytes 2308
  20.8 2.3 %copy-start.4 = (f32[192]{0:T(256)S(1)}, f32[192]{0:T(256)}, u32[]{:S(2)}) copy-start(f32[192]{0:T(256)} %param.15) | copy-start | bytes 2308
  20.8 2.3 %copy-start.5 = (f32[192]{0:T(256)S(1)}, f32[192]{0:T(256)}, u32[]{:S(2)}) copy-start(f32[192]{0:T(256)} %param.17) | copy-start | bytes 2308

commit v6 on v5

--- a/solution.py
+++ b/solution.py
@@ -294,19 +294,25 @@
     for a in range(2):
         reads = ((1, 0), (0, 0), (1, 1)) if a == 0 else ((0, 0), (1, 1), (0, 1))
         for b in (1, 0):
-            cols, rhs = [], []
+            cols, rhs, half = [], [], []
             for kt in range(3):
                 for kh in range(3):
                     ph, sh = reads[kh]
                     first = jnp.concatenate([planes[ph, sh, q, kt] for q in range(4)], axis=0)
                     second = jnp.concatenate([planes[ph, sh, q + 1, kt] for q in range(4)], axis=0)
-                    k0, k1, k2 = (wf[kt, kh, kw] for kw in range(3))
+                    k0, k1, k2 = (wf.at[kt, kh, kw] for kw in range(3))
                     if b == 0:
-                        cols += [first, second[:, 128:]]
-                        rhs += [k1, k0, zero, k2]
+                        cols += [first, second[:, 256:]]
+                        rhs += [k1[...], k0[...], k2[64:, :]]
+                        half.append((second[:, 192:256], k2[0:64, :]))
                     else:
-                        cols += [first[:, :256], second]
-                        rhs += [k0, zero, k2, k1]
+                        cols += [first[:, :128], second]
+                        rhs += [k0[0:128, :], k2[...], k1[...]]
+                        half.append((first[:, 128:192], k0[128:, :]))
+            for i in range(0, 9, 2):
+                pair = half[i:i + 2] if i < 8 else [half[8], (half[8][0], zero)]
+                cols.append(jnp.concatenate([v for v, _ in pair], axis=1))
+                rhs += [k for _, k in pair]
             d = dot(jnp.concatenate(cols, axis=1), jnp.concatenate(rhs, axis=0))
             for q in range(4):
                 l = jnp.concatenate([dense(lift.at[a, q + b, b + c], a, 2) for c in range(2)], axis=1)
@@ -345,9 +351,8 @@
         ],
         compiler_params=pltpu.CompilerParams(vmem_limit_bytes=26 << 20),
     )(far(x), far(gain0), far(wc), far(jnp.swapaxes(wu, 2, 3)))
-    both = jnp.concatenate([prev, x], axis=0)
     odd = lax.axis_index("strip") % 2 == 1
-    top, bottom = both[:, :2], both[:, 10:]
+    top, bottom = (jnp.concatenate([v[:, rows] for v in (prev, x)], axis=0) for rows in (slice(0, 2), slice(10, 12)))
     inner = lax.ppermute(jnp.where(odd, top, bottom), axes,
                          [(at(t, s), at(t, s ^ 1)) for t in range(nt) for s in range(ns)])
     outer = lax.ppermute(jnp.where(odd, bottom, top), axes,

time: 29.8 us -> 28.9 us (0.970)
  waiting for transfers between devices: 7.02 us -> 6.22 us
    concatenate x1 -> x0, local copies, waits for them, and re-layouts: 0.98 us -> none  [block(): both = jnp.concatenate([prev, x], axis=0)]
    slice x0 -> x2, local copies, waits for them, and re-layouts: none -> 0.81 us  [block(): v[:, rows]]
    ppermute x1, waiting for transfers between devices: 7.02 us -> 6.22 us  [block(): lax.ppermute(x, axes, [(at(t, s), at(t + 1, s)) for t in range(nt - 1) fo...]
  transfers between devices with their start and end apart: 3 -> 3, of which waited for: 1 -> 1; matrix products, arithmetic and copies ran while one was open for 0% -> 3% of each run, Pallas kernels for 24% -> 25%
where the time goes in v6:
time: 28.9 us; the launch traced here: 28.7 us
  Pallas kernels  13.5 us (47%)
  starting transfers between devices  7.83 us (27%)
  waiting for transfers between devices  6.22 us (22%)
  local copies, waits for them, and re-layouts  0.85 us (3%)
    pallas_call x1, Pallas kernels, block(): pl.pallas_call(functools.partial(kernel, ns - 1), out_shape=jax.ShapeDtyp...  6.49 us
    ppermute x1, waiting for transfers between devices, block(): lax.ppermute(x, axes, [(at(t, s), at(t + 1, s)) for t in range(nt - 1) fo...  6.22 us
    pallas_call x1, Pallas kernels, block(): pl.pallas_call(own, out_shape=(jax.ShapeDtypeStruct((4 * c0, 4 * c1), BF)...  4.79 us
    ppermute x1, starting transfers between devices, block(): lax.ppermute(x, axes, [(at(t, s), at(t + 1, s)) for t in range(nt - 1) fo...  3.11 us
    ppermute x1, starting transfers between devices, block(): lax.ppermute(jnp.where(odd, bottom, top), axes, [(at(t, s), at(t, s + 1 i...  3.1 us
    pallas_call x1, Pallas kernels, block(): pl.pallas_call(old, out_shape=jax.ShapeDtypeStruct((384, c0), F32), in_sp...  2.25 us
    ppermute x1, starting transfers between devices, block(): lax.ppermute(jnp.where(odd, top, bottom), axes, [(at(t, s), at(t, s ^ 1))...  1.62 us
    slice x2, local copies, waits for them, and re-layouts, block(): v[:, rows]  0.81 us
  transfers between devices with their start and end apart: 3, of which 1 were waited for; matrix products, arithmetic and copies ran while one was open for 3% of the time, Pallas kernels for 25%

profile of v6, /device:TPU:137, one launch (start us, length us, event | category | flops | bytes accessed | tf_op | source)
XLA Modules:
  0.0 28.7 jit_solution(17611917745698373507)
XLA Ops:
  0.0 3.1 %collective-permute-start = (bf16[4,12,4,384]{3,2,1,0:T(4,128)(2,1)}, bf16[4,12,4,384]{3,2,1,0:T(4,128)(2,1)S(1)}, u32[]{:S(2)}, u32[]{:S(2)}) collective-permute-start(bf16[4,12,4,384]{3,2,1,0:T(4,128)(2,1)} %x_hbm.1), channel_id=1, source_target_pairs={{0,8},{1,9},{2,10},{3,11},{4,12},{5,13},{6,14},{7,15},{8,16},{9,17... | collective-permute-start | bytes 442376 | tf_op jit(solution)/shard_map/ppermute | solution.py:336
  3.1 0.8 %fusion.1 = (bf16[4,2,4,384]{3,2,1,0:T(4,128)(2,1)S(1)}, bf16[4,2,4,384]{3,2,1,0:T(4,128)(2,1)S(1)}) fusion(bf16[4,12,4,384]{3,2,1,0:T(4,128)(2,1)} %x_hbm.1), kind=kLoop, calls=%fused_computation.5 | loop fusion | bytes 98304 | tf_op jit(solution)/shard_map/slice | solution.py:355
  3.9 6.2 %collective-permute-done.prev = bf16[4,12,4,384]{3,2,1,0:T(4,128)(2,1)S(1)} collective-permute-done((bf16[4,12,4,384]{3,2,1,0:T(4,128)(2,1)}, bf16[4,12,4,384]{3,2,1,0:T(4,128)(2,1)S(1)}, u32[]{:S(2)}, u32[]{:S(2)}) %collective-permute-start) | collective-permute-done | bytes 147488 | tf_op jit(solution)/shard_map/ppermute | solution.py:336
  10.2 0.1 broadcast_select_fusion
  10.3 1.6 %collective-permute-start.1 = (bf16[8,2,4,384]{3,2,1,0:T(4,128)(2,1)S(1)}, bf16[8,2,4,384]{3,2,1,0:T(4,128)(2,1)S(1)}, u32[]{:S(2)}, u32[]{:S(2)}) collective-permute-start(bf16[8,2,4,384]{3,2,1,0:T(4,128)(2,1)S(1)} %get-tuple-element.16), channel_id=1, source_target_pairs={{0,1},{1,0},{2,3},{3,2},{4,5},{5,4},{6,7},{7,6},{8,9},{9,8},{10,11... | collective-permute-start | bytes 147464 | tf_op jit(solution)/shard_map/ppermute | solution.py:356
  11.9 3.1 %collective-permute-start.2 = (bf16[8,2,4,384]{3,2,1,0:T(4,128)(2,1)S(1)}, bf16[8,2,4,384]{3,2,1,0:T(4,128)(2,1)S(1)}, u32[]{:S(2)}, u32[]{:S(2)}) collective-permute-start(bf16[8,2,4,384]{3,2,1,0:T(4,128)(2,1)S(1)} %get-tuple-element.15), channel_id=1, source_target_pairs={{1,2},{2,1},{3,4},{4,3},{5,6},{6,5},{9,10},{10,9},{11,12},{12,11},... | collective-permute-start | bytes 147464 | tf_op jit(solution)/shard_map/ppermute | solution.py:358
  15.0 0.0 copy-start.1
  15.0 0.0 copy-start.2
  15.0 4.8 %shard_map.91 = (bf16[1536,768]{1,0:T(8,128)(2,1)S(1)}, bf16[3,3,3,384,384]{4,3,2,1,0:T(8,128)(2,1)S(1)}, f32[256,384]{1,0:T(8,128)S(1)}) custom-call(bf16[4,12,4,384]{3,2,1,0:T(4,128)(2,1)} %x_hbm.1, f32[384]{0:T(512)} %gain0.3, bf16[3,3,3,384,384]{4,3,2,1,0:T(8,128)(2,1)} %wc.1, bf16[3,3,192,384]{3,2,1,0:T(8,128)(2,1)} %bitcast.7), custom_call_target="tpu_custom_call" | custom-call | tf_op jit(solution)/shard_map/pallas_call | solution.py:337
  19.8 0.0 copy-done.1
  19.8 0.0 copy-done.2
  19.8 0.0 copy-start
  19.8 0.0 copy-start.3
  19.9 0.0 copy-start.4
  19.9 0.0 copy-start.5
  19.9 2.2 %shard_map.92.sums = f32[384,384]{1,0:T(8,128)S(1)} custom-call(f32[256,384]{1,0:T(8,128)S(1)} %get-tuple-element.8.part, bf16[4,12,4,384]{3,2,1,0:T(4,128)(2,1)S(1)} %collective-permute-done.prev, f32[384]{0:T(512)S(1)} %copy-done.1, bf16[3,3,3,384,384]{4,3,2,1,0:T(8,128)(2,1)S(1)} %get-tuple-element.9.wc, f32[384]{0:T(512)S(1)} %copy-done.2), custom_call_target="tpu_custom_call" | custom-call | tf_op jit(solution)/shard_map/pallas_call | solution.py:360
  22.1 0.0 collective-permute-done.1.inner
  22.1 0.0 collective-permute-done.2.outer
  22.2 0.0 copy-done
  22.2 0.0 copy-done.3
  22.2 0.0 copy-done.4
  22.2 0.0 copy-done.5
  22.2 6.5 %shard_map.93 = bf16[4,24,8,192]{3,2,1,0:T(8,128)(2,1)} custom-call(f32[384,384]{1,0:T(8,128)S(1)} %shard_map.92.sums, bf16[8,2,4,384]{3,2,1,0:T(4,128)(2,1)S(1)} %collective-permute-done.1.inner, bf16[8,2,4,384]{3,2,1,0:T(4,128)(2,1)S(1)} %collective-permute-done.2.outer, f32[384]{0:T(512)S(1)} %copy-done.1, ...), custom_call_target="tpu_custom_call" | custom-call | tf_op jit(solution)/shard_map/pallas_call | solution.py:368
  (1 shorter events, 0.0 us)
Async XLA Ops:
  0.0 10.1 %collective-permute-start = (bf16[4,12,4,384]{3,2,1,0:T(4,128)(2,1)}, bf16[4,12,4,384]{3,2,1,0:T(4,128)(2,1)S(1)}, u32[]{:S(2)}, u32[]{:S(2)}) collective-permute-start(bf16[4,12,4,384]{3,2,1,0:T(4,128)(2,1)} %x_hbm.1), channel_id=1, source_target_pairs={{0,8},{1,9},{2,10},{3,11},{4,12},{5,13},{6,14},{7,15},{8,16},{9,17... | collective-permute-start | bytes 442376 | tf_op jit(solution)/shard_map/ppermute | solution.py:336
  10.3 11.9 %collective-permute-start.1 = (bf16[8,2,4,384]{3,2,1,0:T(4,128)(2,1)S(1)}, bf16[8,2,4,384]{3,2,1,0:T(4,128)(2,1)S(1)}, u32[]{:S(2)}, u32[]{:S(2)}) collective-permute-start(bf16[8,2,4,384]{3,2,1,0:T(4,128)(2,1)S(1)} %get-tuple-element.16), channel_id=1, source_target_pairs={{0,1},{1,0},{2,3},{3,2},{4,5},{5,4},{6,7},{7,6},{8,9},{9,8},{10,11... | collective-permute-start | bytes 147464 | tf_op jit(solution)/shard_map/ppermute | solution.py:356
  11.9 10.3 %collective-permute-start.2 = (bf16[8,2,4,384]{3,2,1,0:T(4,128)(2,1)S(1)}, bf16[8,2,4,384]{3,2,1,0:T(4,128)(2,1)S(1)}, u32[]{:S(2)}, u32[]{:S(2)}) collective-permute-start(bf16[8,2,4,384]{3,2,1,0:T(4,128)(2,1)S(1)} %get-tuple-element.15), channel_id=1, source_target_pairs={{1,2},{2,1},{3,4},{4,3},{5,6},{6,5},{9,10},{10,9},{11,12},{12,11},... | collective-permute-start | bytes 147464 | tf_op jit(solution)/shard_map/ppermute | solution.py:358
  15.0 4.8 %copy-start.1 = (f32[384]{0:T(512)S(1)}, f32[384]{0:T(512)}, u32[]{:S(2)}) copy-start(f32[384]{0:T(512)} %gain0.3) | copy-start | bytes 4612
  15.0 4.8 %copy-start.2 = (f32[384]{0:T(512)S(1)}, f32[384]{0:T(512)}, u32[]{:S(2)}) copy-start(f32[384]{0:T(512)} %bias0.1) | copy-start | bytes 4612
  19.8 2.3 %copy-start = (bf16[3,3,3,192,192]{4,3,2,1,0:T(8,128)(2,1)S(1)}, bf16[3,3,3,192,192]{4,3,2,1,0:T(8,128)(2,1)}, u32[]{:S(2)}) copy-start(bf16[3,3,3,192,192]{4,3,2,1,0:T(8,128)(2,1)} %wf.1) | copy-start | bytes 5971972
  19.8 2.3 %copy-start.3 = (f32[192]{0:T(256)S(1)}, f32[192]{0:T(256)}, u32[]{:S(2)}) copy-start(f32[192]{0:T(256)} %param.14) | copy-start | bytes 2308
  19.9 2.3 %copy-start.4 = (f32[192]{0:T(256)S(1)}, f32[192]{0:T(256)}, u32[]{:S(2)}) copy-start(f32[192]{0:T(256)} %param.15) | copy-start | bytes 2308
  19.9 2.3 %copy-start.5 = (f32[192]{0:T(256)S(1)}, f32[192]{0:T(256)}, u32[]{:S(2)}) copy-start(f32[192]{0:T(256)} %param.17) | copy-start | bytes 2308

commit v7 on v5

--- a/solution.py
+++ b/solution.py
@@ -79,7 +79,7 @@
     return jnp.concatenate([wc[kt, kh, kw] for kh in range(3)], axis=0)
 
 
-def own(x_hbm, gain0_hbm, wc, wu_hbm, w4, wv, part, x, gain0, wu, turned, raw, left, sems):
+def own(x_hbm, gain0_hbm, wc, wu_hbm, w4, wv, part, mine, x, gain0, wu, turned, raw, left, sems):
     c0 = x.shape[-1]
     get_x = pltpu.make_async_copy(x_hbm, x, sems.at[3])
     get_x.start()
@@ -93,6 +93,8 @@
         copies[kt].start()
     blank(raw, 4)
     get_x.wait()
+    mine[0] = x[:, :2]
+    mine[1] = x[:, 10:]
     get_g.wait()
     g0 = gain0[...].reshape(1, c0)
     for t in range(4):
@@ -118,7 +120,18 @@
                     part[at:at + 16 * m, :] += v
 
 
-def old(part, prev, gain0, wc, bias0, mid, raw, left):
+def shares(wc, mid, left, kts):
+    for kt in kts:
+        n = 4 - kt
+        for kw in range(3):
+            lo, m = SPAN[kw]
+            d = dot(gather(left, lo, m, kt, n), stack(wc, kt, kw))
+            for u in range(n):
+                at = 64 * u + 16 * (lo + 1 - kw)
+                mid[at:at + 16 * m, :] += d[16 * m * u:16 * m * (u + 1)]
+
+
+def begin(part, prev, gain0, wc, bias0, mid, left, raw):
     c0 = prev.shape[-1]
     g0 = gain0[...].reshape(1, c0)
     b0 = bias0[...].reshape(1, c0)
@@ -131,14 +144,30 @@
         spread(raw, left, t)
     mid[0:128, :] = jnp.broadcast_to(b0, (128, c0))
     mid[128:384, :] = part[...] + b0
-    for kt in range(3):
-        n = 4 - kt
-        for kw in range(3):
-            lo, m = SPAN[kw]
-            d = dot(gather(left, lo, m, kt, n), stack(wc, kt, kw))
-            for u in range(n):
-                at = 64 * u + 16 * (lo + 1 - kw)
-                mid[at:at + 16 * m, :] += d[16 * m * u:16 * m * (u + 1)]
+    shares(wc, mid, left, (0,))
+
+
+def early(part, prev, mine, gain0, wc, bias0, inner, outer, mid, left, raw):
+    odd = lax.axis_index("strip") % 2 == 1
+
+    @pl.when(odd)
+    def _():
+        inner[0:4], inner[4:8] = prev[:, :2], mine[0]
+        outer[0:4], outer[4:8] = prev[:, 10:], mine[1]
+        begin(part, prev, gain0, wc, bias0, mid, left, raw)
+
+    @pl.when(jnp.logical_not(odd))
+    def _():
+        inner[0:4], inner[4:8] = prev[:, 10:], mine[1]
+        outer[0:4], outer[4:8] = prev[:, :2], mine[0]
+
+
+def old(part, prev, gain0, wc, bias0, mid_in, left_in, mid, left, raw):
+    @pl.when(lax.axis_index("strip") % 2 == 0)
+    def _():
+        begin(part, prev, gain0, wc, bias0, mid, left, raw)
+
+    shares(wc, mid, left, (1, 2))
 
 
 def kernel(last, sums, inner, outer, gain0, wc, w4, bias1, gain1, wf, bias2, out,
@@ -161,23 +190,27 @@
         g0 = gain0[...].reshape(1, c0)
         row = lax.broadcasted_iota(jnp.int32, (8, c0), 0)
         none = jnp.zeros((8, c0), F32)
-        for half in range(2):
-            v = normed(raw, 64 * half, g0)
-            for i in range(4):
-                t = 4 * half + i
-                up, down = v[16 * i:16 * i + 8], v[16 * i + 8:16 * i + 16]
-                for kh in range(3):
-                    a = (up, jnp.where(row < 4, pltpu.roll(up, 4, 0), 0.0), none)[kh]
-                    b = (none, jnp.where(row < 4, 0.0, pltpu.roll(down, 4, 0)), down)[kh]
-                    for kw in range(3):
-                        if kw == 0:
-                            e = [jnp.where(row % 4 == 0, 0.0, pltpu.roll(z, 1, 0)) for z in (a, b)]
-                        elif kw == 2:
-                            e = [jnp.where(row % 4 == 3, 0.0, pltpu.roll(z, 7, 0)) for z in (a, b)]
-                        else:
-                            e = [a, b]
-                        ends[kw, kh, 16 * t:16 * t + 16, :] = jnp.concatenate(e, axis=0).astype(BF)
-        every = [(kt, kw, kh) for kt in range(3) for kw in range(3) for kh in range(3)]
+        v = [normed(raw, 64 * half, g0) for half in range(2)]
+        up = [v[t // 4][16 * (t % 4):16 * (t % 4) + 8] for t in range(8)]
+        down = [v[t // 4][16 * (t % 4) + 8:16 * (t % 4) + 16] for t in range(8)]
+
+        def end(kw, kh, t):
+            a = (up[t], jnp.where(row < 4, pltpu.roll(up[t], 4, 0), 0.0), none)[kh]
+            b = (none, jnp.where(row < 4, 0.0, pltpu.roll(down[t], 4, 0)), down[t])[kh]
+            if kw == 0:
+                e = [jnp.where(row % 4 == 0, 0.0, pltpu.roll(z, 1, 0)) for z in (a, b)]
+            elif kw == 2:
+                e = [jnp.where(row % 4 == 3, 0.0, pltpu.roll(z, 7, 0)) for z in (a, b)]
+            else:
+                e = [a, b]
+            return jnp.concatenate(e, axis=0).astype(BF)
+
+        every = [(kt, kw, kh) for kw, kh in ((1, 0), (1, 2), (1, 1), (0, 0), (0, 2), (0, 1), (2, 0), (2, 2), (2, 1))
+                 for kt in range(3)]
+        for kt, kw, kh in every:
+            if kt == 0:
+                for t in range(8):
+                    ends[kw, kh, 16 * t:16 * t + 16, :] = end(kw, kh, t)
         d = dot(jnp.concatenate([ends[kw, kh, 16 * kt:16 * kt + 96, :] for kt, kw, kh in every], axis=1),
                 jnp.concatenate([wc[kt, kh, kw] for kt, kw, kh in every], axis=0))
         for c in range(3):
@@ -328,12 +361,12 @@
     two = lambda v: v.reshape(1, -1)
     axes = ("tm", "strip")
     prev = lax.ppermute(x, axes, [(at(t, s), at(t + 1, s)) for t in range(nt - 1) for s in range(ns)])
-    w4, wv, part = pl.pallas_call(
+    w4, wv, part, mine = pl.pallas_call(
         own,
         out_shape=(jax.ShapeDtypeStruct((4 * c0, 4 * c1), BF), jax.ShapeDtypeStruct(wc.shape, BF),
-                   jax.ShapeDtypeStruct((256, c0), F32)),
+                   jax.ShapeDtypeStruct((256, c0), F32), jax.ShapeDtypeStruct((2, 4, 2) + x.shape[2:], BF)),
         in_specs=[hbm] * 4,
-        out_specs=(vm, vm, vm),
+        out_specs=(vm, vm, vm, vm),
         scratch_shapes=[
             pltpu.VMEM(x.shape, BF),
             pltpu.VMEM((c0,), F32),
@@ -345,21 +378,30 @@
         ],
         compiler_params=pltpu.CompilerParams(vmem_limit_bytes=26 << 20),
     )(far(x), far(gain0), far(wc), far(jnp.swapaxes(wu, 2, 3)))
-    both = jnp.concatenate([prev, x], axis=0)
-    odd = lax.axis_index("strip") % 2 == 1
-    top, bottom = both[:, :2], both[:, 10:]
-    inner = lax.ppermute(jnp.where(odd, top, bottom), axes,
-                         [(at(t, s), at(t, s ^ 1)) for t in range(nt) for s in range(ns)])
-    outer = lax.ppermute(jnp.where(odd, bottom, top), axes,
+    mid = jax.ShapeDtypeStruct((384, c0), F32)
+    left = jax.ShapeDtypeStruct((3, 256, c0), BF)
+    rows = jax.ShapeDtypeStruct((8, 2) + x.shape[2:], BF)
+    params = pltpu.CompilerParams(vmem_limit_bytes=14 << 20)
+    to_inner, to_outer, sums, laid = pl.pallas_call(
+        early,
+        out_shape=(rows, rows, mid, left),
+        in_specs=[vm] * 6,
+        out_specs=(vm,) * 4,
+        scratch_shapes=[pltpu.VMEM((3, 272, 128), F32)],
+        compiler_params=params,
+    )(part, prev, mine, gain0, wv, bias0)
+    inner = lax.ppermute(to_inner, axes, [(at(t, s), at(t, s ^ 1)) for t in range(nt) for s in range(ns)])
+    outer = lax.ppermute(to_outer, axes,
                          [(at(t, s), at(t, s + 1 if s % 2 else s - 1)) for t in range(nt) for s in range(1, ns - 1)])
-    sums = pl.pallas_call(
+    sums, _ = pl.pallas_call(
         old,
-        out_shape=jax.ShapeDtypeStruct((384, c0), F32),
-        in_specs=[vm] * 5,
-        out_specs=vm,
-        scratch_shapes=[pltpu.VMEM((3, 272, 128), F32), pltpu.VMEM((3, 256, c0), BF)],
-        compiler_params=pltpu.CompilerParams(vmem_limit_bytes=14 << 20),
-    )(part, prev, gain0, wv, bias0)
+        out_shape=(mid, left),
+        in_specs=[vm] * 7,
+        out_specs=(vm, vm),
+        scratch_shapes=[pltpu.VMEM((3, 272, 128), F32)],
+        input_output_aliases={5: 0, 6: 1},
+        compiler_params=params,
+    )(part, prev, gain0, wv, bias0, sums, laid)
     return pl.pallas_call(
         functools.partial(kernel, ns - 1),
         out_shape=jax.ShapeDtypeStruct((4, 24, 8, c1), BF),

time: 29.8 us -> 24 us (0.81)
  waiting for transfers between devices: 7.02 us -> 3.07 us
  starting transfers between devices: 7.83 us -> 6.78 us
  local copies, waits for them, and re-layouts: 1.07 us -> 0.03 us
  Pallas kernels: 13.5 us -> 13.8 us
    ppermute x1, waiting for transfers between devices: 7.02 us -> 2.21 us  [block(): lax.ppermute(x, axes, [(at(t, s), at(t + 1, s)) for t in range(nt - 1) fo...]
    ppermute x2, starting transfers between devices: 4.72 us -> 3.67 us  [the longest x1 3.21 us: block(): lax.ppermute(to_outer, axes, [(at(t, s), at(t, s + 1 if s % 2 else s - 1)...]
    concatenate x1 -> x0, local copies, waits for them, and re-layouts: 0.98 us -> none  [block(): both = jnp.concatenate([prev, x], axis=0)]
    ppermute x2, waiting for transfers between devices: 0.01 us -> 0.86 us  [the longest x1 0.86 us: block(): lax.ppermute(to_outer, axes, [(at(t, s), at(t, s + 1 if s % 2 else s - 1)...]
    pallas_call x1 -> x2, Pallas kernels: 2.25 us -> 2.42 us  [the longest x1 1.25 us: block(): pl.pallas_call(old, out_shape=(mid, left), in_specs=[vm] * 7, out_specs=(...]
  transfers between devices with their start and end apart: 3 -> 3, of which waited for: 1 -> 2; matrix products, arithmetic and copies ran while one was open for 0% -> 0% of each run, Pallas kernels for 24% -> 25%
where the time goes in v7:
time: 24 us; the launch traced here: 23.8 us
  Pallas kernels  13.8 us (58%)
  starting transfers between devices  6.78 us (28%)
  waiting for transfers between devices  3.07 us (13%)
    pallas_call x1, Pallas kernels, block(): pl.pallas_call(functools.partial(kernel, ns - 1), out_shape=jax.ShapeDtyp...  6.6 us
    pallas_call x1, Pallas kernels, block(): pl.pallas_call(own, out_shape=(jax.ShapeDtypeStruct((4 * c0, 4 * c1), BF)...  4.79 us
    ppermute x1, starting transfers between devices, block(): lax.ppermute(to_outer, axes, [(at(t, s), at(t, s + 1 if s % 2 else s - 1)...  3.21 us
    ppermute x1, starting transfers between devices, block(): lax.ppermute(x, axes, [(at(t, s), at(t + 1, s)) for t in range(nt - 1) fo...  3.11 us
    ppermute x1, waiting for transfers between devices, block(): lax.ppermute(x, axes, [(at(t, s), at(t + 1, s)) for t in range(nt - 1) fo...  2.21 us
    pallas_call x1, Pallas kernels, block(): pl.pallas_call(old, out_shape=(mid, left), in_specs=[vm] * 7, out_specs=(...  1.25 us
    pallas_call x1, Pallas kernels, block(): pl.pallas_call(early, out_shape=(rows, rows, mid, left), in_specs=[vm] *...  1.17 us
    ppermute x1, waiting for transfers between devices, block(): lax.ppermute(to_outer, axes, [(at(t, s), at(t, s + 1 if s % 2 else s - 1)...  0.86 us
  transfers between devices with their start and end apart: 3, of which 2 were waited for; matrix products, arithmetic and copies ran while one was open for 0% of the time, Pallas kernels for 25%

profile of v7, /device:TPU:137, one launch (start us, length us, event | category | flops | bytes accessed | tf_op | source)
XLA Modules:
  0.0 23.8 jit_solution(7201761600846175830)
XLA Ops:
  0.0 3.1 %collective-permute-start = (bf16[4,12,4,384]{3,2,1,0:T(4,128)(2,1)}, bf16[4,12,4,384]{3,2,1,0:T(4,128)(2,1)S(1)}, u32[]{:S(2)}, u32[]{:S(2)}) collective-permute-start(bf16[4,12,4,384]{3,2,1,0:T(4,128)(2,1)} %x_hbm.1), channel_id=1, source_target_pairs={{0,8},{1,9},{2,10},{3,11},{4,12},{5,13},{6,14},{7,15},{8,16},{9,17... | collective-permute-start | bytes 442376 | tf_op jit(solution)/shard_map/ppermute | solution.py:363
  3.1 0.0 copy-start.1
  3.1 0.0 copy-start.2
  3.1 4.8 %shard_map.91 = (bf16[1536,768]{1,0:T(8,128)(2,1)S(1)}, bf16[3,3,3,384,384]{4,3,2,1,0:T(8,128)(2,1)S(1)}, f32[256,384]{1,0:T(8,128)S(1)}, bf16[2,4,2,4,384]{4,3,2,1,0:T(4,128)(2,1)S(1)}) custom-call(bf16[4,12,4,384]{3,2,1,0:T(4,128)(2,1)} %x_hbm.1, f32[384]{0:T(512)} %gain0.5, bf16[3,3,3,384,384]{4,3,2,1,0:T(8,128)(2,1)} %wc.1, bf16[3,3,192,384]{3,2,1,0:T(8,128)(2,1)} %bitcast.7), custom_call_target="tpu_custom_call" | custom-call | tf_op jit(solution)/shard_map/pallas_call | solution.py:364
  7.9 2.2 %collective-permute-done.prev = bf16[4,12,4,384]{3,2,1,0:T(4,128)(2,1)S(1)} collective-permute-done((bf16[4,12,4,384]{3,2,1,0:T(4,128)(2,1)}, bf16[4,12,4,384]{3,2,1,0:T(4,128)(2,1)S(1)}, u32[]{:S(2)}, u32[]{:S(2)}) %collective-permute-start) | collective-permute-done | bytes 147488 | tf_op jit(solution)/shard_map/ppermute | solution.py:363
  10.1 0.0 copy-done.1
  10.1 0.0 copy-done.2
  10.2 1.2 %shard_map.92 = (bf16[8,2,4,384]{3,2,1,0:T(4,128)(2,1)S(1)}, bf16[8,2,4,384]{3,2,1,0:T(4,128)(2,1)S(1)}, f32[384,384]{1,0:T(8,128)S(1)}, bf16[3,256,384]{2,1,0:T(8,128)(2,1)S(1)}) custom-call(f32[256,384]{1,0:T(8,128)S(1)} %get-tuple-element.14.part, bf16[4,12,4,384]{3,2,1,0:T(4,128)(2,1)S(1)} %collective-permute-done.prev, ...), custom_call_target="tpu_custom_call" | custom-call | tf_op jit(solution)/shard_map/pallas_call | solution.py:385
  11.3 0.5 %collective-permute-start.1 = (bf16[8,2,4,384]{3,2,1,0:T(4,128)(2,1)S(1)}, bf16[8,2,4,384]{3,2,1,0:T(4,128)(2,1)S(1)}, u32[]{:S(2)}, u32[]{:S(2)}) collective-permute-start(bf16[8,2,4,384]{3,2,1,0:T(4,128)(2,1)S(1)} %get-tuple-element.20), channel_id=1, source_target_pairs={{0,1},{1,0},{2,3},{3,2},{4,5},{5,4},{6,7},{7,6},{8,9},{9,8},{10,11... | collective-permute-start | bytes 147464 | tf_op jit(solution)/shard_map/ppermute | solution.py:393
  11.8 3.2 %collective-permute-start.2 = (bf16[8,2,4,384]{3,2,1,0:T(4,128)(2,1)S(1)}, bf16[8,2,4,384]{3,2,1,0:T(4,128)(2,1)S(1)}, u32[]{:S(2)}, u32[]{:S(2)}) collective-permute-start(bf16[8,2,4,384]{3,2,1,0:T(4,128)(2,1)S(1)} %get-tuple-element.21), channel_id=1, source_target_pairs={{1,2},{2,1},{3,4},{4,3},{5,6},{6,5},{9,10},{10,9},{11,12},{12,11},... | collective-permute-start | bytes 147464 | tf_op jit(solution)/shard_map/ppermute | solution.py:394
  15.0 0.0 copy-start
  15.0 0.0 copy-start.3
  15.0 0.0 copy-start.4
  15.0 0.0 copy-start.5
  15.1 1.3 %shard_map.93 = (f32[384,384]{1,0:T(8,128)S(1)}, bf16[3,256,384]{2,1,0:T(8,128)(2,1)S(1)}) custom-call(f32[256,384]{1,0:T(8,128)S(1)} %get-tuple-element.14.part, bf16[4,12,4,384]{3,2,1,0:T(4,128)(2,1)S(1)} %collective-permute-done.prev, f32[384]{0:T(512)S(1)} %copy-done.1, ...), custom_call_target="tpu_custom_call", output_to_operand_aliasing={{0}: (5, {}), {1}: (6, {})} | custom-call | tf_op jit(solution)/shard_map/pallas_call | solution.py:396
  16.3 0.0 collective-permute-done.1.inner
  16.3 0.9 %collective-permute-done.2.outer = bf16[8,2,4,384]{3,2,1,0:T(4,128)(2,1)S(1)} collective-permute-done((bf16[8,2,4,384]{3,2,1,0:T(4,128)(2,1)S(1)}, bf16[8,2,4,384]{3,2,1,0:T(4,128)(2,1)S(1)}, u32[]{:S(2)}, u32[]{:S(2)}) %collective-permute-start.2) | collective-permute-done | bytes 49184 | tf_op jit(solution)/shard_map/ppermute | solution.py:394
  17.2 0.0 copy-done
  17.2 0.0 copy-done.3
  17.2 0.0 copy-done.4
  17.2 0.0 copy-done.5
  17.2 6.6 %shard_map.94 = bf16[4,24,8,192]{3,2,1,0:T(8,128)(2,1)} custom-call(f32[384,384]{1,0:T(8,128)S(1)} %get-tuple-element.19.sums, bf16[8,2,4,384]{3,2,1,0:T(4,128)(2,1)S(1)} %collective-permute-done.1.inner, bf16[8,2,4,384]{3,2,1,0:T(4,128)(2,1)S(1)} %collective-permute-done.2.outer, f32[384]{0:T(512)S(1)} %copy-done.1, ...), custom_call_target="tpu_custom_call" | custom-call | tf_op jit(solution)/shard_map/pallas_call | solution.py:405
Async XLA Ops:
  0.0 10.1 %collective-permute-start = (bf16[4,12,4,384]{3,2,1,0:T(4,128)(2,1)}, bf16[4,12,4,384]{3,2,1,0:T(4,128)(2,1)S(1)}, u32[]{:S(2)}, u32[]{:S(2)}) collective-permute-start(bf16[4,12,4,384]{3,2,1,0:T(4,128)(2,1)} %x_hbm.1), channel_id=1, source_target_pairs={{0,8},{1,9},{2,10},{3,11},{4,12},{5,13},{6,14},{7,15},{8,16},{9,17... | collective-permute-start | bytes 442376 | tf_op jit(solution)/shard_map/ppermute | solution.py:363
  3.1 7.0 %copy-start.1 = (f32[384]{0:T(512)S(1)}, f32[384]{0:T(512)}, u32[]{:S(2)}) copy-start(f32[384]{0:T(512)} %gain0.5) | copy-start | bytes 4612
  3.1 7.0 %copy-start.2 = (f32[384]{0:T(512)S(1)}, f32[384]{0:T(512)}, u32[]{:S(2)}) copy-start(f32[384]{0:T(512)} %bias0.3) | copy-start | bytes 4612
  11.3 5.0 %collective-permute-start.1 = (bf16[8,2,4,384]{3,2,1,0:T(4,128)(2,1)S(1)}, bf16[8,2,4,384]{3,2,1,0:T(4,128)(2,1)S(1)}, u32[]{:S(2)}, u32[]{:S(2)}) collective-permute-start(bf16[8,2,4,384]{3,2,1,0:T(4,128)(2,1)S(1)} %get-tuple-element.20), channel_id=1, source_target_pairs={{0,1},{1,0},{2,3},{3,2},{4,5},{5,4},{6,7},{7,6},{8,9},{9,8},{10,11... | collective-permute-start | bytes 147464 | tf_op jit(solution)/shard_map/ppermute | solution.py:393
  11.8 5.4 %collective-permute-start.2 = (bf16[8,2,4,384]{3,2,1,0:T(4,128)(2,1)S(1)}, bf16[8,2,4,384]{3,2,1,0:T(4,128)(2,1)S(1)}, u32[]{:S(2)}, u32[]{:S(2)}) collective-permute-start(bf16[8,2,4,384]{3,2,1,0:T(4,128)(2,1)S(1)} %get-tuple-element.21), channel_id=1, source_target_pairs={{1,2},{2,1},{3,4},{4,3},{5,6},{6,5},{9,10},{10,9},{11,12},{12,11},... | collective-permute-start | bytes 147464 | tf_op jit(solution)/shard_map/ppermute | solution.py:394
  15.0 2.2 %copy-start = (bf16[3,3,3,192,192]{4,3,2,1,0:T(8,128)(2,1)S(1)}, bf16[3,3,3,192,192]{4,3,2,1,0:T(8,128)(2,1)}, u32[]{:S(2)}) copy-start(bf16[3,3,3,192,192]{4,3,2,1,0:T(8,128)(2,1)} %wf.1) | copy-start | bytes 5971972
  15.0 2.2 %copy-start.3 = (f32[192]{0:T(256)S(1)}, f32[192]{0:T(256)}, u32[]{:S(2)}) copy-start(f32[192]{0:T(256)} %param.14) | copy-start | bytes 2308
  15.0 2.2 %copy-start.4 = (f32[192]{0:T(256)S(1)}, f32[192]{0:T(256)}, u32[]{:S(2)}) copy-start(f32[192]{0:T(256)} %param.15) | copy-start | bytes 2308
  15.0 2.2 %copy-start.5 = (f32[192]{0:T(256)S(1)}, f32[192]{0:T(256)}, u32[]{:S(2)}) copy-start(f32[192]{0:T(256)} %param.17) | copy-start | bytes 2308

commit v8 on v7

--- a/solution.py
+++ b/solution.py
@@ -190,27 +190,23 @@
         g0 = gain0[...].reshape(1, c0)
         row = lax.broadcasted_iota(jnp.int32, (8, c0), 0)
         none = jnp.zeros((8, c0), F32)
-        v = [normed(raw, 64 * half, g0) for half in range(2)]
-        up = [v[t // 4][16 * (t % 4):16 * (t % 4) + 8] for t in range(8)]
-        down = [v[t // 4][16 * (t % 4) + 8:16 * (t % 4) + 16] for t in range(8)]
-
-        def end(kw, kh, t):
-            a = (up[t], jnp.where(row < 4, pltpu.roll(up[t], 4, 0), 0.0), none)[kh]
-            b = (none, jnp.where(row < 4, 0.0, pltpu.roll(down[t], 4, 0)), down[t])[kh]
-            if kw == 0:
-                e = [jnp.where(row % 4 == 0, 0.0, pltpu.roll(z, 1, 0)) for z in (a, b)]
-            elif kw == 2:
-                e = [jnp.where(row % 4 == 3, 0.0, pltpu.roll(z, 7, 0)) for z in (a, b)]
-            else:
-                e = [a, b]
-            return jnp.concatenate(e, axis=0).astype(BF)
-
-        every = [(kt, kw, kh) for kw, kh in ((1, 0), (1, 2), (1, 1), (0, 0), (0, 2), (0, 1), (2, 0), (2, 2), (2, 1))
-                 for kt in range(3)]
-        for kt, kw, kh in every:
-            if kt == 0:
-                for t in range(8):
-                    ends[kw, kh, 16 * t:16 * t + 16, :] = end(kw, kh, t)
+        for half in range(2):
+            v = normed(raw, 64 * half, g0)
+            for i in range(4):
+                t = 4 * half + i
+                up, down = v[16 * i:16 * i + 8], v[16 * i + 8:16 * i + 16]
+                for kh in range(3):
+                    a = (up, jnp.where(row < 4, pltpu.roll(up, 4, 0), 0.0), none)[kh]
+                    b = (none, jnp.where(row < 4, 0.0, pltpu.roll(down, 4, 0)), down)[kh]
+                    for kw in range(3):
+                        if kw == 0:
+                            e = [jnp.where(row % 4 == 0, 0.0, pltpu.roll(z, 1, 0)) for z in (a, b)]
+                        elif kw == 2:
+                            e = [jnp.where(row % 4 == 3, 0.0, pltpu.roll(z, 7, 0)) for z in (a, b)]
+                        else:
+                            e = [a, b]
+                        ends[kw, kh, 16 * t:16 * t + 16, :] = jnp.concatenate(e, axis=0).astype(BF)
+        every = [(kt, kw, kh) for kt in range(3) for kw in range(3) for kh in range(3)]
         d = dot(jnp.concatenate([ends[kw, kh, 16 * kt:16 * kt + 96, :] for kt, kw, kh in every], axis=1),
                 jnp.concatenate([wc[kt, kh, kw] for kt, kw, kh in every], axis=0))
         for c in range(3):

time: 24 us -> 24 us (level)
  no operation moved by 1% of the time
where the time goes in v8:
time: 24 us; the launch traced here: 23.8 us
  Pallas kernels  13.8 us (58%)
  starting transfers between devices  6.78 us (28%)
  waiting for transfers between devices  3.07 us (13%)
    pallas_call x1, Pallas kernels, block(): pl.pallas_call(functools.partial(kernel, ns - 1), out_shape=jax.ShapeDtyp...  6.63 us
    pallas_call x1, Pallas kernels, block(): pl.pallas_call(own, out_shape=(jax.ShapeDtypeStruct((4 * c0, 4 * c1), BF)...  4.79 us
    ppermute x1, starting transfers between devices, block(): lax.ppermute(to_outer, axes, [(at(t, s), at(t, s + 1 if s % 2 else s - 1)...  3.21 us
    ppermute x1, starting transfers between devices, block(): lax.ppermute(x, axes, [(at(t, s), at(t + 1, s)) for t in range(nt - 1) fo...  3.11 us
    ppermute x1, waiting for transfers between devices, block(): lax.ppermute(x, axes, [(at(t, s), at(t + 1, s)) for t in range(nt - 1) fo...  2.21 us
    pallas_call x1, Pallas kernels, block(): pl.pallas_call(old, out_shape=(mid, left), in_specs=[vm] * 7, out_specs=(...  1.25 us
    pallas_call x1, Pallas kernels, block(): pl.pallas_call(early, out_shape=(rows, rows, mid, left), in_specs=[vm] *...  1.17 us
    ppermute x1, waiting for transfers between devices, block(): lax.ppermute(to_outer, axes, [(at(t, s), at(t, s + 1 if s % 2 else s - 1)...  0.86 us
  transfers between devices with their start and end apart: 3, of which 2 were waited for; matrix products, arithmetic and copies ran while one was open for 0% of the time, Pallas kernels for 25%

profile of v8, /device:TPU:137, one launch (start us, length us, event | category | flops | bytes accessed | tf_op | source)
XLA Modules:
  0.0 23.8 jit_solution(14139500528123444745)
XLA Ops:
  0.0 3.1 %collective-permute-start = (bf16[4,12,4,384]{3,2,1,0:T(4,128)(2,1)}, bf16[4,12,4,384]{3,2,1,0:T(4,128)(2,1)S(1)}, u32[]{:S(2)}, u32[]{:S(2)}) collective-permute-start(bf16[4,12,4,384]{3,2,1,0:T(4,128)(2,1)} %x_hbm.1), channel_id=1, source_target_pairs={{0,8},{1,9},{2,10},{3,11},{4,12},{5,13},{6,14},{7,15},{8,16},{9,17... | collective-permute-start | bytes 442376 | tf_op jit(solution)/shard_map/ppermute | solution.py:359
  3.1 0.0 copy-start.1
  3.1 0.0 copy-start.2
  3.1 4.8 %shard_map.91 = (bf16[1536,768]{1,0:T(8,128)(2,1)S(1)}, bf16[3,3,3,384,384]{4,3,2,1,0:T(8,128)(2,1)S(1)}, f32[256,384]{1,0:T(8,128)S(1)}, bf16[2,4,2,4,384]{4,3,2,1,0:T(4,128)(2,1)S(1)}) custom-call(bf16[4,12,4,384]{3,2,1,0:T(4,128)(2,1)} %x_hbm.1, f32[384]{0:T(512)} %gain0.5, bf16[3,3,3,384,384]{4,3,2,1,0:T(8,128)(2,1)} %wc.1, bf16[3,3,192,384]{3,2,1,0:T(8,128)(2,1)} %bitcast.7), custom_call_target="tpu_custom_call" | custom-call | tf_op jit(solution)/shard_map/pallas_call | solution.py:360
  7.9 2.2 %collective-permute-done.prev = bf16[4,12,4,384]{3,2,1,0:T(4,128)(2,1)S(1)} collective-permute-done((bf16[4,12,4,384]{3,2,1,0:T(4,128)(2,1)}, bf16[4,12,4,384]{3,2,1,0:T(4,128)(2,1)S(1)}, u32[]{:S(2)}, u32[]{:S(2)}) %collective-permute-start) | collective-permute-done | bytes 147488 | tf_op jit(solution)/shard_map/ppermute | solution.py:359
  10.1 0.0 copy-done.1
  10.1 0.0 copy-done.2
  10.2 1.2 %shard_map.92 = (bf16[8,2,4,384]{3,2,1,0:T(4,128)(2,1)S(1)}, bf16[8,2,4,384]{3,2,1,0:T(4,128)(2,1)S(1)}, f32[384,384]{1,0:T(8,128)S(1)}, bf16[3,256,384]{2,1,0:T(8,128)(2,1)S(1)}) custom-call(f32[256,384]{1,0:T(8,128)S(1)} %get-tuple-element.14.part, bf16[4,12,4,384]{3,2,1,0:T(4,128)(2,1)S(1)} %collective-permute-done.prev, ...), custom_call_target="tpu_custom_call" | custom-call | tf_op jit(solution)/shard_map/pallas_call | solution.py:381
  11.3 0.5 %collective-permute-start.1 = (bf16[8,2,4,384]{3,2,1,0:T(4,128)(2,1)S(1)}, bf16[8,2,4,384]{3,2,1,0:T(4,128)(2,1)S(1)}, u32[]{:S(2)}, u32[]{:S(2)}) collective-permute-start(bf16[8,2,4,384]{3,2,1,0:T(4,128)(2,1)S(1)} %get-tuple-element.20), channel_id=1, source_target_pairs={{0,1},{1,0},{2,3},{3,2},{4,5},{5,4},{6,7},{7,6},{8,9},{9,8},{10,11... | collective-permute-start | bytes 147464 | tf_op jit(solution)/shard_map/ppermute | solution.py:389
  11.8 3.2 %collective-permute-start.2 = (bf16[8,2,4,384]{3,2,1,0:T(4,128)(2,1)S(1)}, bf16[8,2,4,384]{3,2,1,0:T(4,128)(2,1)S(1)}, u32[]{:S(2)}, u32[]{:S(2)}) collective-permute-start(bf16[8,2,4,384]{3,2,1,0:T(4,128)(2,1)S(1)} %get-tuple-element.21), channel_id=1, source_target_pairs={{1,2},{2,1},{3,4},{4,3},{5,6},{6,5},{9,10},{10,9},{11,12},{12,11},... | collective-permute-start | bytes 147464 | tf_op jit(solution)/shard_map/ppermute | solution.py:390
  15.0 0.0 copy-start
  15.0 0.0 copy-start.3
  15.0 0.0 copy-start.4
  15.0 0.0 copy-start.5
  15.1 1.3 %shard_map.93 = (f32[384,384]{1,0:T(8,128)S(1)}, bf16[3,256,384]{2,1,0:T(8,128)(2,1)S(1)}) custom-call(f32[256,384]{1,0:T(8,128)S(1)} %get-tuple-element.14.part, bf16[4,12,4,384]{3,2,1,0:T(4,128)(2,1)S(1)} %collective-permute-done.prev, f32[384]{0:T(512)S(1)} %copy-done.1, ...), custom_call_target="tpu_custom_call", output_to_operand_aliasing={{0}: (5, {}), {1}: (6, {})} | custom-call | tf_op jit(solution)/shard_map/pallas_call | solution.py:392
  16.3 0.0 collective-permute-done.1.inner
  16.3 0.9 %collective-permute-done.2.outer = bf16[8,2,4,384]{3,2,1,0:T(4,128)(2,1)S(1)} collective-permute-done((bf16[8,2,4,384]{3,2,1,0:T(4,128)(2,1)S(1)}, bf16[8,2,4,384]{3,2,1,0:T(4,128)(2,1)S(1)}, u32[]{:S(2)}, u32[]{:S(2)}) %collective-permute-start.2) | collective-permute-done | bytes 49184 | tf_op jit(solution)/shard_map/ppermute | solution.py:390
  17.2 0.0 copy-done
  17.2 0.0 copy-done.3
  17.2 0.0 copy-done.4
  17.2 0.0 copy-done.5
  17.2 6.6 %shard_map.94 = bf16[4,24,8,192]{3,2,1,0:T(8,128)(2,1)} custom-call(f32[384,384]{1,0:T(8,128)S(1)} %get-tuple-element.19.sums, bf16[8,2,4,384]{3,2,1,0:T(4,128)(2,1)S(1)} %collective-permute-done.1.inner, bf16[8,2,4,384]{3,2,1,0:T(4,128)(2,1)S(1)} %collective-permute-done.2.outer, f32[384]{0:T(512)S(1)} %copy-done.1, ...), custom_call_target="tpu_custom_call" | custom-call | tf_op jit(solution)/shard_map/pallas_call | solution.py:401
Async XLA Ops:
  0.0 10.1 %collective-permute-start = (bf16[4,12,4,384]{3,2,1,0:T(4,128)(2,1)}, bf16[4,12,4,384]{3,2,1,0:T(4,128)(2,1)S(1)}, u32[]{:S(2)}, u32[]{:S(2)}) collective-permute-start(bf16[4,12,4,384]{3,2,1,0:T(4,128)(2,1)} %x_hbm.1), channel_id=1, source_target_pairs={{0,8},{1,9},{2,10},{3,11},{4,12},{5,13},{6,14},{7,15},{8,16},{9,17... | collective-permute-start | bytes 442376 | tf_op jit(solution)/shard_map/ppermute | solution.py:359
  3.1 7.0 %copy-start.1 = (f32[384]{0:T(512)S(1)}, f32[384]{0:T(512)}, u32[]{:S(2)}) copy-start(f32[384]{0:T(512)} %gain0.5) | copy-start | bytes 4612
  3.1 7.0 %copy-start.2 = (f32[384]{0:T(512)S(1)}, f32[384]{0:T(512)}, u32[]{:S(2)}) copy-start(f32[384]{0:T(512)} %bias0.3) | copy-start | bytes 4612
  11.3 5.0 %collective-permute-start.1 = (bf16[8,2,4,384]{3,2,1,0:T(4,128)(2,1)S(1)}, bf16[8,2,4,384]{3,2,1,0:T(4,128)(2,1)S(1)}, u32[]{:S(2)}, u32[]{:S(2)}) collective-permute-start(bf16[8,2,4,384]{3,2,1,0:T(4,128)(2,1)S(1)} %get-tuple-element.20), channel_id=1, source_target_pairs={{0,1},{1,0},{2,3},{3,2},{4,5},{5,4},{6,7},{7,6},{8,9},{9,8},{10,11... | collective-permute-start | bytes 147464 | tf_op jit(solution)/shard_map/ppermute | solution.py:389
  11.8 5.4 %collective-permute-start.2 = (bf16[8,2,4,384]{3,2,1,0:T(4,128)(2,1)S(1)}, bf16[8,2,4,384]{3,2,1,0:T(4,128)(2,1)S(1)}, u32[]{:S(2)}, u32[]{:S(2)}) collective-permute-start(bf16[8,2,4,384]{3,2,1,0:T(4,128)(2,1)S(1)} %get-tuple-element.21), channel_id=1, source_target_pairs={{1,2},{2,1},{3,4},{4,3},{5,6},{6,5},{9,10},{10,9},{11,12},{12,11},... | collective-permute-start | bytes 147464 | tf_op jit(solution)/shard_map/ppermute | solution.py:390
  15.0 2.2 %copy-start = (bf16[3,3,3,192,192]{4,3,2,1,0:T(8,128)(2,1)S(1)}, bf16[3,3,3,192,192]{4,3,2,1,0:T(8,128)(2,1)}, u32[]{:S(2)}) copy-start(bf16[3,3,3,192,192]{4,3,2,1,0:T(8,128)(2,1)} %wf.1) | copy-start | bytes 5971972
  15.0 2.2 %copy-start.3 = (f32[192]{0:T(256)S(1)}, f32[192]{0:T(256)}, u32[]{:S(2)}) copy-start(f32[192]{0:T(256)} %param.14) | copy-start | bytes 2308
  15.0 2.2 %copy-start.4 = (f32[192]{0:T(256)S(1)}, f32[192]{0:T(256)}, u32[]{:S(2)}) copy-start(f32[192]{0:T(256)} %param.15) | copy-start | bytes 2308
  15.0 2.2 %copy-start.5 = (f32[192]{0:T(256)S(1)}, f32[192]{0:T(256)}, u32[]{:S(2)}) copy-start(f32[192]{0:T(256)} %param.17) | copy-start | bytes 2308

commit v9 on v8

--- a/solution.py
+++ b/solution.py
@@ -147,14 +147,13 @@
     shares(wc, mid, left, (0,))
 
 
-def early(part, prev, mine, gain0, wc, bias0, inner, outer, mid, left, raw):
+def early(prev, mine, inner, outer):
     odd = lax.axis_index("strip") % 2 == 1
 
     @pl.when(odd)
     def _():
         inner[0:4], inner[4:8] = prev[:, :2], mine[0]
         outer[0:4], outer[4:8] = prev[:, 10:], mine[1]
-        begin(part, prev, gain0, wc, bias0, mid, left, raw)
 
     @pl.when(jnp.logical_not(odd))
     def _():
@@ -162,11 +161,8 @@
         outer[0:4], outer[4:8] = prev[:, :2], mine[0]
 
 
-def old(part, prev, gain0, wc, bias0, mid_in, left_in, mid, left, raw):
-    @pl.when(lax.axis_index("strip") % 2 == 0)
-    def _():
-        begin(part, prev, gain0, wc, bias0, mid, left, raw)
-
+def old(part, prev, gain0, wc, bias0, mid, left, raw):
+    begin(part, prev, gain0, wc, bias0, mid, left, raw)
     shares(wc, mid, left, (1, 2))
 
 
@@ -374,30 +370,26 @@
         ],
         compiler_params=pltpu.CompilerParams(vmem_limit_bytes=26 << 20),
     )(far(x), far(gain0), far(wc), far(jnp.swapaxes(wu, 2, 3)))
-    mid = jax.ShapeDtypeStruct((384, c0), F32)
-    left = jax.ShapeDtypeStruct((3, 256, c0), BF)
     rows = jax.ShapeDtypeStruct((8, 2) + x.shape[2:], BF)
     params = pltpu.CompilerParams(vmem_limit_bytes=14 << 20)
-    to_inner, to_outer, sums, laid = pl.pallas_call(
+    to_inner, to_outer = pl.pallas_call(
         early,
-        out_shape=(rows, rows, mid, left),
-        in_specs=[vm] * 6,
-        out_specs=(vm,) * 4,
-        scratch_shapes=[pltpu.VMEM((3, 272, 128), F32)],
+        out_shape=(rows, rows),
+        in_specs=[vm] * 2,
+        out_specs=(vm, vm),
         compiler_params=params,
-    )(part, prev, mine, gain0, wv, bias0)
+    )(prev, mine)
     inner = lax.ppermute(to_inner, axes, [(at(t, s), at(t, s ^ 1)) for t in range(nt) for s in range(ns)])
     outer = lax.ppermute(to_outer, axes,
                          [(at(t, s), at(t, s + 1 if s % 2 else s - 1)) for t in range(nt) for s in range(1, ns - 1)])
-    sums, _ = pl.pallas_call(
+    sums = pl.pallas_call(
         old,
-        out_shape=(mid, left),
-        in_specs=[vm] * 7,
-        out_specs=(vm, vm),
-        scratch_shapes=[pltpu.VMEM((3, 272, 128), F32)],
-        input_output_aliases={5: 0, 6: 1},
+        out_shape=jax.ShapeDtypeStruct((384, c0), F32),
+        in_specs=[vm] * 5,
+        out_specs=vm,
+        scratch_shapes=[pltpu.VMEM((3, 256, c0), BF), pltpu.VMEM((3, 272, 128), F32)],
         compiler_params=params,
-    )(part, prev, gain0, wv, bias0, sums, laid)
+    )(part, prev, gain0, wv, bias0)
     return pl.pallas_call(
         functools.partial(kernel, ns - 1),
         out_shape=jax.ShapeDtypeStruct((4, 24, 8, c1), BF),

time: 24 us -> 23.9 us (level)
  starting transfers between devices: 6.78 us -> 7.82 us
  waiting for transfers between devices: 3.07 us -> 2.22 us
  Pallas kernels: 13.8 us -> 13.5 us
    ppermute x1, starting transfers between devices: 0.46 us -> 1.61 us  [block(): lax.ppermute(to_inner, axes, [(at(t, s), at(t, s ^ 1)) for t in range(nt)...]
    ppermute x1, waiting for transfers between devices: 0.86 us -> 0.01 us  [block(): lax.ppermute(to_outer, axes, [(at(t, s), at(t, s + 1 if s % 2 else s - 1)...]
  transfers between devices with their start and end apart: 3 -> 3, of which waited for: 2 -> 1; matrix products, arithmetic and copies ran while one was open for 0% -> 0% of each run, Pallas kernels for 25% -> 30%
where the time goes in v9:
time: 23.9 us; the launch traced here: 23.8 us
  Pallas kernels  13.5 us (56%)
  starting transfers between devices  7.82 us (33%)
  waiting for transfers between devices  2.22 us (9%)
    pallas_call x1, Pallas kernels, block(): pl.pallas_call(functools.partial(kernel, ns - 1), out_shape=jax.ShapeDtyp...  6.48 us
    pallas_call x1, Pallas kernels, block(): pl.pallas_call(own, out_shape=(jax.ShapeDtypeStruct((4 * c0, 4 * c1), BF)...  4.79 us
    ppermute x1, starting transfers between devices, block(): lax.ppermute(x, axes, [(at(t, s), at(t + 1, s)) for t in range(nt - 1) fo...  3.11 us
    ppermute x1, starting transfers between devices, block(): lax.ppermute(to_outer, axes, [(at(t, s), at(t, s + 1 if s % 2 else s - 1)...  3.1 us
    pallas_call x1, Pallas kernels, block(): pl.pallas_call(old, out_shape=jax.ShapeDtypeStruct((384, c0), F32), in_sp...  2.25 us
    ppermute x1, waiting for transfers between devices, block(): lax.ppermute(x, axes, [(at(t, s), at(t + 1, s)) for t in range(nt - 1) fo...  2.21 us
    ppermute x1, starting transfers between devices, block(): lax.ppermute(to_inner, axes, [(at(t, s), at(t, s ^ 1)) for t in range(nt)...  1.61 us
  transfers between devices with their start and end apart: 3, of which 1 were waited for; matrix products, arithmetic and copies ran while one was open for 0% of the time, Pallas kernels for 30%

profile of v9, /device:TPU:137, one launch (start us, length us, event | category | flops | bytes accessed | tf_op | source)
XLA Modules:
  0.0 23.8 jit_solution(9133553661294714598)
XLA Ops:
  0.0 3.1 %collective-permute-start = (bf16[4,12,4,384]{3,2,1,0:T(4,128)(2,1)}, bf16[4,12,4,384]{3,2,1,0:T(4,128)(2,1)S(1)}, u32[]{:S(2)}, u32[]{:S(2)}) collective-permute-start(bf16[4,12,4,384]{3,2,1,0:T(4,128)(2,1)} %x_hbm.1), channel_id=1, source_target_pairs={{0,8},{1,9},{2,10},{3,11},{4,12},{5,13},{6,14},{7,15},{8,16},{9,17... | collective-permute-start | bytes 442376 | tf_op jit(solution)/shard_map/ppermute | solution.py:355
  3.1 0.0 copy-start.1
  3.1 0.0 copy-start.2
  3.1 4.8 %shard_map.91 = (bf16[1536,768]{1,0:T(8,128)(2,1)S(1)}, bf16[3,3,3,384,384]{4,3,2,1,0:T(8,128)(2,1)S(1)}, f32[256,384]{1,0:T(8,128)S(1)}, bf16[2,4,2,4,384]{4,3,2,1,0:T(4,128)(2,1)S(1)}) custom-call(bf16[4,12,4,384]{3,2,1,0:T(4,128)(2,1)} %x_hbm.1, f32[384]{0:T(512)} %gain0.3, bf16[3,3,3,384,384]{4,3,2,1,0:T(8,128)(2,1)} %wc.1, bf16[3,3,192,384]{3,2,1,0:T(8,128)(2,1)} %bitcast.7), custom_call_target="tpu_custom_call" | custom-call | tf_op jit(solution)/shard_map/pallas_call | solution.py:356
  7.9 2.2 %collective-permute-done.prev = bf16[4,12,4,384]{3,2,1,0:T(4,128)(2,1)S(1)} collective-permute-done((bf16[4,12,4,384]{3,2,1,0:T(4,128)(2,1)}, bf16[4,12,4,384]{3,2,1,0:T(4,128)(2,1)S(1)}, u32[]{:S(2)}, u32[]{:S(2)}) %collective-permute-start) | collective-permute-done | bytes 147488 | tf_op jit(solution)/shard_map/ppermute | solution.py:355
  10.2 1.6 %collective-permute-start.1 = (bf16[8,2,4,384]{3,2,1,0:T(4,128)(2,1)S(1)}, bf16[8,2,4,384]{3,2,1,0:T(4,128)(2,1)S(1)}, u32[]{:S(2)}, u32[]{:S(2)}) collective-permute-start(bf16[8,2,4,384]{3,2,1,0:T(4,128)(2,1)S(1)} %get-tuple-element.14), channel_id=1, source_target_pairs={{0,1},{1,0},{2,3},{3,2},{4,5},{5,4},{6,7},{7,6},{8,9},{9,8},{10,11... | collective-permute-start | bytes 147464 | tf_op jit(solution)/shard_map/ppermute | solution.py:382
  11.8 3.1 %collective-permute-start.2 = (bf16[8,2,4,384]{3,2,1,0:T(4,128)(2,1)S(1)}, bf16[8,2,4,384]{3,2,1,0:T(4,128)(2,1)S(1)}, u32[]{:S(2)}, u32[]{:S(2)}) collective-permute-start(bf16[8,2,4,384]{3,2,1,0:T(4,128)(2,1)S(1)} %get-tuple-element.15), channel_id=1, source_target_pairs={{1,2},{2,1},{3,4},{4,3},{5,6},{6,5},{9,10},{10,9},{11,12},{12,11},... | collective-permute-start | bytes 147464 | tf_op jit(solution)/shard_map/ppermute | solution.py:383
  14.9 0.0 copy-done.1
  14.9 0.0 copy-done.2
  14.9 0.0 copy-start
  14.9 0.0 copy-start.3
  14.9 0.0 copy-start.4
  14.9 0.0 copy-start.5
  15.0 2.3 %shard_map.92.sums = f32[384,384]{1,0:T(8,128)S(1)} custom-call(f32[256,384]{1,0:T(8,128)S(1)} %get-tuple-element.11.part, bf16[4,12,4,384]{3,2,1,0:T(4,128)(2,1)S(1)} %collective-permute-done.prev, f32[384]{0:T(512)S(1)} %copy-done.1, bf16[3,3,3,384,384]{4,3,2,1,0:T(8,128)(2,1)S(1)} %get-tuple-element.12.wc, f32[384]{0:T(512)S(1)} %copy-done.2), custom_call_target="tpu_custom_call" | custom-call | tf_op jit(solution)/shard_map/pallas_call | solution.py:385
  17.2 0.0 collective-permute-done.1.inner
  17.2 0.0 collective-permute-done.2.outer
  17.2 0.0 copy-done
  17.3 0.0 copy-done.3
  17.3 0.0 copy-done.4
  17.3 0.0 copy-done.5
  17.3 6.5 %shard_map.94 = bf16[4,24,8,192]{3,2,1,0:T(8,128)(2,1)} custom-call(f32[384,384]{1,0:T(8,128)S(1)} %shard_map.92.sums, bf16[8,2,4,384]{3,2,1,0:T(4,128)(2,1)S(1)} %collective-permute-done.1.inner, bf16[8,2,4,384]{3,2,1,0:T(4,128)(2,1)S(1)} %collective-permute-done.2.outer, f32[384]{0:T(512)S(1)} %copy-done.1, ...), custom_call_target="tpu_custom_call" | custom-call | tf_op jit(solution)/shard_map/pallas_call | solution.py:393
  (1 shorter events, 0.0 us)
Async XLA Ops:
  0.0 10.1 %collective-permute-start = (bf16[4,12,4,384]{3,2,1,0:T(4,128)(2,1)}, bf16[4,12,4,384]{3,2,1,0:T(4,128)(2,1)S(1)}, u32[]{:S(2)}, u32[]{:S(2)}) collective-permute-start(bf16[4,12,4,384]{3,2,1,0:T(4,128)(2,1)} %x_hbm.1), channel_id=1, source_target_pairs={{0,8},{1,9},{2,10},{3,11},{4,12},{5,13},{6,14},{7,15},{8,16},{9,17... | collective-permute-start | bytes 442376 | tf_op jit(solution)/shard_map/ppermute | solution.py:355
  3.1 11.8 %copy-start.1 = (f32[384]{0:T(512)S(1)}, f32[384]{0:T(512)}, u32[]{:S(2)}) copy-start(f32[384]{0:T(512)} %gain0.3) | copy-start | bytes 4612
  3.1 11.8 %copy-start.2 = (f32[384]{0:T(512)S(1)}, f32[384]{0:T(512)}, u32[]{:S(2)}) copy-start(f32[384]{0:T(512)} %bias0.1) | copy-start | bytes 4612
  10.2 7.1 %collective-permute-start.1 = (bf16[8,2,4,384]{3,2,1,0:T(4,128)(2,1)S(1)}, bf16[8,2,4,384]{3,2,1,0:T(4,128)(2,1)S(1)}, u32[]{:S(2)}, u32[]{:S(2)}) collective-permute-start(bf16[8,2,4,384]{3,2,1,0:T(4,128)(2,1)S(1)} %get-tuple-element.14), channel_id=1, source_target_pairs={{0,1},{1,0},{2,3},{3,2},{4,5},{5,4},{6,7},{7,6},{8,9},{9,8},{10,11... | collective-permute-start | bytes 147464 | tf_op jit(solution)/shard_map/ppermute | solution.py:382
  11.8 5.5 %collective-permute-start.2 = (bf16[8,2,4,384]{3,2,1,0:T(4,128)(2,1)S(1)}, bf16[8,2,4,384]{3,2,1,0:T(4,128)(2,1)S(1)}, u32[]{:S(2)}, u32[]{:S(2)}) collective-permute-start(bf16[8,2,4,384]{3,2,1,0:T(4,128)(2,1)S(1)} %get-tuple-element.15), channel_id=1, source_target_pairs={{1,2},{2,1},{3,4},{4,3},{5,6},{6,5},{9,10},{10,9},{11,12},{12,11},... | collective-permute-start | bytes 147464 | tf_op jit(solution)/shard_map/ppermute | solution.py:383
  14.9 2.3 %copy-start = (bf16[3,3,3,192,192]{4,3,2,1,0:T(8,128)(2,1)S(1)}, bf16[3,3,3,192,192]{4,3,2,1,0:T(8,128)(2,1)}, u32[]{:S(2)}) copy-start(bf16[3,3,3,192,192]{4,3,2,1,0:T(8,128)(2,1)} %wf.1) | copy-start | bytes 5971972
  14.9 2.3 %copy-start.3 = (f32[192]{0:T(256)S(1)}, f32[192]{0:T(256)}, u32[]{:S(2)}) copy-start(f32[192]{0:T(256)} %param.14) | copy-start | bytes 2308
  14.9 2.3 %copy-start.4 = (f32[192]{0:T(256)S(1)}, f32[192]{0:T(256)}, u32[]{:S(2)}) copy-start(f32[192]{0:T(256)} %param.15) | copy-start | bytes 2308
  14.9 2.3 %copy-start.5 = (f32[192]{0:T(256)S(1)}, f32[192]{0:T(256)}, u32[]{:S(2)}) copy-start(f32[192]{0:T(256)} %param.17) | copy-start | bytes 2308
